TPU v7x, 32 devices: a whole 2x2x4 slice. The times are simulated.
32 devices in a mesh: section: 2 (over core), gx: 4 (over z), gy: 4 (over y, x).
Axes of the slice: x: 2, y: 2, z: 4, core: 2. Of those that a mesh axis runs over, the one named last changes fastest.
Arguments:
- inputs: bfloat16 [4, 4, 128, 2048], P(None, 'gy', 'gx'), may hold values from -6 to 6
- out_grad: bfloat16 [4, 4, 128, 2048], P(None, 'gy', 'gx'), may hold values from -6 to 6
- segments: int32 [4, 4, 128], P(None, 'gy'), may hold values from 0 to 3, never falling along the last dimension, each value on 1 to 64 neighbouring positions
- routes: int32 [2, 4, 4, 128, 8], P('section', None, 'gy', 'gx'), may hold values from 0 to 15, all different within a row; in each aligned block of 32 rows (0 to 31, 32 to 63, ..., all dimensions but the last counted through in order) at most 32 rows name the same one
- gates: float32 [2, 4, 4, 128, 8], P('section', None, 'gy', 'gx'), may hold values from 0.05 to 0.3
- gain_attn: float32 [2, 2048], P('section'), may hold values from 0.5 to 1.5
- gain_ffn: float32 [2, 2048], P('section'), may hold values from 0.5 to 1.5
- gain_query: float32 [2, 128], P('section'), may hold values from 0.5 to 1.5
- gain_key: float32 [2, 128], P('section'), may hold values from 0.5 to 1.5
- w_query: bfloat16 [2, 2048, 4096], P('section', 'gy', 'gx'), may hold values from -0.125 to 0.125
- w_key: bfloat16 [2, 2048, 512], P('section', 'gy'), may hold values from -0.125 to 0.125
- w_value: bfloat16 [2, 2048, 512], P('section', 'gy'), may hold values from -0.125 to 0.125
- w_out: bfloat16 [2, 2048, 4096], P('section', 'gy', 'gx'), may hold values from -0.5 to 0.5
- w_gate: bfloat16 [2, 16, 2048, 768], P('section', ('gx', 'gy')), may hold values from -0.125 to 0.125
- w_up: bfloat16 [2, 16, 2048, 768], P('section', ('gx', 'gy')), may hold values from -0.125 to 0.125
- w_down: bfloat16 [2, 16, 768, 2048], P('section', ('gx', 'gy')), may hold values from -0.625 to 0.625
Outputs:
- layer_out: bfloat16 [2, 4, 4, 128, 2048], P('section', None, 'gy', 'gx')
- input_grad: bfloat16 [2, 4, 4, 128, 2048], P('section', None, 'gy', 'gx')
- grad_gain_attn: float32 [2, 2048], P('section')
- grad_gain_ffn: float32 [2, 2048], P('section')
- grad_gain_query: float32 [2, 128], P('section')
- grad_gain_key: float32 [2, 128], P('section')
- grad_w_query: float32 [2, 2048, 4096], P('section', 'gy', 'gx')
- grad_w_key: float32 [2, 2048, 512], P('section', 'gy')
- grad_w_value: float32 [2, 2048, 512], P('section', 'gy')
- grad_w_out: float32 [2, 2048, 4096], P('section', 'gy', 'gx')
- grad_w_gate: float32 [2, 16, 2048, 768], P('section', ('gx', 'gy'))
- grad_w_up: float32 [2, 16, 2048, 768], P('section', ('gx', 'gy'))
- grad_w_down: float32 [2, 16, 768, 2048], P('section', ('gx', 'gy'))
Inputs may be any that keep to these rules, and one draw needn't show every extreme that they name: `routes`: each row names 8 different experts. Within each aligned block of 32 rows (the tokens of one device for one layer and micro-batch) no expert is named by more than 32 rows, a bound that some block reaches. `segments`: along a group's 128 tokens the sequence numbers never fall; each sequence has 1 to 64 tokens and one has exactly 64.
All inputs are finite; a program needn't handle non-finite values.
Results may differ from a plain program's by a relative error of at most 0.028.
Values may be sent and summed in bfloat16 or wider, within the bound.
A program may use at most 448 MiB of HBM per device.

v0:
```python
import math

import jax
import jax.numpy as jnp
from jax import lax
from jax.sharding import PartitionSpec as P

HQ = 32
KVH = 4
HD = 128
TOPK = 8


EPSILON = 1e-06
ROPE_BASE = 1000000.0
ROW_PAIR = (((0,), (0,)), ((), ()))
COL_PAIR = (((1,), (1,)), ((), ()))


def from_behind(block, axis, distance):
    devices = range(lax.axis_size(axis))
    route = [(i - distance, i) for i in devices if i - distance in devices]
    return lax.ppermute(block, axis, route)


def normalize(tensor):
    scaling = lax.rsqrt(jnp.mean(tensor * tensor, axis=-1, keepdims=True) + EPSILON)
    return (tensor * scaling, scaling)


def norm_back(gradient, unit_vec, scaling):
    return scaling * (gradient - unit_vec * jnp.mean(gradient * unit_vec, axis=-1, keepdims=True))


def rotate(tensor, cosine, sine_part):
    halfway = tensor.shape[-1] // 2
    leading = tensor[..., :halfway]
    trailing = tensor[..., halfway:]
    return jnp.concatenate(
        [leading * cosine - trailing * sine_part, trailing * cosine + leading * sine_part], axis=-1
    )


def rotate_back(gradient, cosine, sine_part):
    halfway = gradient.shape[-1] // 2
    leading = gradient[..., :halfway]
    trailing = gradient[..., halfway:]
    return jnp.concatenate(
        [leading * cosine + trailing * sine_part, trailing * cosine - leading * sine_part], axis=-1
    )


def seq_tables(segment_ids, head_dim):
    length_all = segment_ids.shape[0]
    position_ids = jnp.arange(length_all, dtype=jnp.int32)
    allowed = (segment_ids[:, None] == segment_ids[None, :]) & (
        position_ids[:, None] >= position_ids[None, :]
    )
    positions = jnp.sum(allowed.astype(jnp.int32), axis=1) - 1
    halfway = head_dim // 2
    inverse = ROPE_BASE ** (-2.0 * jnp.arange(halfway, dtype=jnp.float32) / head_dim)
    angles = positions.astype(jnp.float32)[:, None] * inverse[None, :]
    return (allowed, jnp.cos(angles), jnp.sin(angles))


def dispatch_tables(route_ids, gate_vals, experts, capacity):
    token_count, top_count = route_ids.shape
    flat_ids = route_ids.reshape(-1)
    onehot = (flat_ids[:, None] == jnp.arange(experts, dtype=jnp.int32)[None, :]).astype(jnp.int32)
    earlier = jnp.cumsum(onehot, axis=0) - onehot
    slot_ids = jnp.sum(earlier * onehot, axis=1)
    targets = flat_ids * capacity + slot_ids
    select = targets[None, :] == jnp.arange(experts * capacity, dtype=jnp.int32)[:, None]
    placing = jnp.sum(
        select.astype(jnp.float32).reshape(experts * capacity, token_count, top_count), axis=2
    )
    weighting = jnp.sum(
        jnp.where(select, gate_vals.reshape(-1)[None, :], 0.0).reshape(
            experts * capacity, token_count, top_count
        ),
        axis=2,
    )
    return (placing.astype(jnp.bfloat16), weighting)


def dispatch(buffer):
    return lax.all_to_all(buffer, ("gx", "gy"), split_axis=0, concat_axis=0, tiled=True)


def collect(buffer):
    return lax.all_to_all(buffer, ("gx", "gy"), split_axis=0, concat_axis=0, tiled=True)


def local(
    inputs,
    out_grad,
    segments,
    routes,
    gates,
    gain_attn,
    gain_ffn,
    gain_query,
    gain_key,
    w_query,
    w_key,
    w_value,
    w_out,
    w_gate,
    w_up,
    w_down,
):
    micro_count = inputs.shape[0]
    local_rows = inputs.shape[2]
    model_width = inputs.shape[3]
    n_gx = lax.axis_size("gx")
    n_gy = lax.axis_size("gy")
    local_heads = w_query.shape[2] // HD
    experts = n_gx * n_gy
    capacity = 2 * local_rows * TOPK // experts
    slot_count = experts * capacity
    group_len = segments.shape[2]
    section_index = lax.axis_index("section")
    is_first = section_index == 0
    inv_root = 1.0 / math.sqrt(HD)
    query_full, key_full, value_full, w_out_full = (
        lax.all_gather(w_query[0], "gy", axis=0, tiled=True),
        lax.all_gather(w_key[0], "gy", axis=0, tiled=True),
        lax.all_gather(w_value[0], "gy", axis=0, tiled=True),
        lax.all_gather(w_out[0], "gy", axis=0, tiled=True),
    )
    kv_head = lax.axis_index("gx") * local_heads // (HQ // KVH)
    key_own = lax.dynamic_slice_in_dim(key_full, kv_head * HD, HD, 1)
    value_own = lax.dynamic_slice_in_dim(value_full, kv_head * HD, HD, 1)
    w_forward = jnp.concatenate([query_full, key_own, value_own], axis=1)
    w_backward = jnp.concatenate(
        [query_full] + [key_own] * local_heads + [value_own] * local_heads, axis=1
    )
    gain_attn_vec = gain_attn[0]
    gain_ffn_vec = gain_ffn[0]
    gain_query_vec = gain_query[0]
    gain_key_vec = gain_key[0]
    gate_mat = w_gate[0, 0]
    up_mat = w_up[0, 0]
    down_mat = w_down[0, 0]
    segment_table = segments[:, 0]
    route_table = routes[0, :, 0]
    gate_table = gates[0, :, 0]
    zero_rows = jnp.zeros((local_rows, model_width), jnp.bfloat16)
    saved_steps = []
    out_steps = []
    carried = zero_rows
    for fwd_step in range(micro_count + 1):
        batch_index = jnp.clip(fwd_step - section_index, 0, micro_count - 1)
        section_input = inputs[fwd_step, 0] if fwd_step < micro_count else zero_rows
        layer_in = jnp.where(is_first, section_input, carried)
        segment_ids = lax.dynamic_index_in_dim(segment_table, batch_index, 0, keepdims=False)
        route_ids = lax.dynamic_index_in_dim(route_table, batch_index, 0, keepdims=False)
        gate_vals = lax.dynamic_index_in_dim(gate_table, batch_index, 0, keepdims=False)
        hidden = layer_in.astype(jnp.float32)
        forward_attn_unit, forward_attn_scale = normalize(hidden)
        normed = (forward_attn_unit * gain_attn_vec).astype(jnp.bfloat16)
        forward_normed_all = lax.all_gather(normed, "gx", axis=0, tiled=True)
        projected = jnp.dot(forward_normed_all, w_forward, preferred_element_type=jnp.float32)
        query_proj = projected[:, : local_heads * HD].reshape(group_len, local_heads, HD)
        key_proj = projected[:, local_heads * HD : (local_heads + 1) * HD]
        forward_value_low = projected[:, (local_heads + 1) * HD :].astype(jnp.bfloat16)
        forward_allowed, forward_cosine, forward_sine_part = seq_tables(segment_ids, HD)
        forward_query_unit, forward_query_scale = normalize(query_proj)
        forward_key_unit, forward_key_scale = normalize(key_proj)
        forward_query_rope = rotate(
            forward_query_unit * gain_query_vec,
            forward_cosine[:, None, :],
            forward_sine_part[:, None, :],
        ).astype(jnp.bfloat16)
        forward_key_rope = rotate(
            forward_key_unit * gain_key_vec, forward_cosine, forward_sine_part
        ).astype(jnp.bfloat16)
        forward_scores = (
            jnp.einsum(
                "thd,sd->hts",
                forward_query_rope,
                forward_key_rope,
                preferred_element_type=jnp.float32,
            )
            * inv_root
        )
        exponent = jnp.where(forward_allowed[None], jnp.exp(forward_scores), 0.0)
        forward_log_total = jnp.log(jnp.sum(exponent, axis=-1))
        forward_probability = jnp.where(
            forward_allowed[None], jnp.exp(forward_scores - forward_log_total[..., None]), 0.0
        ).astype(jnp.bfloat16)
        forward_mixed_heads = jnp.einsum(
            "hts,sd->thd",
            forward_probability,
            forward_value_low,
            preferred_element_type=jnp.float32,
        )
        forward_mixed_heads = forward_mixed_heads.astype(jnp.bfloat16).reshape(
            group_len, local_heads * HD
        )
        attn_out = lax.psum_scatter(
            lax.dot_general(
                forward_mixed_heads, w_out_full, COL_PAIR, preferred_element_type=jnp.float32
            ),
            "gx",
            scatter_dimension=0,
            tiled=True,
        )
        middle = hidden + attn_out
        forward_ffn_unit, forward_ffn_scale = normalize(middle)
        expert_in = (forward_ffn_unit * gain_ffn_vec).astype(jnp.bfloat16)
        forward_placing, forward_weighting = dispatch_tables(
            route_ids, gate_vals, experts, capacity
        )
        outgoing = jnp.dot(forward_placing, expert_in, preferred_element_type=jnp.float32).astype(
            jnp.bfloat16
        )
        forward_arrived = dispatch(outgoing.reshape(experts, capacity, model_width)).reshape(
            slot_count, model_width
        )
        forward_gate_pre = jnp.dot(forward_arrived, gate_mat, preferred_element_type=jnp.float32)
        forward_up_proj = jnp.dot(forward_arrived, up_mat, preferred_element_type=jnp.float32)
        forward_inner_act = (jax.nn.silu(forward_gate_pre) * forward_up_proj).astype(jnp.bfloat16)
        result = jnp.dot(forward_inner_act, down_mat, preferred_element_type=jnp.float32).astype(
            jnp.bfloat16
        )
        returned = collect(result.reshape(experts, capacity, model_width)).reshape(
            slot_count, model_width
        )
        expert_sum = jnp.dot(
            forward_weighting.T, returned.astype(jnp.float32), precision=lax.Precision.HIGHEST
        )
        result_low = (middle + expert_sum).astype(jnp.bfloat16)
        forward_saved = (
            forward_attn_unit,
            forward_attn_scale,
            forward_normed_all,
            forward_query_unit,
            forward_query_scale,
            forward_key_unit,
            forward_key_scale,
            forward_cosine,
            forward_sine_part,
            forward_allowed,
            forward_query_rope,
            forward_key_rope,
            forward_value_low,
            forward_log_total,
            forward_mixed_heads,
            forward_ffn_unit,
            forward_ffn_scale,
            forward_placing,
            forward_weighting,
            forward_arrived,
            forward_gate_pre,
            forward_up_proj,
            forward_inner_act,
        )
        result_low, saved = (result_low, forward_saved)
        saved_steps.append(saved)
        out_steps.append(result_low)
        if fwd_step < micro_count:
            carried = from_behind(result_low, "section", 1)
    zero_grad = jnp.zeros((local_rows, model_width), jnp.float32)
    returned_grad = zero_grad
    totals = None
    grad_steps = []
    for back_step in range(micro_count + 1):
        saved = saved_steps[micro_count - back_step]
        cotangent = (
            out_grad[micro_count - 1 - back_step, 0].astype(jnp.float32)
            if back_step < micro_count
            else zero_grad
        )
        gradient = jnp.where(is_first, returned_grad, cotangent)
        (
            attn_unit,
            attn_scale,
            normed_all,
            query_unit,
            query_scale,
            key_unit,
            key_scale,
            cosine,
            sine_part,
            allowed,
            query_rope,
            key_rope,
            value_low,
            log_total,
            mixed_heads,
            ffn_unit,
            ffn_scale,
            placing,
            weighting,
            arrived,
            gate_pre,
            up_proj,
            inner_act,
        ) = saved
        grad_send = jnp.dot(weighting, gradient, precision=lax.Precision.HIGHEST).astype(
            jnp.bfloat16
        )
        grad_result = dispatch(grad_send.reshape(experts, capacity, model_width)).reshape(
            slot_count, model_width
        )
        grad_inner = lax.dot_general(
            grad_result, down_mat, COL_PAIR, preferred_element_type=jnp.float32
        )
        backward_grad_down = lax.dot_general(
            inner_act, grad_result, ROW_PAIR, preferred_element_type=jnp.float32
        )
        sigmoid_gate = jax.nn.sigmoid(gate_pre)
        silu_gate = gate_pre * sigmoid_gate
        grad_gate_pre = (
            grad_inner * up_proj * sigmoid_gate * (1.0 + gate_pre * (1.0 - sigmoid_gate))
        ).astype(jnp.bfloat16)
        grad_up_proj = (grad_inner * silu_gate).astype(jnp.bfloat16)
        backward_grad_gate = lax.dot_general(
            arrived, grad_gate_pre, ROW_PAIR, preferred_element_type=jnp.float32
        )
        backward_grad_up = lax.dot_general(
            arrived, grad_up_proj, ROW_PAIR, preferred_element_type=jnp.float32
        )
        grad_arrived = (
            lax.dot_general(grad_gate_pre, gate_mat, COL_PAIR, preferred_element_type=jnp.float32)
            + lax.dot_general(grad_up_proj, up_mat, COL_PAIR, preferred_element_type=jnp.float32)
        ).astype(jnp.bfloat16)
        grad_returned = collect(grad_arrived.reshape(experts, capacity, model_width)).reshape(
            slot_count, model_width
        )
        grad_expert_in = lax.dot_general(
            placing, grad_returned, ROW_PAIR, preferred_element_type=jnp.float32
        )
        backward_grad_ffn_gain = jnp.sum(grad_expert_in * ffn_unit, axis=0)
        grad_middle = gradient + norm_back(grad_expert_in * gain_ffn_vec, ffn_unit, ffn_scale)
        middle_low = grad_middle.astype(jnp.bfloat16)
        middle_all = lax.all_gather(middle_low, "gx", axis=0, tiled=True)
        backward_grad_out_w = lax.dot_general(
            middle_all, mixed_heads, ROW_PAIR, preferred_element_type=jnp.float32
        )
        grad_heads = jnp.dot(middle_all, w_out_full, preferred_element_type=jnp.float32)
        grad_heads = grad_heads.astype(jnp.bfloat16).reshape(group_len, local_heads, HD)
        scores = (
            jnp.einsum("thd,sd->hts", query_rope, key_rope, preferred_element_type=jnp.float32)
            * inv_root
        )
        probability = jnp.where(allowed[None], jnp.exp(scores - log_total[..., None]), 0.0)
        prob_low = probability.astype(jnp.bfloat16)
        grad_value = jnp.einsum(
            "hts,thd->shd", prob_low, grad_heads, preferred_element_type=jnp.float32
        )
        grad_prob = jnp.einsum(
            "thd,sd->hts", grad_heads, value_low, preferred_element_type=jnp.float32
        )
        mixed_split = mixed_heads.reshape(group_len, local_heads, HD)
        delta_rows = jnp.sum(
            grad_heads.astype(jnp.float32) * mixed_split.astype(jnp.float32), axis=-1
        ).T
        grad_scores = (probability * (grad_prob - delta_rows[..., None])).astype(jnp.bfloat16)
        grad_query = (
            jnp.einsum("hts,sd->thd", grad_scores, key_rope, preferred_element_type=jnp.float32)
            * inv_root
        )
        grad_key = (
            jnp.einsum("hts,thd->shd", grad_scores, query_rope, preferred_element_type=jnp.float32)
            * inv_root
        )
        cos_heads = cosine[:, None, :]
        sin_heads = sine_part[:, None, :]
        query_turn = rotate_back(grad_query, cos_heads, sin_heads)
        backward_grad_query_gain = jnp.sum(query_turn * query_unit, axis=(0, 1))
        grad_query_pre = norm_back(query_turn * gain_query_vec, query_unit, query_scale)
        key_turn = rotate_back(grad_key, cos_heads, sin_heads)
        key_unit_heads = key_unit[:, None, :]
        backward_grad_key_gain = jnp.sum(key_turn * key_unit_heads, axis=(0, 1))
        grad_key_pre = norm_back(key_turn * gain_key_vec, key_unit_heads, key_scale[:, None, :])
        grad_proj = jnp.concatenate(
            [
                grad_query_pre.reshape(group_len, -1),
                grad_key_pre.reshape(group_len, -1),
                grad_value.reshape(group_len, -1),
            ],
            axis=1,
        ).astype(jnp.bfloat16)
        backward_grad_weights = lax.dot_general(
            normed_all, grad_proj, ROW_PAIR, preferred_element_type=jnp.float32
        )
        grad_normed = lax.psum_scatter(
            lax.dot_general(
                grad_proj, w_backward, COL_PAIR, preferred_element_type=jnp.float32
            ).astype(jnp.bfloat16),
            "gx",
            scatter_dimension=0,
            tiled=True,
        ).astype(jnp.float32)
        backward_grad_attn_gain = jnp.sum(grad_normed * attn_unit, axis=0)
        grad_input = (
            grad_middle + norm_back(grad_normed * gain_attn_vec, attn_unit, attn_scale)
        ).astype(jnp.bfloat16)
        grad_input, grads = (
            grad_input,
            (
                backward_grad_weights,
                backward_grad_out_w,
                backward_grad_attn_gain,
                backward_grad_ffn_gain,
                backward_grad_query_gain,
                backward_grad_key_gain,
                backward_grad_gate,
                backward_grad_up,
                backward_grad_down,
            ),
        )
        grad_steps.append(grad_input)
        if totals is None:
            totals = grads
        else:
            totals = jax.tree.map(lambda left, right: left + right, totals, grads)
        if back_step < micro_count:
            returned_grad = from_behind(grad_input, "section", -1).astype(jnp.float32)
    (
        grad_weights,
        grad_out_w,
        grad_attn_gain,
        grad_ffn_gain,
        grad_query_gain,
        grad_key_gain,
        grad_gate,
        grad_up,
        grad_down,
    ) = totals
    full_width = query_full.shape[0]
    span = local_heads * HD
    block_len = full_width // n_gy
    query_grad_local = grad_weights[:, :span]
    key_cols = grad_weights[:, span : 2 * span].reshape(full_width, local_heads, HD).sum(axis=1)
    value_cols = grad_weights[:, 2 * span :].reshape(full_width, local_heads, HD).sum(axis=1)
    query_grad, out_w_grad = (
        lax.psum_scatter(
            query_grad_local.astype(jnp.bfloat16), "gy", scatter_dimension=0, tiled=True
        ).astype(jnp.float32),
        lax.psum_scatter(
            grad_out_w.astype(jnp.bfloat16), "gy", scatter_dimension=0, tiled=True
        ).astype(jnp.float32),
    )
    empty_wide = jnp.zeros((full_width, KVH * HD), jnp.float32)
    key_wide = lax.dynamic_update_slice_in_dim(empty_wide, key_cols, kv_head * HD, 1)
    value_wide = lax.dynamic_update_slice_in_dim(empty_wide, value_cols, kv_head * HD, 1)
    key_sum, value_sum, attn_gain_sum, ffn_gain_sum, query_gain_sum, key_gain_sum = lax.psum(
        (key_wide, value_wide, grad_attn_gain, grad_ffn_gain, grad_query_gain, grad_key_gain),
        ("gx", "gy"),
    )
    key_part = lax.dynamic_slice_in_dim(key_sum, lax.axis_index("gy") * block_len, block_len, 0)
    value_part = lax.dynamic_slice_in_dim(value_sum, lax.axis_index("gy") * block_len, block_len, 0)
    layer_out = jnp.where(is_first, jnp.stack(out_steps[:micro_count]), jnp.stack(out_steps[1:]))
    input_grad = jnp.where(
        is_first, jnp.stack(grad_steps[1:][::-1]), jnp.stack(grad_steps[:micro_count][::-1])
    )
    return (
        layer_out.reshape(1, micro_count, 1, local_rows, model_width),
        input_grad.reshape(1, micro_count, 1, local_rows, model_width),
        attn_gain_sum[None],
        ffn_gain_sum[None],
        query_gain_sum[None],
        key_gain_sum[None],
        query_grad[None],
        key_part[None],
        value_part[None],
        out_w_grad[None],
        grad_gate[None, None],
        grad_up[None, None],
        grad_down[None, None],
    )


def solution(mesh):
    return jax.shard_map(
        local,
        mesh=mesh,
        in_specs=(
            P(None, "gy", "gx", None),
            P(None, "gy", "gx", None),
            P(None, "gy", None),
            P("section", None, "gy", "gx", None),
            P("section", None, "gy", "gx", None),
            P("section", None),
            P("section", None),
            P("section", None),
            P("section", None),
            P("section", "gy", "gx"),
            P("section", "gy", None),
            P("section", "gy", None),
            P("section", "gy", "gx"),
            P("section", ("gx", "gy"), None, None),
            P("section", ("gx", "gy"), None, None),
            P("section", ("gx", "gy"), None, None),
        ),
        out_specs=(
            P("section", None, "gy", "gx", None),
            P("section", None, "gy", "gx", None),
            P("section", None),
            P("section", None),
            P("section", None),
            P("section", None),
            P("section", "gy", "gx"),
            P("section", "gy", None),
            P("section", "gy", None),
            P("section", "gy", "gx"),
            P("section", ("gx", "gy"), None, None),
            P("section", ("gx", "gy"), None, None),
            P("section", ("gx", "gy"), None, None),
        ),
        check_vma=False,
    )
```

profile of v0, /device:TPU:0, one launch (start us, length us, event | category | flops | bytes accessed | tf_op | source)
XLA Modules:
  0.0 2471.5 jit_solution(13325799077946933159)
XLA Ops:
  13.0 18.0 all_gather.42
  31.0 34.2 %all-gather.9.cloned.1.call-done = bf16[1,2048,1024]{2,1,0:T(8,128)(2,1)} async-done(((bf16[1,512,1024]{2,1,0:T(8,128)(2,1)}), bf16[1,2048,1024]{2,1,0:T(8,128)(2,1)}) %all-gather.9.cloned.1.call-update) | async-done | bytes 4194320 | tf_op jit(solution)/shard_map/all_gather | solution.py:126
  69.8 32.4 %all-gather.11.cloned.1.call-done = bf16[1,2048,512]{2,1,0:T(8,128)(2,1)} async-done(((bf16[1,512,512]{2,1,0:T(8,128)(2,1)}), bf16[1,2048,512]{2,1,0:T(8,128)(2,1)}) %all-gather.11.cloned.1.call-update) | async-done | bytes 2097168 | tf_op jit(solution)/shard_map/all_gather | solution.py:127
  110.5 28.8 %all-gather.13.cloned.1.call-done = bf16[1,2048,512]{2,1,0:T(8,128)(2,1)} async-done(((bf16[1,512,512]{2,1,0:T(8,128)(2,1)}), bf16[1,2048,512]{2,1,0:T(8,128)(2,1)}) %all-gather.13.cloned.1.call-update) | async-done | bytes 2097168 | tf_op jit(solution)/shard_map/all_gather | solution.py:128
  156.7 36.9 %all-gather.15.cloned.1.call-done = bf16[1,2048,1024]{2,1,0:T(8,128)(2,1)} async-done(((bf16[1,512,1024]{2,1,0:T(8,128)(2,1)}), bf16[1,2048,1024]{2,1,0:T(8,128)(2,1)}) %all-gather.15.cloned.1.call-update) | async-done | bytes 4194320 | tf_op jit(solution)/shard_map/all_gather | solution.py:129
  201.4 24.4 reduce-scatter.13.cloned.1.call-done
  227.8 53.0 %all_to_all.100 = bf16[16,32,2048]{2,1,0:T(8,128)(2,1)S(1)} all-to-all(bf16[16,32,2048]{2,1,0:T(8,128)(2,1)S(1)} %bitcast.1044), channel_id=1, replica_groups=mesh['section'=2,'gx'=4,'gy'=4] {'gx','gy'}, dimensions={0} | all-to-all | bytes 4194304 | tf_op jit(solution)/shard_map/all_to_all | solution.py:87
  294.2 41.4 %all-to-all-done.1 = bf16[16,32,2048]{2,1,0:T(8,128)(2,1)} async-done(((bf16[16,32,2048]{2,1,0:T(8,128)(2,1)}), bf16[16,32,2048]{2,1,0:T(8,128)(2,1)}, u32[]{:S(2)}, u32[]{:S(2)}) %all-to-all-start.1) | async-done | bytes 2097184 | tf_op jit(solution)/shard_map/all_to_all | solution.py:91
  342.2 21.0 all_gather.47
  382.9 23.2 reduce-scatter.15.cloned.1.call-done
  408.9 53.1 %all_to_all.101 = bf16[16,32,2048]{2,1,0:T(8,128)(2,1)S(1)} all-to-all(bf16[16,32,2048]{2,1,0:T(8,128)(2,1)S(1)} %bitcast.1045), channel_id=1, replica_groups=mesh['section'=2,'gx'=4,'gy'=4] {'gx','gy'}, dimensions={0} | all-to-all | bytes 4194304 | tf_op jit(solution)/shard_map/all_to_all | solution.py:87
  475.4 41.3 %all-to-all-done.3 = bf16[16,32,2048]{2,1,0:T(8,128)(2,1)} async-done(((bf16[16,32,2048]{2,1,0:T(8,128)(2,1)}), bf16[16,32,2048]{2,1,0:T(8,128)(2,1)}, u32[]{:S(2)}, u32[]{:S(2)}) %all-to-all-start.3) | async-done | bytes 2097184 | tf_op jit(solution)/shard_map/all_to_all | solution.py:91
  523.4 21.0 all_gather.48
  564.3 23.2 reduce-scatter.17.cloned.1.call-done
  590.2 52.8 %all_to_all.102 = bf16[16,32,2048]{2,1,0:T(8,128)(2,1)S(1)} all-to-all(bf16[16,32,2048]{2,1,0:T(8,128)(2,1)S(1)} %bitcast.1046), channel_id=1, replica_groups=mesh['section'=2,'gx'=4,'gy'=4] {'gx','gy'}, dimensions={0} | all-to-all | bytes 4194304 | tf_op jit(solution)/shard_map/all_to_all | solution.py:87
  656.5 41.3 %all-to-all-done.5 = bf16[16,32,2048]{2,1,0:T(8,128)(2,1)} async-done(((bf16[16,32,2048]{2,1,0:T(8,128)(2,1)}), bf16[16,32,2048]{2,1,0:T(8,128)(2,1)}, u32[]{:S(2)}, u32[]{:S(2)}) %all-to-all-start.5) | async-done | bytes 2097184 | tf_op jit(solution)/shard_map/all_to_all | solution.py:91
  704.5 21.0 all_gather.49
  745.2 23.2 reduce-scatter.19.cloned.1.call-done
  771.2 52.9 %all_to_all.103 = bf16[16,32,2048]{2,1,0:T(8,128)(2,1)S(1)} all-to-all(bf16[16,32,2048]{2,1,0:T(8,128)(2,1)S(1)} %bitcast.1047), channel_id=1, replica_groups=mesh['section'=2,'gx'=4,'gy'=4] {'gx','gy'}, dimensions={0} | all-to-all | bytes 4194304 | tf_op jit(solution)/shard_map/all_to_all | solution.py:87
  845.9 32.9 %all-to-all-done.7 = bf16[16,32,2048]{2,1,0:T(8,128)(2,1)} async-done(((bf16[16,32,2048]{2,1,0:T(8,128)(2,1)}), bf16[16,32,2048]{2,1,0:T(8,128)(2,1)}, u32[]{:S(2)}, u32[]{:S(2)}) %all-to-all-start.7) | async-done | bytes 2097184 | tf_op jit(solution)/shard_map/all_to_all | solution.py:91
  894.5 51.8 %all_gather.50 = bf16[128,2048]{1,0:T(8,128)(2,1)S(1)} all-gather(bf16[32,2048]{1,0:T(8,128)(2,1)S(1)} %fusion.282), channel_id=1, replica_groups=mesh['section'=2,'gx'=4,'gy'=4] {'gx'}, dimensions={0}, use_global_device_ids=true | all-gather | bytes 655360 | tf_op jit(solution)/shard_map/all_gather | solution.py:162
  962.2 28.8 %reduce-scatter.21.cloned.1.call-done = f32[32,2048]{1,0:T(8,128)} async-done(((f32[128,2048]{1,0:T(8,128)}), f32[32,2048]{1,0:T(8,128)}) %reduce-scatter.21.cloned.1.call-update) | async-done | bytes 262160 | tf_op jit(solution)/shard_map/reduce_scatter | solution.py:201
  1005.5 37.5 %all-to-all-done.8 = bf16[16,32,2048]{2,1,0:T(8,128)(2,1)} async-done(((bf16[16,32,2048]{2,1,0:T(8,128)(2,1)}), bf16[16,32,2048]{2,1,0:T(8,128)(2,1)}, u32[]{:S(2)}, u32[]{:S(2)}) %all-to-all-start.8) | async-done | bytes 2097184 | tf_op jit(solution)/shard_map/all_to_all | solution.py:87
  1082.3 26.8 %all-to-all-done.11 = bf16[16,32,2048]{2,1,0:T(8,128)(2,1)} async-done(((bf16[16,32,2048]{2,1,0:T(8,128)(2,1)}), bf16[16,32,2048]{2,1,0:T(8,128)(2,1)}, u32[]{:S(2)}, u32[]{:S(2)}) %all-to-all-start.11) | async-done | bytes 2097184 | tf_op jit(solution)/shard_map/all_to_all | solution.py:91
  1113.6 20.4 all_gather.51
  1174.0 21.6 reduce-scatter.23.cloned.1.call-done
  1206.6 52.8 %all_to_all.104 = bf16[16,32,2048]{2,1,0:T(8,128)(2,1)S(1)} all-to-all(bf16[16,32,2048]{2,1,0:T(8,128)(2,1)S(1)} %bitcast.1041), channel_id=1, replica_groups=mesh['section'=2,'gx'=4,'gy'=4] {'gx','gy'}, dimensions={0} | all-to-all | bytes 4194304 | tf_op jit(solution)/shard_map/all_to_all | solution.py:87
  1274.9 39.2 %all-to-all-done.13 = bf16[16,32,2048]{2,1,0:T(8,128)(2,1)} async-done(((bf16[16,32,2048]{2,1,0:T(8,128)(2,1)}), bf16[16,32,2048]{2,1,0:T(8,128)(2,1)}, u32[]{:S(2)}, u32[]{:S(2)}) %all-to-all-start.13) | async-done | bytes 2097184 | tf_op jit(solution)/shard_map/all_to_all | solution.py:91
  1318.8 20.4 all_gather.52
  1374.9 21.6 reduce-scatter.25.cloned.1.call-done
  1407.3 53.0 %all_to_all.105 = bf16[16,32,2048]{2,1,0:T(8,128)(2,1)S(1)} all-to-all(bf16[16,32,2048]{2,1,0:T(8,128)(2,1)S(1)} %bitcast.1042), channel_id=1, replica_groups=mesh['section'=2,'gx'=4,'gy'=4] {'gx','gy'}, dimensions={0} | all-to-all | bytes 4194304 | tf_op jit(solution)/shard_map/all_to_all | solution.py:87
  1475.9 39.2 %all-to-all-done.15 = bf16[16,32,2048]{2,1,0:T(8,128)(2,1)} async-done(((bf16[16,32,2048]{2,1,0:T(8,128)(2,1)}), bf16[16,32,2048]{2,1,0:T(8,128)(2,1)}, u32[]{:S(2)}, u32[]{:S(2)}) %all-to-all-start.15) | async-done | bytes 2097184 | tf_op jit(solution)/shard_map/all_to_all | solution.py:91
  1519.7 20.4 all_gather.53
  1575.9 21.6 reduce-scatter.27.cloned.1.call-done
  1608.2 53.1 %all_to_all.106 = bf16[16,32,2048]{2,1,0:T(8,128)(2,1)S(1)} all-to-all(bf16[16,32,2048]{2,1,0:T(8,128)(2,1)S(1)} %bitcast.1043), channel_id=1, replica_groups=mesh['section'=2,'gx'=4,'gy'=4] {'gx','gy'}, dimensions={0} | all-to-all | bytes 4194304 | tf_op jit(solution)/shard_map/all_to_all | solution.py:87
  1676.9 39.3 %all-to-all-done.17 = bf16[16,32,2048]{2,1,0:T(8,128)(2,1)} async-done(((bf16[16,32,2048]{2,1,0:T(8,128)(2,1)}), bf16[16,32,2048]{2,1,0:T(8,128)(2,1)}, u32[]{:S(2)}, u32[]{:S(2)}) %all-to-all-start.17) | async-done | bytes 2097184 | tf_op jit(solution)/shard_map/all_to_all | solution.py:91
  1720.8 20.4 all_gather.54
  1776.9 21.6 reduce-scatter.29.cloned.1.call-done
  1817.8 13.0 fusion.249
  1830.8 27.2 %all-to-all-done.18 = bf16[16,32,2048]{2,1,0:T(8,128)(2,1)} async-done(((bf16[16,32,2048]{2,1,0:T(8,128)(2,1)}), bf16[16,32,2048]{2,1,0:T(8,128)(2,1)}, u32[]{:S(2)}, u32[]{:S(2)}) %all-to-all-start.18) | async-done | bytes 2097184 | tf_op jit(solution)/shard_map/all_to_all | solution.py:87
  1924.2 20.8 all_gather.55
  1969.6 41.2 %add_add_fusion = f32[2048,3072]{1,0:T(8,128)} fusion(f32[2048,3072]{1,0:T(8,128)} %fusion.246, f32[2048,3072]{1,0:T(8,128)} %fusion.247, f32[2048,3072]{1,0:T(8,128)} %fusion.249, f32[2048,3072]{1,0:T(8,128)} %fusion.248, bf16[128,2048]{1,0:T(8,128)(2,1)S(1)} %copy-done.29, bf16[128,1024]{1,0:T(8,128)(2,1)S(1)} %copy.753, ...), kind=kOutput, calls=%fused_computation.5 | convolution fusion | flops 1638137856 | bytes 127139840 | tf_op jit(solution)/shard_map/dot_general | solution.py:386
  2077.9 14.4 add_convert_fusion
  2122.2 50.3 %all-to-all-done.9 = bf16[16,32,2048]{2,1,0:T(8,128)(2,1)S(1)} async-done(((bf16[16,32,2048]{2,1,0:T(8,128)(2,1)}), bf16[16,32,2048]{2,1,0:T(8,128)(2,1)S(1)}, u32[]{:S(2)}, u32[]{:S(2)}) %all-to-all-start.9) | async-done | bytes 2097184 | tf_op jit(solution)/shard_map/all_to_all | solution.py:91
  2224.0 15.0 add_bitcast_fusion
  2265.6 85.0 %all-reduce = (f32[1,2048]{1,0:T(1,128)}, f32[1,2048]{1,0:T(1,128)}, f32[1,128]{1,0:T(1,128)}, f32[1,128]{1,0:T(1,128)}) all-reduce(f32[1,2048]{1,0:T(1,128)S(1)} %bitcast.1167, f32[1,2048]{1,0:T(1,128)S(1)} %bitcast.1166, f32[1,128]{1,0:T(1,128)S(1)} %add_bitcast_fusion.9, ...), channel_id=1, replica_groups=mesh['section'=2,'gx'=4,'gy'=4] {'gx','gy'}, use_global_device_ids=true, to_apply=%region_95.96 | all-reduce | flops 4352 | bytes 34816 | tf_op jit(solution)/shard_map/psum | solution.py:450
  2357.4 49.1 %reduce-scatter.35.cloned.1.call-done = bf16[512,1024]{1,0:T(8,128)(2,1)} async-done(((bf16[2048,1024]{1,0:T(8,128)(2,1)}), bf16[512,1024]{1,0:T(8,128)(2,1)}) %reduce-scatter.35.cloned.1.call-update) | async-done | bytes 1048592 | tf_op jit(solution)/shard_map/reduce_scatter | solution.py:443
  2409.3 52.7 %reduce-scatter.33.cloned.1.call-done = bf16[512,1024]{1,0:T(8,128)(2,1)} async-done(((bf16[2048,1024]{1,0:T(8,128)(2,1)}), bf16[512,1024]{1,0:T(8,128)(2,1)}) %reduce-scatter.33.cloned.1.call-update) | async-done | bytes 1048592 | tf_op jit(solution)/shard_map/reduce_scatter | solution.py:440
  (1204 shorter events, 818.8 us)
Async XLA Ops:
  7.2 275.4 %copy-start = (bf16[1,1,2048,768]{3,2,1,0:T(8,128)(2,1)S(1)}, bf16[1,1,2048,768]{3,2,1,0:T(8,128)(2,1)}, u32[]{:S(2)}) copy-start(bf16[1,1,2048,768]{3,2,1,0:T(8,128)(2,1)} %param.30) | copy-start | bytes 9437188
  7.2 58.0 %all-gather.9.cloned.1.call-start = ((), (), s32[]{:S(2)}) async-start(), calls=%async_computation.44 | async-start | bytes 5242880 | tf_op jit(solution)/shard_map/all_gather | solution.py:126
  8.0 94.3 %all-gather.11.cloned.1.call-start = ((), (), s32[]{:S(2)}) async-start(), calls=%async_computation.45 | async-start | bytes 2621440 | tf_op jit(solution)/shard_map/all_gather | solution.py:127
  8.7 130.6 %all-gather.13.cloned.1.call-start = ((), (), s32[]{:S(2)}) async-start(), calls=%async_computation.46 | async-start | bytes 2621440 | tf_op jit(solution)/shard_map/all_gather | solution.py:128
  9.4 184.2 %all-gather.15.cloned.1.call-start = ((), (), s32[]{:S(2)}) async-start(), calls=%async_computation.47 | async-start | bytes 5242880 | tf_op jit(solution)/shard_map/all_gather | solution.py:129
  10.0 215.8 %reduce-scatter.13.cloned.1.call-start = ((), (), s32[]{:S(2)}) async-start(), calls=%async_computation.32 | async-start | bytes 1310720 | tf_op jit(solution)/shard_map/reduce_scatter | solution.py:201
  10.9 144.2 %copy-start.276 = (pred[128,128]{0,1:T(8,128)(4,1)}, pred[128,128]{0,1:T(8,128)(4,1)S(1)}, u32[]{:S(2)}) copy-start(pred[128,128]{0,1:T(8,128)(4,1)S(1)} %fusion.345) | copy-start | bytes 49156
  31.0 120.2 %copy-start.282 = (f32[64]{0:T(128)}, f32[64]{0:T(128)S(1)}, u32[]{:S(2)}) copy-start(f32[64]{0:T(128)S(1)} %multiply_power_fusion) | copy-start | bytes 772
  201.4 134.1 %copy-start.177 = (f32[512,32]{0,1:T(8,128)}, f32[512,32]{0,1:T(8,128)S(1)}, u32[]{:S(2)}) copy-start(f32[512,32]{0,1:T(8,128)S(1)} %get-tuple-element.52) | copy-start | bytes 196612
  288.7 46.8 %all-to-all-start.1 = ((bf16[16,32,2048]{2,1,0:T(8,128)(2,1)}), bf16[16,32,2048]{2,1,0:T(8,128)(2,1)}, u32[]{:S(2)}, u32[]{:S(2)}) async-start(bf16[16,32,2048]{2,1,0:T(8,128)(2,1)} %bitcast.1095), calls=%async_computation.2 | async-start | bytes 4194304 | tf_op jit(solution)/shard_map/all_to_all | solution.py:91
  293.3 112.8 %reduce-scatter.15.cloned.1.call-start = ((), (), s32[]{:S(2)}) async-start(), calls=%async_computation.33 | async-start | bytes 1310720 | tf_op jit(solution)/shard_map/reduce_scatter | solution.py:201
  338.2 2.3 collective-permute-start
  407.2 109.5 %copy-start.30 = (f32[32,2048]{1,0:T(8,128)}, f32[32,2048]{1,0:T(8,128)S(1)}, u32[]{:S(2)}) copy-start(f32[32,2048]{1,0:T(8,128)S(1)} %get-tuple-element.86) | copy-start | bytes 786436
  469.9 46.8 %all-to-all-start.3 = ((bf16[16,32,2048]{2,1,0:T(8,128)(2,1)}), bf16[16,32,2048]{2,1,0:T(8,128)(2,1)}, u32[]{:S(2)}, u32[]{:S(2)}) async-start(bf16[16,32,2048]{2,1,0:T(8,128)(2,1)} %bitcast.1096), calls=%async_computation.5 | async-start | bytes 4194304 | tf_op jit(solution)/shard_map/all_to_all | solution.py:91
  474.5 112.9 %reduce-scatter.17.cloned.1.call-start = ((), (), s32[]{:S(2)}) async-start(), calls=%async_computation.34 | async-start | bytes 1310720 | tf_op jit(solution)/shard_map/reduce_scatter | solution.py:201
  519.4 2.3 collective-permute-start.1
  588.5 109.3 %copy-start.32 = (f32[32,2048]{1,0:T(8,128)}, f32[32,2048]{1,0:T(8,128)S(1)}, u32[]{:S(2)}) copy-start(f32[32,2048]{1,0:T(8,128)S(1)} %get-tuple-element.80) | copy-start | bytes 786436
  651.1 46.8 %all-to-all-start.5 = ((bf16[16,32,2048]{2,1,0:T(8,128)(2,1)}), bf16[16,32,2048]{2,1,0:T(8,128)(2,1)}, u32[]{:S(2)}, u32[]{:S(2)}) async-start(bf16[16,32,2048]{2,1,0:T(8,128)(2,1)} %bitcast.1097), calls=%async_computation.8 | async-start | bytes 4194304 | tf_op jit(solution)/shard_map/all_to_all | solution.py:91
  655.6 112.8 %reduce-scatter.19.cloned.1.call-start = ((), (), s32[]{:S(2)}) async-start(), calls=%async_computation.35 | async-start | bytes 1310720 | tf_op jit(solution)/shard_map/reduce_scatter | solution.py:201
  700.6 2.3 collective-permute-start.2
  769.5 119.3 %copy-start.34 = (f32[32,2048]{1,0:T(8,128)}, f32[32,2048]{1,0:T(8,128)S(1)}, u32[]{:S(2)}) copy-start(f32[32,2048]{1,0:T(8,128)S(1)} %get-tuple-element.74) | copy-start | bytes 786436
  832.0 46.8 %all-to-all-start.7 = ((bf16[16,32,2048]{2,1,0:T(8,128)(2,1)}), bf16[16,32,2048]{2,1,0:T(8,128)(2,1)}, u32[]{:S(2)}, u32[]{:S(2)}) async-start(bf16[16,32,2048]{2,1,0:T(8,128)(2,1)} %bitcast.1091), calls=%async_computation.11 | async-start | bytes 4194304 | tf_op jit(solution)/shard_map/all_to_all | solution.py:91
  878.8 116.7 %all-to-all-start.10 = ((bf16[16,32,2048]{2,1,0:T(8,128)(2,1)}), bf16[16,32,2048]{2,1,0:T(8,128)(2,1)}, u32[]{:S(2)}, u32[]{:S(2)}) async-start(bf16[16,32,2048]{2,1,0:T(8,128)(2,1)} %bitcast.1036), calls=%async_computation.15 | async-start | bytes 4194304 | tf_op jit(solution)/shard_map/all_to_all | solution.py:87
  888.7 102.3 %reduce-scatter.21.cloned.1.call-start = ((), (), s32[]{:S(2)}) async-start(), calls=%async_computation.36 | async-start | bytes 1310720 | tf_op jit(solution)/shard_map/reduce_scatter | solution.py:201
  891.5 2.3 collective-permute-start.3
  992.2 205.1 %copy-start.20 = (f32[32,2048]{1,0:T(8,128)}, f32[32,2048]{1,0:T(8,128)S(1)}, u32[]{:S(2)}) copy-start(f32[32,2048]{1,0:T(8,128)S(1)} %get-tuple-element.70) | copy-start | bytes 786436
  995.6 47.5 %all-to-all-start.8 = ((bf16[16,32,2048]{2,1,0:T(8,128)(2,1)}), bf16[16,32,2048]{2,1,0:T(8,128)(2,1)}, u32[]{:S(2)}, u32[]{:S(2)}) async-start(bf16[16,32,2048]{2,1,0:T(8,128)(2,1)} %bitcast.1040), calls=%async_computation.13 | async-start | bytes 4194304 | tf_op jit(solution)/shard_map/all_to_all | solution.py:87
  1056.4 52.7 %all-to-all-start.11 = ((bf16[16,32,2048]{2,1,0:T(8,128)(2,1)}), bf16[16,32,2048]{2,1,0:T(8,128)(2,1)}, u32[]{:S(2)}, u32[]{:S(2)}) async-start(bf16[16,32,2048]{2,1,0:T(8,128)(2,1)} %bitcast.1093), calls=%async_computation.16 | async-start | bytes 4194304 | tf_op jit(solution)/shard_map/all_to_all | solution.py:91
  1066.5 129.1 %reduce-scatter.23.cloned.1.call-start = ((), (), s32[]{:S(2)}) async-start(), calls=%async_computation.37 | async-start | bytes 655360 | tf_op jit(solution)/shard_map/reduce_scatter | solution.py:389
  1198.6 3.5 collective-permute-start.4
  1267.4 46.8 %all-to-all-start.13 = ((bf16[16,32,2048]{2,1,0:T(8,128)(2,1)}), bf16[16,32,2048]{2,1,0:T(8,128)(2,1)}, u32[]{:S(2)}, u32[]{:S(2)}) async-start(bf16[16,32,2048]{2,1,0:T(8,128)(2,1)} %bitcast.1098), calls=%async_computation.19 | async-start | bytes 4194304 | tf_op jit(solution)/shard_map/all_to_all | solution.py:91
  1272.0 124.5 %reduce-scatter.25.cloned.1.call-start = ((), (), s32[]{:S(2)}) async-start(), calls=%async_computation.38 | async-start | bytes 655360 | tf_op jit(solution)/shard_map/reduce_scatter | solution.py:389
  1399.3 3.5 collective-permute-start.5
  1468.3 46.8 %all-to-all-start.15 = ((bf16[16,32,2048]{2,1,0:T(8,128)(2,1)}), bf16[16,32,2048]{2,1,0:T(8,128)(2,1)}, u32[]{:S(2)}, u32[]{:S(2)}) async-start(bf16[16,32,2048]{2,1,0:T(8,128)(2,1)} %bitcast.1099), calls=%async_computation.22 | async-start | bytes 4194304 | tf_op jit(solution)/shard_map/all_to_all | solution.py:91
  1472.9 124.5 %reduce-scatter.27.cloned.1.call-start = ((), (), s32[]{:S(2)}) async-start(), calls=%async_computation.39 | async-start | bytes 655360 | tf_op jit(solution)/shard_map/reduce_scatter | solution.py:389
  1600.3 3.5 collective-permute-start.6
  1669.4 46.8 %all-to-all-start.17 = ((bf16[16,32,2048]{2,1,0:T(8,128)(2,1)}), bf16[16,32,2048]{2,1,0:T(8,128)(2,1)}, u32[]{:S(2)}, u32[]{:S(2)}) async-start(bf16[16,32,2048]{2,1,0:T(8,128)(2,1)} %bitcast.1100), calls=%async_computation.25 | async-start | bytes 4194304 | tf_op jit(solution)/shard_map/all_to_all | solution.py:91
  1674.0 124.5 %reduce-scatter.29.cloned.1.call-start = ((), (), s32[]{:S(2)}) async-start(), calls=%async_computation.40 | async-start | bytes 655360 | tf_op jit(solution)/shard_map/reduce_scatter | solution.py:389
  1801.3 3.2 collective-permute-start.7
  1804.6 119.5 %copy-start.125 = (bf16[32,2048]{1,0:T(8,128)(2,1)}, bf16[32,2048]{1,0:T(8,128)(2,1)S(1)}, u32[]{:S(2)}) copy-start(bf16[32,2048]{1,0:T(8,128)(2,1)S(1)} %collective-permute-done.7) | copy-start | bytes 393220
  1810.2 47.9 %all-to-all-start.18 = ((bf16[16,32,2048]{2,1,0:T(8,128)(2,1)}), bf16[16,32,2048]{2,1,0:T(8,128)(2,1)}, u32[]{:S(2)}, u32[]{:S(2)}) async-start(bf16[16,32,2048]{2,1,0:T(8,128)(2,1)} %bitcast.1039), calls=%async_computation.27 | async-start | bytes 4194304 | tf_op jit(solution)/shard_map/all_to_all | solution.py:87
  1869.3 53.6 %all-to-all-start.19 = ((bf16[16,32,2048]{2,1,0:T(8,128)(2,1)}), bf16[16,32,2048]{2,1,0:T(8,128)(2,1)S(1)}, u32[]{:S(2)}, u32[]{:S(2)}) async-start(bf16[16,32,2048]{2,1,0:T(8,128)(2,1)} %bitcast.1094), calls=%async_computation.28 | async-start | bytes 4194304 | tf_op jit(solution)/shard_map/all_to_all | solution.py:91
  1880.2 384.0 %reduce-scatter.31.cloned.1.call-start = ((), (), s32[]{:S(2)}) async-start(), calls=%async_computation.41 | async-start | bytes 655360 | tf_op jit(solution)/shard_map/reduce_scatter | solution.py:389
  1969.1 383.7 %all-reduce.4.cloned.1.call-start = ((), (), s32[]{:S(2)}) async-start(), calls=%async_computation.48 | async-start | bytes 16777216 | tf_op jit(solution)/shard_map/psum | solution.py:450
  2058.1 348.4 %reduce-scatter.35.cloned.1.call-start = ((), (), s32[]{:S(2)}) async-start(), calls=%async_computation.43 | async-start | bytes 5242880 | tf_op jit(solution)/shard_map/reduce_scatter | solution.py:443
  2098.5 74.0 %all-to-all-start.9 = ((bf16[16,32,2048]{2,1,0:T(8,128)(2,1)}), bf16[16,32,2048]{2,1,0:T(8,128)(2,1)S(1)}, u32[]{:S(2)}, u32[]{:S(2)}) async-start(bf16[16,32,2048]{2,1,0:T(8,128)(2,1)} %bitcast.1092), calls=%async_computation.14 | async-start | bytes 4194304 | tf_op jit(solution)/shard_map/all_to_all | solution.py:91
  2103.4 358.6 %reduce-scatter.33.cloned.1.call-start = ((), (), s32[]{:S(2)}) async-start(), calls=%async_computation.42 | async-start | bytes 5242880 | tf_op jit(solution)/shard_map/reduce_scatter | solution.py:440
  2355.0 109.7 %copy-start.1 = (bf16[1,1,2048,768]{3,2,1,0:T(8,128)(2,1)S(1)}, bf16[1,1,2048,768]{3,2,1,0:T(8,128)(2,1)}, u32[]{:S(2)}) copy-start(bf16[1,1,2048,768]{3,2,1,0:T(8,128)(2,1)} %param.30) | copy-start | bytes 9437188
  (343 other events, 5305.4 us)
Sparse Core Ops, SparseCore 0:
  9.9 55.2 all-gather.8
  67.0 35.1 all-gather.10
  104.1 35.1 all-gather.12
  141.0 52.5 all-gather.14
  198.5 27.3 reduce-scatter.12
  379.3 26.7 reduce-scatter.14
  560.6 26.7 reduce-scatter.16
  741.6 26.7 reduce-scatter.18
  962.4 28.6 reduce-scatter.20
  1174.1 21.4 reduce-scatter.22
  1375.0 21.3 reduce-scatter.24
  1576.0 21.3 reduce-scatter.26
  1777.1 21.4 reduce-scatter.28
  1969.2 21.4 reduce-scatter.30
  2058.2 293.5 all-reduce.3
  2354.7 51.7 reduce-scatter.34
  2409.3 52.5 reduce-scatter.32
where the time goes:
time: 2480 us; the launch traced here: 2470 us
  waiting for transfers between devices  884 us (36%)
  blocking collectives  691 us (28%)
  matrix products  511 us (21%)
  other arithmetic  153 us (6%)
  local copies, waits for them, and re-layouts  124 us (5%)
  starting transfers between devices  89.8 us (4%)
    all_to_all x7, blocking collectives, dispatch(): lax.all_to_all(buffer, ('gx', 'gy'), split_axis=0, concat_axis=0, tiled=T...  371 us
    all_to_all x10, waiting for transfers between devices, collect(): lax.all_to_all(buffer, ('gx', 'gy'), split_axis=0, concat_axis=0, tiled=T...  362 us
    all_gather x5, blocking collectives, local(): forward_normed_all = lax.all_gather(normed, 'gx', axis=0, tiled=True)  133 us
    reduce_scatter x5, waiting for transfers between devices, local(): lax.psum_scatter(lax.dot_general(forward_mixed_heads, w_out_full, COL_PAI...  123 us
    all_gather x5, blocking collectives, local(): middle_all = lax.all_gather(middle_low, 'gx', axis=0, tiled=True)  103 us
    reduce_scatter x5, waiting for transfers between devices, local(): lax.psum_scatter(lax.dot_general(grad_proj, w_backward, COL_PAIR, preferr...  86.4 us
    dot_general x5, matrix products, local(): lax.dot_general(normed_all, grad_proj, ROW_PAIR, preferred_element_type=j...  85.9 us
    psum x1, blocking collectives, local(): lax.psum((key_wide, value_wide, grad_attn_gain, grad_ffn_gain, grad_query...  85 us
  transfers between devices with their start and end apart: 38, of which 35 were waited for; matrix products, arithmetic and copies ran while one was open for 16% of the time, Pallas kernels for 0%

commit v1 on v0

v1 whole, which is shorter than its diff:
```python
import functools
import math

import jax
import jax.numpy as jnp
from jax import lax
from jax.experimental import pallas as pl
from jax.experimental.pallas import tpu as pltpu
from jax.sharding import PartitionSpec as P

HQ = 32
KVH = 4
HD = 128
TOPK = 8

EPSILON = 1e-06
ROPE_BASE = 1000000.0
ROW_PAIR = (((0,), (0,)), ((), ()))
COL_PAIR = (((1,), (1,)), ((), ()))
F32 = jnp.float32
BF16 = jnp.bfloat16
MOST_ROWS = 1024


def normalize(tensor):
    scaling = lax.rsqrt(jnp.mean(tensor * tensor, axis=-1, keepdims=True) + EPSILON)
    return (tensor * scaling, scaling)


def norm_back(gradient, unit_vec, scaling):
    return scaling * (gradient - unit_vec * jnp.mean(gradient * unit_vec, axis=-1, keepdims=True))


def rotate(tensor, cosine, sine_part):
    halfway = tensor.shape[-1] // 2
    leading = tensor[..., :halfway]
    trailing = tensor[..., halfway:]
    return jnp.concatenate(
        [leading * cosine - trailing * sine_part, trailing * cosine + leading * sine_part], axis=-1
    )


def rotate_back(gradient, cosine, sine_part):
    return rotate(gradient, cosine, -sine_part)


def seq_tables(segment_ids, head_dim):
    length_all = segment_ids.shape[-1]
    position_ids = jnp.arange(length_all, dtype=jnp.int32)
    allowed = (segment_ids[:, :, None] == segment_ids[:, None, :]) & (
        position_ids[:, None] >= position_ids[None, :]
    )
    positions = jnp.sum(allowed.astype(jnp.int32), axis=-1) - 1
    halfway = head_dim // 2
    inverse = ROPE_BASE ** (-2.0 * jnp.arange(halfway, dtype=jnp.float32) / head_dim)
    angles = positions.astype(jnp.float32)[..., None] * inverse
    return (allowed, jnp.cos(angles), jnp.sin(angles))


def dot32(left, right, dims=None):
    if dims is None:
        return jnp.dot(left, right, preferred_element_type=F32)
    return lax.dot_general(left, right, dims, preferred_element_type=F32)


def gather_z(rows):
    return lax.all_gather(rows, "gx", axis=1, tiled=True)


def scatter_z(rows):
    return lax.psum_scatter(rows, "gx", scatter_dimension=1, tiled=True)


def gather_all(rows):
    return lax.all_gather(rows, ("gx", "gy"), axis=0, tiled=True)


def scatter_all(rows):
    return lax.psum_scatter(rows, ("gx", "gy"), scatter_dimension=0, tiled=True)


def both_layers(tensor):
    return lax.all_gather(tensor, "section", axis=0, tiled=False)


def dense_gates(route_ids, gate_vals, experts):
    onehot = route_ids[..., None] == jnp.arange(experts, dtype=jnp.int32)
    return jnp.sum(jnp.where(onehot, gate_vals[..., None], 0.0), axis=-2)


def swap_sections(tensor):
    return lax.ppermute(tensor, "section", [(0, 1), (1, 0)])


def remote(src, dst, send_sem, recv_sem, **where):
    return pltpu.make_async_remote_copy(
        src_ref=src,
        dst_ref=dst,
        send_sem=send_sem,
        recv_sem=recv_sem,
        device_id=where,
        device_id_type=pl.DeviceIdType.MESH,
    )


def hello(n, me, gy, with_plane):
    barrier = pltpu.get_barrier_semaphore()
    mesh_ids = pl.DeviceIdType.MESH

    @pl.when(me + 1 < n)
    def _():
        pl.semaphore_signal(barrier, 1, device_id={"gx": me + 1}, device_id_type=mesh_ids)

    @pl.when(me > 0)
    def _():
        pl.semaphore_signal(barrier, 1, device_id={"gx": me - 1}, device_id_type=mesh_ids)

    if with_plane:
        for bit in (1, 2):
            pl.semaphore_signal(
                barrier, 1, device_id={"gy": gy_flip(gy, bit)}, device_id_type=mesh_ids
            )
    peers = 2 if with_plane else 0
    at_end = (me == 0) | (me == n - 1)

    @pl.when(at_end)
    def _():
        pl.semaphore_wait(barrier, peers + 1)

    @pl.when(jnp.logical_not(at_end))
    def _():
        pl.semaphore_wait(barrier, peers + 2)


def gy_flip(gy, bits):
    low = lax.rem(gy, 2)
    high = gy // 2
    if bits & 1:
        low = 1 - low
    if bits & 2:
        high = 1 - high
    return high * 2 + low


def z_gather_steps(n, me, slot, sems, after):
    send_up, recv_up, send_down, recv_down = sems
    sends = []

    def up(k):
        return remote(slot(me - k), slot(me - k), send_up.at[k], recv_up.at[k], gx=me + 1)

    def down(k):
        return remote(slot(me + k), slot(me + k), send_down.at[k], recv_down.at[k], gx=me - 1)

    for k in range(n):
        @pl.when(me - k >= 0)
        def _():
            if k:
                remote(
                    slot(me - k), slot(me - k), send_up.at[k - 1], recv_up.at[k - 1], gx=me
                ).wait_recv()
            if k < n - 1:

                @pl.when(me + 1 < n)
                def _():
                    up(k).start()

            if k == 0:

                @pl.when(me > 0)
                def _():
                    down(0).start()

            after(me - k, k)

        if k:

            @pl.when(me + k < n)
            def _():
                remote(
                    slot(me + k), slot(me + k), send_down.at[k - 1], recv_down.at[k - 1], gx=me
                ).wait_recv()
                if k < n - 1:

                    @pl.when(me > 0)
                    def _():
                        down(k).start()

                after(me + k, k)


def z_gather_drain(n, me, slot, sems):
    send_up, recv_up, send_down, recv_down = sems
    for k in range(n - 1):

        @pl.when((me - k >= 0) & (me + 1 < n))
        def _():
            remote(slot(me - k), slot(me - k), send_up.at[k], recv_up.at[k], gx=me + 1).wait_send()

        @pl.when((me + k < n) & (me > 0))
        def _():
            remote(
                slot(me + k), slot(me + k), send_down.at[k], recv_down.at[k], gx=me - 1
            ).wait_send()


def flip_by(gy, step):
    low = lax.rem(lax.rem(gy, 2) + lax.rem(step, 2), 2)
    high = lax.rem(gy // 2 + step // 2, 2)
    return high * 2 + low


class Plane:
    def __init__(self, n, sems):
        self.n = n
        self.me = lax.axis_index("gx")
        self.gy = lax.axis_index("gy")
        self.cx, self.cy, self.cd = (gy_flip(self.gy, bits) for bits in (1, 2, 3))
        self.gather_sems = sems[:10]
        self.scatter_sems = sems[10:20]
        self.z_list = []
        for k in range((n + 1) // 2):
            self.z_list += [n - 1 - k] + ([k] if k != n - 1 - k else [])


    def gather_own_column(self, slot):
        su, ru, sd, rd, sx, rx, sy, ry, sf, rf = self.gather_sems
        c = self.gy

        def after(z, k):
            remote(slot(z, c), slot(z, c), sx.at[z], rx.at[z], gy=self.cx).start()
            remote(slot(z, c), slot(z, c), sy.at[z], ry.at[z], gy=self.cy).start()

        z_gather_steps(self.n, self.me, lambda z: slot(z, c), (su, ru, sd, rd), after)

    def gather_pass_on(self, slot):
        su, ru, sd, rd, sx, rx, sy, ry, sf, rf = self.gather_sems

        def forward(z):
            remote(slot(z, self.cx), slot(z, self.cx), sx.at[z], rx.at[z], gy=self.cx).wait_recv()
            remote(slot(z, self.cy), slot(z, self.cy), sy.at[z], ry.at[z], gy=self.cy).wait_recv()

            @pl.when(lax.rem(z, 2) == 0)
            def _():
                remote(
                    slot(z, self.cy), slot(z, self.cy), sf.at[z], rf.at[z], gy=self.cx
                ).start()

            @pl.when(lax.rem(z, 2) == 1)
            def _():
                remote(
                    slot(z, self.cx), slot(z, self.cx), sf.at[z], rf.at[z], gy=self.cy
                ).start()

        for k in range(self.n):

            @pl.when(self.me - k >= 0)
            def _():
                forward(self.me - k)

            if k:

                @pl.when(self.me + k < self.n)
                def _():
                    forward(self.me + k)

    def gather_far_column(self, slot):
        sf, rf = self.gather_sems[8:]
        for z in range(self.n):
            remote(slot(z, self.cd), slot(z, self.cd), sf.at[z], rf.at[z], gy=self.cx).wait_recv()

    def gather_drain(self, slot):
        su, ru, sd, rd, sx, rx, sy, ry, sf, rf = self.gather_sems
        z_gather_drain(self.n, self.me, lambda z: slot(z, self.gy), (su, ru, sd, rd))
        for z in range(self.n):
            one = slot(z, self.gy)
            remote(one, one, sx.at[z], rx.at[z], gy=self.cx).wait_send()
            remote(one, one, sy.at[z], ry.at[z], gy=self.cy).wait_send()
            remote(one, one, sf.at[z], rf.at[z], gy=self.cx).wait_send()


    def to_x(self, z):
        sx, rx = self.scatter_sems[4:6]
        return remote(self.part(z, self.cx), self.xin.at[z], sx.at[z], rx.at[z], gy=self.cx)

    def to_y(self, z):
        sy, ry = self.scatter_sems[6:8]
        return remote(self.part(z, self.cy), self.yin.at[z], sy.at[z], ry.at[z], gy=self.cy)

    def far(self, z):
        sf, rf = self.scatter_sems[8:]
        return remote(
            self.part(z, self.cd),
            self.din.at[z],
            sf.at[z],
            rf.at[z],
            gy=self.cx if z % 2 == 0 else self.cy,
        )

    def scatter_setup(self, part, xin, yin, din, zup, zdn, stage, acc):
        self.part, self.xin, self.yin, self.din = part, xin, yin, din
        self.zup, self.zdn, self.stage, self.acc = zup, zdn, stage, acc

    def scatter_x(self):
        for z in self.z_list:
            if z % 2 == 0:
                self.to_x(z).start()

    def scatter_y(self):
        for z in self.z_list:
            if z % 2 == 1:
                self.to_y(z).start()

    def scatter_far(self):
        for z in self.z_list:
            self.far(z).start()

    def scatter_pass_on(self, z):
        self.far(z).wait_recv()
        mine = self.part(z, self.cy if z % 2 == 0 else self.cx)
        add_rows(mine, mine, self.din.at[z])
        (self.to_y if z % 2 == 0 else self.to_x)(z).start()

    def scatter_line(self, z, total):
        n, me, acc = self.n, self.me, self.acc
        su, ru, sd, rd = self.scatter_sems[:4]
        self.to_x(z).wait_recv()
        self.to_y(z).wait_recv()
        add_rows(acc, self.part(z, self.gy), self.xin.at[z], self.yin.at[z])
        up = remote(self.stage.at[z], self.zup.at[z], su.at[z], ru.at[z], gx=me + 1)
        down = remote(self.stage.at[z], self.zdn.at[z], sd.at[z], rd.at[z], gx=me - 1)

        @pl.when((me < z) & (me > 0))
        def _():
            up.wait_recv()
            add_rows(acc, acc, self.zup.at[z])

        @pl.when((me > z) & (me < n - 1))
        def _():
            down.wait_recv()
            add_rows(acc, acc, self.zdn.at[z])

        @pl.when(me != z)
        def _():
            add_rows(self.stage.at[z], acc)

        @pl.when(me < z)
        def _():
            up.start()

        @pl.when(me > z)
        def _():
            down.start()

        @pl.when(me == z)
        def _():
            add_rows(total, acc)

    def scatter_finish(self, total):
        n, me = self.n, self.me
        su, ru, sd, rd = self.scatter_sems[:4]

        @pl.when(me > 0)
        def _():
            remote(self.stage.at[me], self.zup.at[me], su.at[me], ru.at[me], gx=me - 1).wait_recv()
            add_rows(total, total, self.zup.at[me])

        @pl.when(me < n - 1)
        def _():
            remote(self.stage.at[me], self.zdn.at[me], sd.at[me], rd.at[me], gx=me + 1).wait_recv()
            add_rows(total, total, self.zdn.at[me])

        for z in self.z_list:
            self.to_x(z).wait_send()
            self.to_y(z).wait_send()
            self.far(z).wait_send()

            @pl.when(me < z)
            def _():
                remote(self.stage.at[z], self.zup.at[z], su.at[z], ru.at[z], gx=me + 1).wait_send()

            @pl.when(me > z)
            def _():
                remote(self.stage.at[z], self.zdn.at[z], sd.at[z], rd.at[z], gx=me - 1).wait_send()


def add_rows(out, *terms):
    rows = out.shape[0]
    step = 16

    def body(i, carry):
        at = pl.ds(pl.multiple_of(i * step, step), step)
        value = terms[0][at].astype(F32)
        for term in terms[1:]:
            value = value + term[at].astype(F32)
        out[at] = value.astype(out.dtype)
        return carry

    lax.fori_loop(0, rows // step, body, 0)


def fetch_layer(layer, own, other, held, sems):
    section = lax.axis_index("section")

    @pl.when(section == layer)
    def _():
        for k, ref in enumerate(own):
            pltpu.make_async_copy(ref, held[k], sems.at[k]).start()

    @pl.when(section != layer)
    def _():
        for k, ref in enumerate(other):
            pltpu.make_async_copy(ref, held[k], sems.at[k]).start()


def fetch_wait(own, held, sems, which):
    for k in which:
        pltpu.make_async_copy(own[k], held[k], sems.at[k]).wait()


def moe_forward_kernel(
    n,
    layer,
    mid_ref,
    pay_ref,
    wg_own,
    wu_own,
    wd_own,
    wg_other,
    wu_other,
    wd_other,
    out_ref,
    arrived_ref,
    weight_ref,
    gp_ref,
    up_ref,
    inner_ref,
    pay,
    wg,
    wu,
    wd,
    part,
    xin,
    yin,
    din,
    zup,
    zdn,
    stage,
    acc,
    total,
    gp,
    up,
    inner,
    wsem,
    osem,
    *sems,
):
    r, d = mid_ref.shape
    ff = wg.shape[1]
    rows = n * r
    experts = 4 * n
    own, other, held = (
        (wg_own, wu_own, wd_own),
        (wg_other, wu_other, wd_other),
        (wg, wu, wd),
    )
    fetch_layer(layer, own, other, held, wsem)
    plane = Plane(n, sems)
    me, gy = plane.me, plane.gy
    hello(n, me, gy, True)
    pay[pl.ds(pl.multiple_of((gy * n + me) * r, r), r)] = pay_ref[...]

    def slot(z, c):
        return pay.at[pl.ds((c * n + z) * r, r)]

    plane.scatter_setup(lambda z, c: part.at[c * n + z], xin, yin, din, zup, zdn, stage, acc)
    plane.gather_own_column(slot)
    fetch_wait(own, held, wsem, range(3))
    expert = me * 4 + gy

    def column(s, carry):
        c = flip_by(gy, s)

        @pl.when(s == 1)
        def _():
            plane.gather_pass_on(slot)

        @pl.when(s == 3)
        def _():
            plane.gather_far_column(slot)

        at = pl.ds(pl.multiple_of(c * rows, rows), rows)
        gate_cols = pay[at, d : d + 128].astype(F32)
        lane = lax.broadcasted_iota(jnp.int32, (rows, 128), 1)
        hit = ((lane == expert) | (lane == expert + experts)) & (lane < 2 * experts)
        weight = jnp.sum(jnp.where(hit, gate_cols, 0.0), axis=1, keepdims=True)
        weight_ref[at] = weight
        block = pay[at, :d]
        for j in range(ff // 256):
            cols = slice(j * 256, (j + 1) * 256)
            g = jnp.dot(block, wg[:, cols], preferred_element_type=F32)
            u = jnp.dot(block, wu[:, cols], preferred_element_type=F32)
            gp[at, cols] = g.astype(BF16)
            up[at, cols] = u.astype(BF16)
            inner[at, cols] = (g / (1.0 + jnp.exp(-g)) * u).astype(BF16)
        act = inner[at]
        for j in range(d // 256):
            cols = slice(j * 256, (j + 1) * 256)
            res = jnp.dot(act, wd[:, cols], preferred_element_type=F32) * weight
            part[pl.ds(pl.multiple_of(c * n, n), n), :, cols] = (
                res.astype(BF16).reshape(n, r, 256)
            )

        @pl.when(s == 1)
        def _():
            plane.scatter_x()

        @pl.when(s == 2)
        def _():
            plane.scatter_y()

        return carry

    lax.fori_loop(0, 4, column, 0)
    plane.scatter_far()
    saves = [
        pltpu.make_async_copy(pay.at[:, pl.ds(0, d)], arrived_ref, osem.at[0]),
        pltpu.make_async_copy(gp, gp_ref, osem.at[1]),
        pltpu.make_async_copy(up, up_ref, osem.at[2]),
        pltpu.make_async_copy(inner, inner_ref, osem.at[3]),
    ]
    for save in saves:
        save.start()
    for z in plane.z_list:
        plane.scatter_pass_on(z)
    for z in plane.z_list:
        plane.scatter_line(z, total)
    plane.scatter_finish(total)
    add_rows(out_ref, mid_ref, total)
    plane.gather_drain(slot)
    for save in saves:
        save.wait()


def scatter_buffers(n, r, d):
    return [pltpu.VMEM((4 * n, r, d), BF16)] + [pltpu.VMEM((n, r, d), BF16)] * 6 + [
        pltpu.VMEM((r, d), F32)
    ] * 2


def in_vmem(count):
    return [pl.BlockSpec(memory_space=pltpu.VMEM)] * count


def in_place(count):
    return [pl.BlockSpec(memory_space=pl.ANY)] * count


def moe_forward(layer, n, mid, payload, own, other, cid):
    r, d = mid.shape
    ff = own[0].shape[1]
    total_rows = 4 * n * r
    width = payload.shape[1]
    return pl.pallas_call(
        functools.partial(moe_forward_kernel, n, layer),
        out_shape=(
            jax.ShapeDtypeStruct((r, d), BF16),
            jax.ShapeDtypeStruct((total_rows, d), BF16),
            jax.ShapeDtypeStruct((total_rows, 1), F32),
            jax.ShapeDtypeStruct((total_rows, ff), BF16),
            jax.ShapeDtypeStruct((total_rows, ff), BF16),
            jax.ShapeDtypeStruct((total_rows, ff), BF16),
        ),
        in_specs=in_vmem(2) + in_place(6),
        out_specs=tuple(in_vmem(1) + in_place(1) + in_vmem(1) + in_place(3)),
        scratch_shapes=[
            pltpu.VMEM((total_rows, width), BF16),
            pltpu.VMEM((d, ff), BF16),
            pltpu.VMEM((d, ff), BF16),
            pltpu.VMEM((ff, d), BF16),
        ]
        + scatter_buffers(n, r, d)
        + [pltpu.VMEM((total_rows, ff), BF16)] * 3
        + [pltpu.SemaphoreType.DMA((3,)), pltpu.SemaphoreType.DMA((4,))]
        + [pltpu.SemaphoreType.DMA((n,))] * 20,
        compiler_params=pltpu.CompilerParams(
            collective_id=cid, has_side_effects=True, vmem_limit_bytes=63 << 20
        ),
        name="moe_forward",
    )(mid, payload, *own, *other)


def moe_backward_kernel(
    n,
    layer,
    cot_ref,
    mid_ref,
    gain_ref,
    weight_ref,
    arrived_hbm,
    gp_hbm,
    up_hbm,
    inner_hbm,
    wg_own,
    wu_own,
    wd_own,
    wg_other,
    wu_other,
    wd_other,
    dmid_ref,
    dgain_ref,
    grad_gate_ref,
    grad_up_ref,
    grad_down_ref,
    cots,
    wg,
    wu,
    wd,
    part,
    xin,
    yin,
    din,
    zup,
    zdn,
    stage,
    acc,
    total,
    arrived,
    gp,
    up,
    inner,
    de,
    out_gate,
    out_up,
    out_down,
    wsem,
    isem,
    osem,
    *sems,
):
    r, d = mid_ref.shape
    ff = wg.shape[1]
    rows = n * r
    own, other, held = (
        (wg_own, wu_own, wd_own),
        (wg_other, wu_other, wd_other),
        (wg, wu, wd),
    )
    loads = [
        pltpu.make_async_copy(gp_hbm, gp, isem.at[0]),
        pltpu.make_async_copy(up_hbm, up, isem.at[1]),
        pltpu.make_async_copy(arrived_hbm, arrived, isem.at[2]),
        pltpu.make_async_copy(inner_hbm, inner, isem.at[3]),
    ]
    fetch_layer(layer, own, other, held, wsem)
    for load in loads:
        load.start()
    plane = Plane(n, sems)
    me, gy = plane.me, plane.gy
    hello(n, me, gy, True)
    cots[pl.ds(pl.multiple_of((gy * n + me) * r, r), r)] = cot_ref[...]

    def slot(z, c):
        return cots.at[pl.ds((c * n + z) * r, r)]

    plane.scatter_setup(lambda z, c: part.at[c * n + z], xin, yin, din, zup, zdn, stage, acc)
    plane.gather_own_column(slot)
    fetch_wait(own, held, wsem, range(3))
    for load in loads:
        load.wait()

    def column(s, carry):
        c = flip_by(gy, s)

        @pl.when(s == 1)
        def _():
            plane.gather_pass_on(slot)

        @pl.when(s == 3)
        def _():
            plane.gather_far_column(slot)

        at = pl.ds(pl.multiple_of(c * rows, rows), rows)
        de[at] = (cots[at].astype(F32) * weight_ref[at]).astype(BF16)
        block = de[at]
        for j in range(ff // 256):
            cols = slice(j * 256, (j + 1) * 256)
            dz = dot32(block, wd[cols], COL_PAIR)
            g = gp[at, cols].astype(F32)
            u = up[at, cols].astype(F32)
            sg = 1.0 / (1.0 + jnp.exp(-g))
            gp[at, cols] = (dz * u * sg * (1.0 + g * (1.0 - sg))).astype(BF16)
            up[at, cols] = (dz * g * sg).astype(BF16)
        dgp = gp[at]
        dup = up[at]
        for j in range(d // 256):
            cols = slice(j * 256, (j + 1) * 256)
            res = dot32(dgp, wg[cols], COL_PAIR) + dot32(dup, wu[cols], COL_PAIR)
            part[pl.ds(pl.multiple_of(c * n, n), n), :, cols] = (
                res.astype(BF16).reshape(n, r, 256)
            )

        @pl.when(s == 1)
        def _():
            plane.scatter_x()

        @pl.when(s == 2)
        def _():
            plane.scatter_y()

        return carry

    lax.fori_loop(0, 4, column, 0)
    plane.scatter_far()

    def chunk_saves(i):
        at = pl.ds(pl.multiple_of(i * 256, 256), 256)
        return (
            pltpu.make_async_copy(out_gate.at[at], grad_gate_ref.at[at], osem.at[0, i]),
            pltpu.make_async_copy(out_up.at[at], grad_up_ref.at[at], osem.at[1, i]),
            pltpu.make_async_copy(out_down.at[:, at], grad_down_ref.at[:, at], osem.at[2, i]),
        )

    def weight_grads(first, last):
        def chunk(i, carry):
            at = pl.ds(pl.multiple_of(i * 256, 256), 256)
            left = arrived[:, at]
            out_gate[at] = dot32(left, gp[...], ROW_PAIR).astype(BF16)
            out_up[at] = dot32(left, up[...], ROW_PAIR).astype(BF16)
            out_down[:, at] = dot32(inner[...], de[:, at], ROW_PAIR).astype(BF16)
            for save in chunk_saves(i):
                save.start()
            return carry

        lax.fori_loop(first, last, chunk, 0)

    chunks = d // 256
    cut = [0, chunks * 2 // 8, chunks * 4 // 8, chunks * 6 // 8, chunks]
    weight_grads(cut[0], cut[1])
    for z in plane.z_list:
        plane.scatter_pass_on(z)
    weight_grads(cut[1], cut[2])
    for k, z in enumerate(plane.z_list):
        plane.scatter_line(z, total)
        if k == 0:
            weight_grads(cut[2], cut[3])
    weight_grads(cut[3], cut[4])
    plane.scatter_finish(total)

    mid = mid_ref[...]
    scale = lax.rsqrt(jnp.mean(mid * mid, axis=-1, keepdims=True) + EPSILON)
    unit = mid * scale
    db = total[...]
    dgain_ref[...] = jnp.sum(db * unit, axis=0, keepdims=True)
    dmid_ref[...] = cot_ref[...].astype(F32) + norm_back(db * gain_ref[...], unit, scale)
    plane.gather_drain(slot)
    for i in range(chunks):
        for save in chunk_saves(i):
            save.wait()


def moe_backward(layer, n, cot, mid, gain, weight, arrived, gp, up, inner, own, other, cid):
    r, d = mid.shape
    ff = own[0].shape[1]
    total_rows = 4 * n * r
    return pl.pallas_call(
        functools.partial(moe_backward_kernel, n, layer),
        out_shape=(
            jax.ShapeDtypeStruct((r, d), F32),
            jax.ShapeDtypeStruct((1, d), F32),
            jax.ShapeDtypeStruct((d, ff), BF16),
            jax.ShapeDtypeStruct((d, ff), BF16),
            jax.ShapeDtypeStruct((ff, d), BF16),
        ),
        in_specs=in_vmem(4) + in_place(10),
        out_specs=tuple(in_vmem(2) + in_place(3)),
        scratch_shapes=[
            pltpu.VMEM((total_rows, d), BF16),
            pltpu.VMEM((d, ff), BF16),
            pltpu.VMEM((d, ff), BF16),
            pltpu.VMEM((ff, d), BF16),
        ]
        + scatter_buffers(n, r, d)
        + [pltpu.VMEM((total_rows, d), BF16)]
        + [pltpu.VMEM((total_rows, ff), BF16)] * 3
        + [pltpu.VMEM((total_rows, d), BF16)]
        + [pltpu.VMEM((d, ff), BF16)] * 2
        + [pltpu.VMEM((ff, d), BF16)]
        + [
            pltpu.SemaphoreType.DMA((3,)),
            pltpu.SemaphoreType.DMA((4,)),
            pltpu.SemaphoreType.DMA((3, d // 256)),
        ]
        + [pltpu.SemaphoreType.DMA((n,))] * 20,
        compiler_params=pltpu.CompilerParams(
            collective_id=cid, has_side_effects=True, vmem_limit_bytes=63 << 20
        ),
        name="moe_backward",
    )(cot, mid, gain, weight, arrived, gp, up, inner, *own, *other)


class Line:
    def __init__(self, n, sems, zup, zdn, stage, acc):
        self.n = n
        self.me = lax.axis_index("gx")
        self.sems = sems
        self.zup, self.zdn, self.stage, self.acc = zup, zdn, stage, acc
        self.z_list = []
        for k in range((n + 1) // 2):
            self.z_list += [n - 1 - k] + ([k] if k != n - 1 - k else [])

    def up(self, z):
        su, ru = self.sems[:2]
        return remote(self.stage.at[z], self.zup.at[z], su.at[z], ru.at[z], gx=self.me + 1)

    def down(self, z):
        sd, rd = self.sems[2:]
        return remote(self.stage.at[z], self.zdn.at[z], sd.at[z], rd.at[z], gx=self.me - 1)

    def move(self, z, total):
        n, me, acc = self.n, self.me, self.acc

        @pl.when((me < z) & (me > 0))
        def _():
            self.up(z).wait_recv()
            add_rows(acc, acc, self.zup.at[z])

        @pl.when((me > z) & (me < n - 1))
        def _():
            self.down(z).wait_recv()
            add_rows(acc, acc, self.zdn.at[z])

        @pl.when(me != z)
        def _():
            add_rows(self.stage.at[z], acc)

        @pl.when(me < z)
        def _():
            self.up(z).start()

        @pl.when(me > z)
        def _():
            self.down(z).start()

        @pl.when(me == z)
        def _():
            add_rows(total, acc)

    def finish(self, total):
        n, me = self.n, self.me

        @pl.when(me > 0)
        def _():
            self.up(me).wait_recv()
            add_rows(total, total, self.zup.at[me])

        @pl.when(me < n - 1)
        def _():
            self.down(me).wait_recv()
            add_rows(total, total, self.zdn.at[me])

        for z in self.z_list:

            @pl.when(me < z)
            def _():
                self.up(z).wait_send()

            @pl.when(me > z)
            def _():
                self.down(z).wait_send()


def unit_of(value):
    scale = lax.rsqrt(jnp.mean(value * value, axis=-1, keepdims=True) + EPSILON)
    return value * scale, scale


def half_turn(value):
    return pltpu.roll(value, value.shape[-1] // 2, axis=value.ndim - 1)


def attn_forward_kernel(
    n,
    layer,
    heads,
    x_ref,
    gain_attn,
    gain_ffn,
    gain_query,
    gain_key,
    cos_ref,
    sin_ref,
    mask_ref,
    gates_ref,
    win_own,
    wout_own,
    win_other,
    wout_other,
    mid_ref,
    pay_ref,
    normed_hbm,
    proj_hbm,
    qr_hbm,
    kr_ref,
    v_ref,
    prob_hbm,
    mixed_hbm,
    win,
    wout,
    normed,
    proj,
    qr,
    prob,
    mixed,
    col,
    zup,
    zdn,
    stage,
    acc,
    total,
    wsem,
    osem,
    *sems,
):
    mb, length, d = normed.shape
    t = length // n
    r = mb * t
    span = heads * HD
    me = lax.axis_index("gx")
    own, other, held = (win_own, wout_own), (win_other, wout_other), (win, wout)
    fetch_layer(layer, own, other, held, wsem)
    hello(n, me, None, False)
    hidden = x_ref[...].astype(F32)
    unit, _ = unit_of(hidden)
    low = (unit * gain_attn[...]).astype(BF16)
    normed[:, pl.ds(pl.multiple_of(me * t, t), t)] = low.reshape(mb, t, d)

    def slot(z):
        return normed.at[:, pl.ds(z * t, t)]

    z_gather_steps(n, me, slot, sems[:4], lambda z, k: None)
    saves = [
        pltpu.make_async_copy(normed, normed_hbm, osem.at[0]),
        pltpu.make_async_copy(proj, proj_hbm, osem.at[1]),
        pltpu.make_async_copy(qr, qr_hbm, osem.at[2]),
        pltpu.make_async_copy(prob, prob_hbm, osem.at[3]),
        pltpu.make_async_copy(mixed, mixed_hbm, osem.at[4]),
    ]
    saves[0].start()
    fetch_wait(own, held, wsem, (0,))
    every = normed[...].reshape(mb * length, d)
    for j in range((span + 2 * HD) // 256):
        cols = slice(j * 256, (j + 1) * 256)
        proj[:, cols] = jnp.dot(every, win[:, cols], preferred_element_type=F32)
    saves[1].start()
    cosine, sine = cos_ref[...], sin_ref[...]
    key_unit, _ = unit_of(proj[:, span : span + HD])
    key = key_unit * gain_key[...]
    kr_ref[...] = (key * cosine + half_turn(key) * sine).astype(BF16)
    v_ref[...] = proj[:, span + HD :].astype(BF16)

    def head(h, carry):
        at = pl.ds(pl.multiple_of(h * HD, HD), HD)
        query_unit, _ = unit_of(proj[:, at])
        query = query_unit * gain_query[...]
        turned = (query * cosine + half_turn(query) * sine).astype(BF16)
        qr[:, at] = turned
        for m in range(mb):
            rows = slice(m * length, (m + 1) * length)
            scores = dot32(turned[rows], kr_ref[rows], COL_PAIR) * (1.0 / math.sqrt(HD))
            exponent = jnp.where(mask_ref[m] > 0.5, jnp.exp(scores), 0.0)
            p = (exponent / jnp.sum(exponent, axis=-1, keepdims=True)).astype(BF16)
            prob[m * heads + h] = p
            mixed[rows, at] = jnp.dot(p, v_ref[rows], preferred_element_type=F32).astype(BF16)
        return carry

    lax.fori_loop(0, heads, head, 0)
    saves[2].start()
    saves[3].start()
    saves[4].start()
    fetch_wait(own, held, wsem, (1,))
    both = mixed[...]

    def out_cols(j, carry):
        at = pl.ds(pl.multiple_of(j * 256, 256), 256)
        res = dot32(both, wout[at], COL_PAIR).astype(BF16)
        for m in range(mb):
            for z in range(n):
                col[z, m * t : (m + 1) * t, at] = res[m * length + z * t : m * length + (z + 1) * t]
        return carry

    lax.fori_loop(0, d // 256, out_cols, 0)
    line = Line(n, sems[4:], zup, zdn, stage, acc)
    for z in line.z_list:
        add_rows(acc, col.at[z])
        line.move(z, total)
    line.finish(total)
    mid = x_ref[...].astype(F32) + total[...]
    mid_ref[...] = mid
    unit, _ = unit_of(mid)
    pay_ref[:, :d] = (unit * gain_ffn[...]).astype(BF16)
    pay_ref[:, d:] = gates_ref[...]
    z_gather_drain(n, me, slot, sems[:4])
    for save in saves:
        save.wait()


def line_buffers(n, r, d):
    return [pltpu.VMEM((n, r, d), BF16)] * 4 + [pltpu.VMEM((r, d), F32)] * 2


def attn_forward(layer, n, x, gains, tables, gate_cols, own, other, cid, mb):
    r, d = x.shape
    cosine, sine, mask = tables
    total_rows = cosine.shape[0]
    length = total_rows // mb
    width = own[0].shape[1]
    heads = own[1].shape[1] // HD
    span = heads * HD
    shape = jax.ShapeDtypeStruct
    return pl.pallas_call(
        functools.partial(attn_forward_kernel, n, layer, heads),
        out_shape=(
            shape((r, d), F32),
            shape((r, d + 128), BF16),
            shape((mb, length, d), BF16),
            shape((total_rows, width), F32),
            shape((total_rows, span), BF16),
            shape((total_rows, HD), BF16),
            shape((total_rows, HD), BF16),
            shape((mb * heads, length, length), BF16),
            shape((total_rows, span), BF16),
        ),
        in_specs=in_vmem(9) + in_place(4),
        out_specs=tuple(in_vmem(2) + in_place(3) + in_vmem(2) + in_place(2)),
        scratch_shapes=[
            pltpu.VMEM((d, width), BF16),
            pltpu.VMEM((d, span), BF16),
            pltpu.VMEM((mb, length, d), BF16),
            pltpu.VMEM((total_rows, width), F32),
            pltpu.VMEM((total_rows, span), BF16),
            pltpu.VMEM((mb * heads, length, length), BF16),
            pltpu.VMEM((total_rows, span), BF16),
        ]
        + line_buffers(n, r, d)
        + [pltpu.SemaphoreType.DMA((2,)), pltpu.SemaphoreType.DMA((5,))]
        + [pltpu.SemaphoreType.DMA((n,))] * 8,
        compiler_params=pltpu.CompilerParams(
            collective_id=cid, has_side_effects=True, vmem_limit_bytes=60 << 20
        ),
        name="attn_forward",
    )(x, *gains, cosine, sine, mask, gate_cols, *own, *other)


def attn_backward_kernel(
    n,
    layer,
    heads,
    dmid_ref,
    x_ref,
    gain_attn,
    gain_query,
    gain_key,
    cos_ref,
    sin_ref,
    kr_ref,
    v_ref,
    normed_hbm,
    proj_hbm,
    qr_hbm,
    prob_hbm,
    mixed_hbm,
    win_own,
    wout_own,
    win_other,
    wout_other,
    cot_ref,
    dgain_attn,
    dgain_query,
    dgain_key,
    grad_in_hbm,
    grad_out_hbm,
    win,
    wout,
    normed,
    proj,
    qr,
    prob,
    mixed,
    dmids,
    dheads,
    dproj,
    dkey,
    dvalue,
    grad_in,
    grad_out,
    col,
    zup,
    zdn,
    stage,
    acc,
    total,
    wsem,
    isem,
    osem,
    *sems,
):
    mb, length, d = normed.shape
    t = length // n
    span = heads * HD
    me = lax.axis_index("gx")
    inv_root = 1.0 / math.sqrt(HD)
    own, other, held = (wout_own, win_own), (wout_other, win_other), (wout, win)
    fetch_layer(layer, own, other, held, wsem)
    loads = [
        pltpu.make_async_copy(prob_hbm, prob, isem.at[0]),
        pltpu.make_async_copy(mixed_hbm, mixed, isem.at[1]),
        pltpu.make_async_copy(qr_hbm, qr, isem.at[2]),
        pltpu.make_async_copy(proj_hbm, proj, isem.at[3]),
        pltpu.make_async_copy(normed_hbm, normed, isem.at[4]),
    ]
    for load in loads:
        load.start()
    hello(n, me, None, False)
    dmids[:, pl.ds(pl.multiple_of(me * t, t), t)] = dmid_ref[...].astype(BF16).reshape(mb, t, d)

    def slot(z):
        return dmids.at[:, pl.ds(z * t, t)]

    z_gather_steps(n, me, slot, sems[:4], lambda z, k: None)
    fetch_wait(own, held, wsem, (0,))
    every = dmids[...].reshape(mb * length, d)
    for j in range(span // 256):
        cols = slice(j * 256, (j + 1) * 256)
        dheads[:, cols] = jnp.dot(every, wout[:, cols], preferred_element_type=F32).astype(BF16)
    for load in loads:
        load.wait()
    cosine, sine = cos_ref[...], sin_ref[...]
    dkey[...] = jnp.zeros_like(dkey)
    dvalue[...] = jnp.zeros_like(dvalue)
    dgain_query[...] = jnp.zeros_like(dgain_query)

    def head(h, carry):
        at = pl.ds(pl.multiple_of(h * HD, HD), HD)
        for m in range(mb):
            rows = slice(m * length, (m + 1) * length)
            p = prob[m * heads + h]
            dh = dheads[rows, at]
            dvalue[rows] += dot32(p, dh, ROW_PAIR)
            dp = dot32(dh, v_ref[rows], COL_PAIR)
            delta = jnp.sum(
                dh.astype(F32) * mixed[rows, at].astype(F32), axis=-1, keepdims=True
            )
            ds = (p.astype(F32) * (dp - delta)).astype(BF16)
            dkey[rows] += dot32(ds, qr[rows, at], ROW_PAIR) * inv_root
            dq = jnp.dot(ds, kr_ref[rows], preferred_element_type=F32) * inv_root
            turned = dq * cosine[rows] - half_turn(dq) * sine[rows]
            unit, scale = unit_of(proj[rows, at])
            dgain_query[...] += jnp.sum(turned * unit, axis=0, keepdims=True)
            dproj[rows, at] = norm_back(turned * gain_query[...], unit, scale).astype(BF16)
        return carry

    lax.fori_loop(0, heads, head, 0)
    dk = dkey[...]
    turned = dk * cosine - half_turn(dk) * sine
    unit, scale = unit_of(proj[:, span : span + HD])
    dgain_key[...] = jnp.sum(turned * unit, axis=0, keepdims=True)
    dproj[:, span : span + HD] = norm_back(turned * gain_key[...], unit, scale).astype(BF16)
    dproj[:, span + HD :] = dvalue[...].astype(BF16)
    fetch_wait(own, held, wsem, (1,))
    both = dproj[...]

    def in_cols(j, carry):
        at = pl.ds(pl.multiple_of(j * 256, 256), 256)
        res = dot32(both, win[at], COL_PAIR).astype(BF16)
        for m in range(mb):
            for z in range(n):
                col[z, m * t : (m + 1) * t, at] = res[m * length + z * t : m * length + (z + 1) * t]
        return carry

    lax.fori_loop(0, d // 256, in_cols, 0)
    line = Line(n, sems[4:], zup, zdn, stage, acc)

    def chunk_saves(i):
        at = pl.ds(pl.multiple_of(i * 256, 256), 256)
        return (
            pltpu.make_async_copy(grad_in.at[at], grad_in_hbm.at[at], osem.at[0, i]),
            pltpu.make_async_copy(grad_out.at[at], grad_out_hbm.at[at], osem.at[1, i]),
        )

    def weight_grads(first, last):
        def chunk(i, carry):
            at = pl.ds(pl.multiple_of(i * 256, 256), 256)
            left = normed[:, :, at].reshape(mb * length, 256)
            grad_in[at] = dot32(left, dproj[...], ROW_PAIR).astype(BF16)
            left = dmids[:, :, at].reshape(mb * length, 256)
            grad_out[at] = dot32(left, mixed[...], ROW_PAIR).astype(BF16)
            for save in chunk_saves(i):
                save.start()
            return carry

        lax.fori_loop(first, last, chunk, 0)

    chunks = d // 256
    for k, z in enumerate(line.z_list):
        add_rows(acc, col.at[z])
        line.move(z, total)
        weight_grads(chunks * k // len(line.z_list), chunks * (k + 1) // len(line.z_list))
    line.finish(total)
    hidden = x_ref[...].astype(F32)
    unit, scale = unit_of(hidden)
    da = total[...]
    dgain_attn[...] = jnp.sum(da * unit, axis=0, keepdims=True)
    cot_ref[...] = (dmid_ref[...] + norm_back(da * gain_attn[...], unit, scale)).astype(BF16)
    z_gather_drain(n, me, slot, sems[:4])
    for i in range(chunks):
        for save in chunk_saves(i):
            save.wait()


def attn_backward(layer, n, dmid, x, gains, tables, kept, own, other, cid, mb):
    r, d = x.shape
    cosine, sine, _ = tables
    normed, proj, qr, kr, v, prob, mixed = kept
    total_rows = cosine.shape[0]
    length = total_rows // mb
    width = own[0].shape[1]
    heads = own[1].shape[1] // HD
    span = heads * HD
    shape = jax.ShapeDtypeStruct
    return pl.pallas_call(
        functools.partial(attn_backward_kernel, n, layer, heads),
        out_shape=(
            shape((r, d), BF16),
            shape((1, d), F32),
            shape((1, HD), F32),
            shape((1, HD), F32),
            shape((d, width), BF16),
            shape((d, span), BF16),
        ),
        in_specs=in_vmem(9) + in_place(9),
        out_specs=tuple(in_vmem(4) + in_place(2)),
        scratch_shapes=[
            pltpu.VMEM((d, width), BF16),
            pltpu.VMEM((d, span), BF16),
            pltpu.VMEM((mb, length, d), BF16),
            pltpu.VMEM((total_rows, width), F32),
            pltpu.VMEM((total_rows, span), BF16),
            pltpu.VMEM((mb * heads, length, length), BF16),
            pltpu.VMEM((total_rows, span), BF16),
            pltpu.VMEM((mb, length, d), BF16),
            pltpu.VMEM((total_rows, span), BF16),
            pltpu.VMEM((total_rows, width), BF16),
            pltpu.VMEM((total_rows, HD), F32),
            pltpu.VMEM((total_rows, HD), F32),
            pltpu.VMEM((d, width), BF16),
            pltpu.VMEM((d, span), BF16),
        ]
        + line_buffers(n, r, d)
        + [
            pltpu.SemaphoreType.DMA((2,)),
            pltpu.SemaphoreType.DMA((5,)),
            pltpu.SemaphoreType.DMA((2, d // 256)),
        ]
        + [pltpu.SemaphoreType.DMA((n,))] * 8,
        compiler_params=pltpu.CompilerParams(
            collective_id=cid, has_side_effects=True, vmem_limit_bytes=60 << 20
        ),
        name="attn_backward",
    )(
        dmid,
        x,
        *gains,
        cosine,
        sine,
        kr,
        v,
        normed,
        proj,
        qr,
        prob,
        mixed,
        *own,
        *other,
    )


def local_wide(
    inputs,
    out_grad,
    segments,
    routes,
    gates,
    gain_attn,
    gain_ffn,
    gain_query,
    gain_key,
    w_query,
    w_key,
    w_value,
    w_out,
    w_gate,
    w_up,
    w_down,
):
    micro_count, _, local_rows, width = inputs.shape
    n_sec = lax.axis_size("section")
    n_gx = lax.axis_size("gx")
    n_gy = lax.axis_size("gy")
    heads = w_query.shape[2] // HD
    span = heads * HD
    experts = n_gx * n_gy
    group_len = segments.shape[2]
    mb = micro_count // n_sec
    rows_own = mb * local_rows
    rows_attn = mb * group_len
    section = lax.axis_index("section")
    gx = lax.axis_index("gx")
    gy = lax.axis_index("gy")
    expert_own = gx * n_gy + gy
    inv_root = 1.0 / math.sqrt(HD)
    first = section * mb

    kv_head = gx * heads // (HQ // KVH)
    key_own = lax.dynamic_slice_in_dim(w_key[0], kv_head * HD, HD, 1)
    value_own = lax.dynamic_slice_in_dim(w_value[0], kv_head * HD, HD, 1)
    w_in_shard = jnp.concatenate([w_query[0], key_own, value_own], axis=1)
    w_in_all = both_layers(lax.all_gather(w_in_shard, "gy", axis=0, tiled=True))
    w_out_all = both_layers(lax.all_gather(w_out[0], "gy", axis=0, tiled=True))
    w_gate_all = both_layers(w_gate[0, 0])
    w_up_all = both_layers(w_up[0, 0])
    w_down_all = both_layers(w_down[0, 0])
    table = dense_gates(routes[0, :, 0], gates[0, :, 0], experts)
    small = jnp.concatenate(
        [
            table.reshape(-1),
            gain_attn[0],
            gain_ffn[0],
            gain_query[0],
            gain_key[0],
        ]
    )
    small_all = both_layers(small)
    table_size = micro_count * local_rows * experts
    table_all = small_all[:, :table_size].reshape(n_sec, micro_count, local_rows, experts)
    gains_all = small_all[:, table_size:]

    table_mine = lax.dynamic_slice_in_dim(table_all, first, mb, 1).reshape(
        n_sec, rows_own, experts
    )
    x_mine = lax.dynamic_slice_in_dim(inputs[:, 0], first, mb, 0).reshape(rows_own, width)
    cot_mine = lax.dynamic_slice_in_dim(out_grad[:, 0], first, mb, 0).reshape(rows_own, width)
    segs = lax.dynamic_slice_in_dim(segments[:, 0], first, mb, 0)
    allowed, cosine, sine = seq_tables(segs, HD)
    cos_q = cosine.reshape(rows_attn, 1, HD // 2)
    sin_q = sine.reshape(rows_attn, 1, HD // 2)
    cos_k = cosine.reshape(rows_attn, HD // 2)
    sin_k = sine.reshape(rows_attn, HD // 2)

    def split_gains(layer):
        g = gains_all[layer]
        return (
            g[:width],
            g[width : 2 * width],
            g[2 * width : 2 * width + HD],
            g[2 * width + HD :],
        )

    saved_all = []
    outs = []
    layer_in = x_mine
    for layer in range(n_sec):
        g_attn, g_ffn, g_query, g_key = split_gains(layer)
        hidden = layer_in.astype(F32)
        attn_unit, attn_scale = normalize(hidden)
        normed = (attn_unit * g_attn).astype(BF16)
        normed_all = gather_z(normed.reshape(mb, local_rows, width)).reshape(rows_attn, width)
        projected = dot32(normed_all, w_in_all[layer])
        query = projected[:, :span].reshape(rows_attn, heads, HD)
        key = projected[:, span : span + HD]
        value_low = projected[:, span + HD :].astype(BF16).reshape(mb, group_len, HD)
        query_unit, query_scale = normalize(query)
        key_unit, key_scale = normalize(key)
        query_rope = (
            rotate(query_unit * g_query, cos_q, sin_q)
            .astype(BF16)
            .reshape(mb, group_len, heads, HD)
        )
        key_rope = rotate(key_unit * g_key, cos_k, sin_k).astype(BF16).reshape(mb, group_len, HD)
        scores = (
            jnp.einsum("mthd,msd->mhts", query_rope, key_rope, preferred_element_type=F32)
            * inv_root
        )
        exponent = jnp.where(allowed[:, None], jnp.exp(scores), 0.0)
        log_total = jnp.log(jnp.sum(exponent, axis=-1, keepdims=True))
        prob = jnp.where(allowed[:, None], jnp.exp(scores - log_total), 0.0)
        mixed = (
            jnp.einsum("mhts,msd->mthd", prob.astype(BF16), value_low, preferred_element_type=F32)
            .astype(BF16)
            .reshape(rows_attn, span)
        )
        attn_part = dot32(mixed, w_out_all[layer], COL_PAIR).astype(BF16)
        attn_out = scatter_z(attn_part.reshape(mb, group_len, width)).reshape(rows_own, width)
        middle = hidden + attn_out.astype(F32)
        ffn_unit, ffn_scale = normalize(middle)
        expert_in = (ffn_unit * g_ffn).astype(BF16)
        tab = table_mine[layer]
        tab_hi = tab.astype(BF16)
        tab_lo = (tab - tab_hi.astype(F32)).astype(BF16)
        payload = jnp.concatenate([expert_in, tab_hi, tab_lo], axis=1)
        arrived_all = gather_all(payload)
        arrived = arrived_all[:, :width]
        gate_cols = arrived_all[:, width:].astype(F32)
        is_mine = jnp.arange(2 * experts) % experts == expert_own
        weight = jnp.sum(jnp.where(is_mine[None], gate_cols, 0.0), axis=1, keepdims=True)
        gate_pre = dot32(arrived, w_gate_all[layer])
        up_proj = dot32(arrived, w_up_all[layer])
        inner = (jax.nn.silu(gate_pre) * up_proj).astype(BF16)
        result = dot32(inner, w_down_all[layer])
        weighted = (result * weight).astype(BF16)
        expert_sum = scatter_all(weighted)
        layer_out = (middle + expert_sum.astype(F32)).astype(BF16)
        outs.append(layer_out)
        layer_in = layer_out
        saved_all.append(
            (
                attn_unit,
                attn_scale,
                normed_all,
                query_unit,
                query_scale,
                key_unit,
                key_scale,
                query_rope,
                key_rope,
                value_low,
                prob,
                mixed,
                ffn_unit,
                ffn_scale,
                arrived,
                weight,
                gate_pre,
                up_proj,
                inner,
            )
        )

    cot = cot_mine
    in_grads = [None] * n_sec
    expert_grads = [None] * n_sec
    attn_grads = [None] * n_sec
    gain_grads = [None] * n_sec
    for layer in reversed(range(n_sec)):
        g_attn, g_ffn, g_query, g_key = split_gains(layer)
        (
            attn_unit,
            attn_scale,
            normed_all,
            query_unit,
            query_scale,
            key_unit,
            key_scale,
            query_rope,
            key_rope,
            value_low,
            prob,
            mixed,
            ffn_unit,
            ffn_scale,
            arrived,
            weight,
            gate_pre,
            up_proj,
            inner,
        ) = saved_all[layer]
        gradient = cot.astype(F32)
        grad_all = gather_all(cot)
        grad_result = (grad_all.astype(F32) * weight).astype(BF16)
        grad_inner = dot32(grad_result, w_down_all[layer], COL_PAIR)
        grad_down = dot32(inner, grad_result, ROW_PAIR)
        sig = jax.nn.sigmoid(gate_pre)
        grad_gate_pre = (grad_inner * up_proj * sig * (1.0 + gate_pre * (1.0 - sig))).astype(BF16)
        grad_up_proj = (grad_inner * gate_pre * sig).astype(BF16)
        grad_gate = dot32(arrived, grad_gate_pre, ROW_PAIR)
        grad_up = dot32(arrived, grad_up_proj, ROW_PAIR)
        grad_arrived = (
            dot32(grad_gate_pre, w_gate_all[layer], COL_PAIR)
            + dot32(grad_up_proj, w_up_all[layer], COL_PAIR)
        ).astype(BF16)
        expert_grads[layer] = (grad_gate, grad_up, grad_down)
        grad_expert_in = scatter_all(grad_arrived).astype(F32)
        grad_ffn_gain = jnp.sum(grad_expert_in * ffn_unit, axis=0)
        grad_middle = gradient + norm_back(grad_expert_in * g_ffn, ffn_unit, ffn_scale)
        middle_low = grad_middle.astype(BF16)
        middle_all = gather_z(middle_low.reshape(mb, local_rows, width)).reshape(rows_attn, width)
        grad_out_w = dot32(middle_all, mixed, ROW_PAIR)
        grad_heads = (
            dot32(middle_all, w_out_all[layer]).astype(BF16).reshape(mb, group_len, heads, HD)
        )
        grad_value = jnp.einsum(
            "mhts,mthd->mshd", prob.astype(BF16), grad_heads, preferred_element_type=F32
        )
        grad_prob = jnp.einsum(
            "mthd,msd->mhts", grad_heads, value_low, preferred_element_type=F32
        )
        mixed_split = mixed.reshape(mb, group_len, heads, HD)
        delta = jnp.sum(grad_heads.astype(F32) * mixed_split.astype(F32), axis=-1)
        delta = jnp.swapaxes(delta, 1, 2)[..., None]
        grad_scores = (prob * (grad_prob - delta)).astype(BF16)
        grad_query = (
            jnp.einsum("mhts,msd->mthd", grad_scores, key_rope, preferred_element_type=F32)
            * inv_root
        ).reshape(rows_attn, heads, HD)
        grad_key = (
            jnp.einsum("mhts,mthd->mshd", grad_scores, query_rope, preferred_element_type=F32)
            * inv_root
        ).reshape(rows_attn, heads, HD)
        query_turn = rotate_back(grad_query, cos_q, sin_q)
        grad_query_gain = jnp.sum(query_turn * query_unit, axis=(0, 1))
        grad_query_pre = norm_back(query_turn * g_query, query_unit, query_scale)
        key_turn = rotate_back(jnp.sum(grad_key, axis=1), cos_k, sin_k)
        grad_key_gain = jnp.sum(key_turn * key_unit, axis=0)
        grad_key_pre = norm_back(key_turn * g_key, key_unit, key_scale)
        grad_proj = jnp.concatenate(
            [
                grad_query_pre.reshape(rows_attn, span),
                grad_key_pre,
                jnp.sum(grad_value, axis=2).reshape(rows_attn, HD),
            ],
            axis=1,
        ).astype(BF16)
        grad_in_w = dot32(normed_all, grad_proj, ROW_PAIR)
        normed_part = dot32(grad_proj, w_in_all[layer], COL_PAIR).astype(BF16)
        grad_normed = (
            scatter_z(normed_part.reshape(mb, group_len, width))
            .reshape(rows_own, width)
            .astype(F32)
        )
        grad_attn_gain = jnp.sum(grad_normed * attn_unit, axis=0)
        cot = (grad_middle + norm_back(grad_normed * g_attn, attn_unit, attn_scale)).astype(BF16)
        in_grads[layer] = cot
        attn_grads[layer] = jnp.concatenate([grad_in_w, grad_out_w], axis=1).astype(BF16)
        gain_grads[layer] = jnp.concatenate(
            [grad_attn_gain, grad_ffn_gain, grad_query_gain, grad_key_gain]
        )

    def own_layer_sum(pieces):
        return lax.psum_scatter(
            jnp.stack([piece.astype(BF16) for piece in pieces]),
            "section",
            scatter_dimension=0,
            tiled=True,
        ).astype(F32)

    grad_gate, grad_up, grad_down = (
        own_layer_sum([expert_grads[layer][k] for layer in range(n_sec)]) for k in range(3)
    )
    attn_sum = lax.psum_scatter(
        jnp.concatenate(attn_grads, axis=0), ("section", "gy"), scatter_dimension=0, tiled=True
    ).astype(F32)
    query_grad = attn_sum[:, :span]
    out_w_grad = attn_sum[:, span + 2 * HD :]
    kv_all = lax.all_gather(attn_sum[:, span : span + 2 * HD], "gx", axis=0, tiled=False)
    kv_all = jnp.sum(kv_all.reshape(KVH, n_gx // KVH, -1, 2, HD), axis=1)
    key_part = jnp.swapaxes(kv_all[:, :, 0], 0, 1).reshape(-1, KVH * HD)
    value_part = jnp.swapaxes(kv_all[:, :, 1], 0, 1).reshape(-1, KVH * HD)
    gain_sum = lax.psum(jnp.stack(gain_grads), ("section", "gx", "gy"))
    gain_sum = lax.dynamic_index_in_dim(gain_sum, section, 0, keepdims=True)

    def own_layer_rows(pieces):
        stacked = jnp.stack(pieces).reshape(n_sec, mb, local_rows, width)
        return lax.all_to_all(stacked, "section", split_axis=0, concat_axis=0, tiled=True).reshape(
            1, micro_count, 1, local_rows, width
        )

    return (
        own_layer_rows(outs),
        own_layer_rows(in_grads),
        gain_sum[:, :width],
        gain_sum[:, width : 2 * width],
        gain_sum[:, 2 * width : 2 * width + HD],
        gain_sum[:, 2 * width + HD :],
        query_grad[None],
        key_part[None],
        value_part[None],
        out_w_grad[None],
        grad_gate[:, None],
        grad_up[:, None],
        grad_down[:, None],
    )


def local_fused(
    inputs,
    out_grad,
    segments,
    routes,
    gates,
    gain_attn,
    gain_ffn,
    gain_query,
    gain_key,
    w_query,
    w_key,
    w_value,
    w_out,
    w_gate,
    w_up,
    w_down,
):
    micro_count, _, local_rows, width = inputs.shape
    n_sec = lax.axis_size("section")
    n_gx = lax.axis_size("gx")
    n_gy = lax.axis_size("gy")
    heads = w_query.shape[2] // HD
    span = heads * HD
    experts = n_gx * n_gy
    group_len = segments.shape[2]
    mb = micro_count // n_sec
    rows_own = mb * local_rows
    rows_attn = mb * group_len
    section = lax.axis_index("section")
    gx = lax.axis_index("gx")
    first = section * mb

    kv_head = gx * heads // (HQ // KVH)
    key_own = lax.dynamic_slice_in_dim(w_key[0], kv_head * HD, HD, 1)
    value_own = lax.dynamic_slice_in_dim(w_value[0], kv_head * HD, HD, 1)
    w_in_shard = jnp.concatenate([w_query[0], key_own, value_own], axis=1)
    attn_own = (
        lax.all_gather(w_in_shard, "gy", axis=0, tiled=True),
        lax.all_gather(w_out[0], "gy", axis=0, tiled=True),
    )
    moe_own = (w_gate[0, 0], w_up[0, 0], w_down[0, 0])
    attn_other = tuple(swap_sections(w) for w in attn_own)
    moe_other = tuple(swap_sections(w) for w in moe_own)
    table = dense_gates(routes[0, :, 0], gates[0, :, 0], experts)
    small = jnp.concatenate(
        [table.reshape(-1), gain_attn[0], gain_ffn[0], gain_query[0], gain_key[0]]
    )
    small_all = both_layers(small)
    table_size = micro_count * local_rows * experts
    table_all = small_all[:, :table_size].reshape(n_sec, micro_count, local_rows, experts)
    gains_all = small_all[:, table_size:]
    table_mine = lax.dynamic_slice_in_dim(table_all, first, mb, 1).reshape(
        n_sec, rows_own, experts
    )
    x_mine = lax.dynamic_slice_in_dim(inputs[:, 0], first, mb, 0).reshape(rows_own, width)
    cot = lax.dynamic_slice_in_dim(out_grad[:, 0], first, mb, 0).reshape(rows_own, width)
    segs = lax.dynamic_slice_in_dim(segments[:, 0], first, mb, 0)
    allowed, cosine, sine = seq_tables(segs, HD)
    tables = (
        jnp.concatenate([cosine, cosine], axis=-1).reshape(rows_attn, HD),
        jnp.concatenate([-sine, sine], axis=-1).reshape(rows_attn, HD),
        allowed.astype(F32),
    )

    def split_gains(layer):
        g = gains_all[layer : layer + 1]
        return (
            g[:, :width],
            g[:, width : 2 * width],
            g[:, 2 * width : 2 * width + HD],
            g[:, 2 * width + HD :],
        )

    kept = []
    outs = []
    layer_in = x_mine
    for layer in range(n_sec):
        tab = table_mine[layer]
        tab_hi = tab.astype(BF16)
        tab_lo = (tab - tab_hi.astype(F32)).astype(BF16)
        pad = jnp.zeros((rows_own, 128 - 2 * experts), BF16)
        gate_cols = jnp.concatenate([tab_hi, tab_lo, pad], axis=1)
        mid, payload, normed, proj, qr, kr, v, prob, mixed = attn_forward(
            layer,
            n_gx,
            layer_in,
            split_gains(layer),
            tables,
            gate_cols,
            attn_own,
            attn_other,
            1 + layer,
            mb,
        )
        layer_out, *moe_kept = moe_forward(
            layer, n_gx, mid, payload, moe_own, moe_other, 3 + layer
        )
        kept.append((layer_in, mid, (normed, proj, qr, kr, v, prob, mixed), moe_kept))
        outs.append(layer_out)
        layer_in = layer_out

    in_grads = [None] * n_sec
    moe_grads = [None] * n_sec
    attn_grads = [None] * n_sec
    gain_grads = [None] * n_sec
    for layer in reversed(range(n_sec)):
        g_attn, g_ffn, g_query, g_key = split_gains(layer)
        layer_in, mid, attn_kept, (arrived, weight, gp, up, inner) = kept[layer]
        dmid, d_ffn, *moe_grads[layer] = moe_backward(
            layer,
            n_gx,
            cot,
            mid,
            g_ffn,
            weight,
            arrived,
            gp,
            up,
            inner,
            moe_own,
            moe_other,
            5 + layer,
        )
        cot, d_attn, d_query, d_key, *attn_grads[layer] = attn_backward(
            layer,
            n_gx,
            dmid,
            layer_in,
            (g_attn, g_query, g_key),
            tables,
            attn_kept,
            attn_own,
            attn_other,
            7 + layer,
            mb,
        )
        in_grads[layer] = cot
        gain_grads[layer] = jnp.concatenate([d_attn, d_ffn, d_query, d_key], axis=1)

    def own_layer_sum(pieces):
        from_other = [
            lax.ppermute(piece, "section", [(1 - layer, layer)])
            for layer, piece in enumerate(pieces)
        ]
        sums = [a.astype(F32) + b.astype(F32) for a, b in zip(pieces, from_other)]
        return jnp.where(section == 0, sums[0], sums[1])

    grad_gate, grad_up, grad_down = (
        own_layer_sum([moe_grads[layer][k] for layer in range(n_sec)])[None] for k in range(3)
    )
    grad_in, grad_out = (
        lax.psum_scatter(
            own_layer_sum([attn_grads[layer][k] for layer in range(n_sec)]).astype(BF16),
            "gy",
            scatter_dimension=0,
            tiled=True,
        ).astype(F32)
        for k in range(2)
    )
    query_grad = grad_in[:, :span]
    kv_all = lax.all_gather(grad_in[:, span:], "gx", axis=0, tiled=False)
    kv_all = jnp.sum(kv_all.reshape(KVH, n_gx // KVH, -1, 2, HD), axis=1)
    key_part = jnp.swapaxes(kv_all[:, :, 0], 0, 1).reshape(-1, KVH * HD)
    value_part = jnp.swapaxes(kv_all[:, :, 1], 0, 1).reshape(-1, KVH * HD)
    gain_sum = lax.psum(jnp.concatenate(gain_grads, axis=0), ("section", "gx", "gy"))
    gain_sum = lax.dynamic_index_in_dim(gain_sum, section, 0, keepdims=True)

    def own_layer_rows(pieces):
        stacked = jnp.stack(pieces).reshape(n_sec, mb, local_rows, width)
        return lax.all_to_all(stacked, "section", split_axis=0, concat_axis=0, tiled=True).reshape(
            1, micro_count, 1, local_rows, width
        )

    return (
        own_layer_rows(outs),
        own_layer_rows(in_grads),
        gain_sum[:, :width],
        gain_sum[:, width : 2 * width],
        gain_sum[:, 2 * width : 2 * width + HD],
        gain_sum[:, 2 * width + HD :],
        query_grad[None],
        key_part[None],
        value_part[None],
        grad_out[None],
        grad_gate[:, None],
        grad_up[:, None],
        grad_down[:, None],
    )


def local(*args):
    inputs = args[0]
    n = lax.axis_size("gx")
    rows_own = inputs.shape[0] // lax.axis_size("section") * inputs.shape[2]
    if 4 * n * rows_own > MOST_ROWS:
        return local_wide(*args)
    return local_fused(*args)


def solution(mesh):
    return jax.shard_map(
        local,
        mesh=mesh,
        in_specs=(
            P(None, "gy", "gx", None),
            P(None, "gy", "gx", None),
            P(None, "gy", None),
            P("section", None, "gy", "gx", None),
            P("section", None, "gy", "gx", None),
            P("section", None),
            P("section", None),
            P("section", None),
            P("section", None),
            P("section", "gy", "gx"),
            P("section", "gy", None),
            P("section", "gy", None),
            P("section", "gy", "gx"),
            P("section", ("gx", "gy"), None, None),
            P("section", ("gx", "gy"), None, None),
            P("section", ("gx", "gy"), None, None),
        ),
        out_specs=(
            P("section", None, "gy", "gx", None),
            P("section", None, "gy", "gx", None),
            P("section", None),
            P("section", None),
            P("section", None),
            P("section", None),
            P("section", "gy", "gx"),
            P("section", "gy", None),
            P("section", "gy", None),
            P("section", "gy", "gx"),
            P("section", ("gx", "gy"), None, None),
            P("section", ("gx", "gy"), None, None),
            P("section", ("gx", "gy"), None, None),
        ),
        check_vma=False,
    )
```

time: 2480 us -> 961 us (0.39)
  waiting for transfers between devices: 884 us -> 175 us
  blocking collectives: 691 us -> 72.4 us
  Pallas kernels: 0 us -> 588 us
  matrix products: 511 us -> 0 us
  local copies, waits for them, and re-layouts: 124 us -> 19 us
  other arithmetic: 153 us -> 54 us
  starting transfers between devices: 89.8 us -> 30.3 us
    pallas_call x0 -> x8, Pallas kernels: none -> 588 us  [the longest x2 183 us: moe_forward(): pl.pallas_call(functools.partial(moe_forward_kernel, n, layer), out_shape...]
    dot_general x125 -> x0, matrix products: 511 us -> none  [the longest x5 85.9 us: local(): lax.dot_general(normed_all, grad_proj, ROW_PAIR, preferred_element_type=j...]
    all_to_all x13 -> x0, waiting for transfers between devices: 427 us -> none  [the longest x10 362 us: collect(): lax.all_to_all(buffer, ('gx', 'gy'), split_axis=0, concat_axis=0, tiled=T...]
    all_to_all x7 -> x2, blocking collectives: 371 us -> 12.2 us  [own_layer_rows(): lax.all_to_all(stacked, 'section', split_axis=0, concat_axis=0, tiled=True)]
    reduce_scatter x12 -> x2, waiting for transfers between devices: 311 us -> 0.01 us  [local_fused(): lax.psum_scatter(own_layer_sum([attn_grads[layer][k] for layer in range(n...]
    all_gather x10 -> x1, blocking collectives: 235 us -> 19.6 us  [both_layers(): return lax.all_gather(tensor, 'section', axis=0, tiled=False)]
    reduce_sum x67 -> x2, other arithmetic: 85.2 us -> 0.22 us  [the longest x1 0.18 us: seq_tables(): positions = jnp.sum(allowed.astype(jnp.int32), axis=-1) - 1]
    all_to_all x13 -> x0, starting transfers between devices: 76.9 us -> none  [the longest x10 57.8 us: collect(): lax.all_to_all(buffer, ('gx', 'gy'), split_axis=0, concat_axis=0, tiled=T...]
  transfers between devices with their start and end apart: 38 -> 20, of which waited for: 35 -> 6; matrix products, arithmetic and copies ran while one was open for 16% -> 5% of each run, Pallas kernels for 0% -> 21%
where the time goes in v1:
time: 961 us; the launch traced here: 953 us
  Pallas kernels  588 us (61%)
  waiting for transfers between devices  175 us (18%)
  blocking collectives  72.4 us (8%)
  other arithmetic  54 us (6%)
  starting transfers between devices  30.3 us (3%)
  local copies, waits for them, and re-layouts  19 us (2%)
  between operations  14.9 us (2%)
    pallas_call x2, Pallas kernels, moe_forward(): pl.pallas_call(functools.partial(moe_forward_kernel, n, layer), out_shape...  183 us
    pallas_call x2, Pallas kernels, moe_backward(): pl.pallas_call(functools.partial(moe_backward_kernel, n, layer), out_shap...  172 us
    pallas_call x2, Pallas kernels, attn_forward(): pl.pallas_call(functools.partial(attn_forward_kernel, n, layer, heads), o...  120 us
    pallas_call x2, Pallas kernels, attn_backward(): pl.pallas_call(functools.partial(attn_backward_kernel, n, layer, heads),...  113 us
    all_gather x1, waiting for transfers between devices, local_fused(): lax.all_gather(w_in_shard, 'gy', axis=0, tiled=True)  63.4 us
    all_gather x1, waiting for transfers between devices, local_fused(): lax.all_gather(w_out[0], 'gy', axis=0, tiled=True)  54.4 us
    psum x1, blocking collectives, local_fused(): lax.psum(jnp.concatenate(gain_grads, axis=0), ('section', 'gx', 'gy'))  40.5 us
    all_gather x1, waiting for transfers between devices, local_fused(): kv_all = lax.all_gather(grad_in[:, span:], 'gx', axis=0, tiled=False)  38.6 us
  transfers between devices with their start and end apart: 20, of which 6 were waited for; matrix products, arithmetic and copies ran while one was open for 5% of the time, Pallas kernels for 21%

profile of v1, /device:TPU:0, one launch (start us, length us, event | category | flops | bytes accessed | tf_op | source)
XLA Modules:
  0.0 953.2 jit_solution(4747964225405763097)
XLA Ops:
  7.3 1.1 dynamic-slice_bitcast_fusion
  8.5 2.4 pad_maximum_fusion
  11.7 63.4 %all-gather.8.cloned.1.call-done.win_own = bf16[2048,1280]{1,0:T(8,128)(2,1)} async-done(((bf16[512,1280]{1,0:T(8,128)(2,1)}), bf16[2048,1280]{1,0:T(8,128)(2,1)}) %all-gather.8.cloned.1.call-update) | async-done | bytes 5242896 | tf_op jit(solution)/shard_map/all_gather | solution.py:1632
  75.1 54.4 %all-gather.10.cloned.1.call-done = bf16[1,2048,1024]{2,1,0:T(8,128)(2,1)} async-done(((bf16[1,512,1024]{2,1,0:T(8,128)(2,1)}), bf16[1,2048,1024]{2,1,0:T(8,128)(2,1)}) %all-gather.10.cloned.1.call-update) | async-done | bytes 4194320 | tf_op jit(solution)/shard_map/all_gather | solution.py:1633
  130.9 19.6 %all-gather.3 = f32[2,1,6400]{2,1,0:T(1,128)S(1)} all-gather(f32[1,1,6400]{2,1,0:T(1,128)S(1)} %reshape.124), channel_id=2, replica_groups=mesh['section'=2,'gx'=4,'gy'=4] {'section'}, dimensions={0}, use_global_device_ids=true | all-gather | bytes 76800 | tf_op jit(solution)/shard_map/all_gather | solution.py:83
  151.6 0.8 pad_maximum_fusion.3
  154.5 1.9 constant_dynamic-slice_fusion.2
  157.0 62.7 %attn_forward.2 = (f32[64,2048]{1,0:T(8,128)}, bf16[64,2176]{1,0:T(8,128)(2,1)}, bf16[2,128,2048]{2,1,0:T(8,128)(2,1)}, f32[256,1280]{1,0:T(8,128)}, bf16[256,10...) custom-call(bf16[64,2048]{1,0:T(8,128)(2,1)} %bitcast.83, ...), custom_call_target="tpu_custom_call" | custom-call | tf_op jit(solution)/shard_map/attn_forward/pallas_call | solution.py:1021
  219.7 94.7 %moe_forward.2 = (bf16[64,2048]{1,0:T(8,128)(2,1)}, bf16[1024,2048]{1,0:T(8,128)(2,1)}, f32[1024,1]{1,0:T(8,128)}, bf16[1024,768]{1,0:T(8,128)(2,1)}, bf16[1024,...) custom-call(f32[64,2048]{1,0:T(8,128)} %get-tuple-element.65.mid_ref, bf16[64,2176]{1,0:T(8,128)(2,1)} %get-tuple-element.66.pay_ref, ...), custom_call_target="tpu_custom_call" | custom-call | tf_op jit(solution)/shard_map/moe_forward/pallas_call | solution.py:564
  314.4 57.2 %attn_forward.3 = (f32[64,2048]{1,0:T(8,128)}, bf16[64,2176]{1,0:T(8,128)(2,1)}, bf16[2,128,2048]{2,1,0:T(8,128)(2,1)}, f32[256,1280]{1,0:T(8,128)}, bf16[256,10...) custom-call(bf16[64,2048]{1,0:T(8,128)(2,1)} %get-tuple-element.67.x, ...), custom_call_target="tpu_custom_call" | custom-call | tf_op jit(solution)/shard_map/attn_forward/pallas_call | solution.py:1021
  371.6 88.7 %moe_forward.3 = (bf16[64,2048]{1,0:T(8,128)(2,1)}, bf16[1024,2048]{1,0:T(8,128)(2,1)}, f32[1024,1]{1,0:T(8,128)}, bf16[1024,768]{1,0:T(8,128)(2,1)}, bf16[1024,...) custom-call(f32[64,2048]{1,0:T(8,128)} %get-tuple-element.68.mid_ref, bf16[64,2176]{1,0:T(8,128)(2,1)} %get-tuple-element.69.pay_ref, ...), custom_call_target="tpu_custom_call" | custom-call | tf_op jit(solution)/shard_map/moe_forward/pallas_call | solution.py:564
  460.3 87.4 %moe_backward.2 = (f32[64,2048]{1,0:T(8,128)}, f32[1,2048]{1,0:T(1,128)}, bf16[2048,768]{1,0:T(8,128)(2,1)}, bf16[2048,768]{1,0:T(8,128)(2,1)}, bf16[768,2048]{1,0:T(8,128)(2,1)}) custom-call(bf16[64,2048]{1,0:T(8,128)(2,1)} %bitcast.88, f32[64,2048]{1,0:T(8,128)} %get-tuple-element.68.mid_ref, f32[1,2048]{1,0:T(1,128)} %get-tuple-element.129.gain_ffn.gain_ref, ...), custom_call_target="tpu_custom_call" | custom-call | tf_op jit(solution)/shard_map/moe_backward/pallas_call | solution.py:766
  547.8 57.2 %attn_backward.2 = (bf16[64,2048]{1,0:T(8,128)(2,1)}, f32[1,2048]{1,0:T(1,128)}, f32[1,128]{1,0:T(1,128)}, f32[1,128]{1,0:T(1,128)}, bf16[2048,1280]{1,0:T(8,128)(2,1)}, /*index=5*/bf16[2048,1024]{1,0:T(8,128)(2,1)}) custom-call(f32[64,2048]{1,0:T(8,128)} %get-tuple-element.76.dmid_ref, bf16[64,2048]{1,0:T(8,128)(2,1)} %get-tuple-element.67.x_ref, ...), custom_call_target="tpu_custom_call" | custom-call | tf_op jit(solution)/shard_map/attn_backward/pallas_call | solution.py:1231
  605.0 3.6 collective-permute-start.6
  608.6 84.3 %moe_backward.3 = (f32[64,2048]{1,0:T(8,128)}, f32[1,2048]{1,0:T(1,128)}, bf16[2048,768]{1,0:T(8,128)(2,1)}, bf16[2048,768]{1,0:T(8,128)(2,1)}, bf16[768,2048]{1,0:T(8,128)(2,1)}) custom-call(bf16[64,2048]{1,0:T(8,128)(2,1)} %get-tuple-element.84.cot_ref, f32[64,2048]{1,0:T(8,128)} %get-tuple-element.65.mid_ref, ...), custom_call_target="tpu_custom_call" | custom-call | tf_op jit(solution)/shard_map/moe_backward/pallas_call | solution.py:766
  692.9 55.5 %attn_backward.3 = (bf16[64,2048]{1,0:T(8,128)(2,1)}, f32[1,2048]{1,0:T(1,128)}, f32[1,128]{1,0:T(1,128)}, f32[1,128]{1,0:T(1,128)}, bf16[2048,1280]{1,0:T(8,128)(2,1)}, /*index=5*/bf16[2048,1024]{1,0:T(8,128)(2,1)}) custom-call(f32[64,2048]{1,0:T(8,128)} %get-tuple-element.90.dmid_ref, bf16[64,2048]{1,0:T(8,128)(2,1)} %bitcast.84, ...), custom_call_target="tpu_custom_call" | custom-call | tf_op jit(solution)/shard_map/attn_backward/pallas_call | solution.py:1231
  748.5 1.3 collective-permute-start.5
  749.8 9.6 %collective-permute-done.5 = bf16[2048,1280]{1,0:T(8,128)(2,1)} collective-permute-done((bf16[2048,1280]{1,0:T(8,128)(2,1)}, bf16[2048,1280]{1,0:T(8,128)(2,1)}, u32[]{:S(2)}, u32[]{:S(2)}) %collective-permute-start.5) | collective-permute-done | bytes 5242912 | tf_op jit(solution)/shard_map/ppermute | solution.py:1736
  759.3 12.0 %select_convert_fusion = bf16[2048,1280]{1,0:T(8,128)(2,1)} fusion(bf16[2048,1280]{1,0:T(8,128)(2,1)} %collective-permute-done.6, bf16[2048,1280]{1,0:T(8,128)(2,1)} %get-tuple-element.108, bf16[2048,1280]{1,0:T(8,128)(2,1)} %collective-permute-done.5, bf16[2048,1280]{1,0:T(8,128)(2,1)} %get-tuple-element.107, pred[]{:T(512)S(6)} %eq.45), kind=kLoop, calls=%fused_computation | loop fusion | flops 20971520 | bytes 26214400 | tf_op jit(solution)/shard_map/convert_element_type | solution.py:1747
  771.4 2.3 collective-permute-start.8
  773.8 1.3 collective-permute-start.7
  775.1 5.4 collective-permute-done.8
  780.5 2.6 collective-permute-done.7
  783.0 6.3 select_convert_fusion.1
  789.5 4.0 collective-permute-start.10
  793.5 1.3 collective-permute-start.9
  794.8 6.4 collective-permute-start.12
  801.2 1.3 collective-permute-start.11
  802.5 6.3 collective-permute-start.14
  808.9 1.3 collective-permute-start.13
  810.2 1.0 pad_maximum_fusion.1
  811.2 7.1 all_to_all.10
  818.3 1.1 pad_maximum_fusion.2
  819.4 5.1 all_to_all.11
  824.6 40.5 %psum.7 = f32[2,4352]{1,0:T(2,128)S(1)} all-reduce(f32[2,4352]{1,0:T(2,128)S(1)} %maximum_maximum_fusion), channel_id=1, replica_groups=mesh['section'=2,'gx'=4,'gy'=4] {'section','gx','gy'}, use_global_device_ids=true, to_apply=%region_2.3 | all-reduce | flops 8704 | bytes 69632 | tf_op jit(solution)/shard_map/psum | solution.py:1759
  866.4 1.8 slice.111
  868.2 8.9 select_bitcast_fusion.2
  877.2 7.1 select_bitcast_fusion.1
  884.3 7.8 select_bitcast_fusion
  892.0 2.8 bitcast_convert_fusion
  894.8 1.5 convert_element_type.119
  896.3 1.6 slice_bitcast_fusion
  897.9 38.6 %all-gather.12.cloned.1.call-done = f32[2048,256]{1,0:T(8,128)} async-done(((f32[512,256]{1,0:T(8,128)}), f32[2048,256]{1,0:T(8,128)}) %all-gather.12.cloned.1.call-update) | async-done | bytes 2097168 | tf_op jit(solution)/shard_map/all_gather | solution.py:1755
  936.5 2.3 reduce_sum.26
  938.8 1.6 fusion.4
  941.1 1.4 broadcast_in_dim_reshape.6
  943.2 1.4 broadcast_in_dim_reshape.7
  944.6 0.8 copy.53
  (109 shorter events, 9.5 us)
Async XLA Ops:
  7.2 143.6 %copy-start = (s32[4,1,128]{2,1,0:T(1,128)S(1)}, s32[4,1,128]{2,1,0:T(1,128)}, u32[]{:S(2)}) copy-start(s32[4,1,128]{2,1,0:T(1,128)} %param.18) | copy-start | bytes 6148
  7.2 122.3 %copy-start.2 = (bf16[1,1,2048,768]{3,2,1,0:T(8,128)(2,1)S(1)}, bf16[1,1,2048,768]{3,2,1,0:T(8,128)(2,1)}, u32[]{:S(2)}) copy-start(bf16[1,1,2048,768]{3,2,1,0:T(8,128)(2,1)} %param.29) | copy-start | bytes 9437188
  7.2 123.3 %copy-start.10 = (f32[1,4,1,32,8]{3,4,2,1,0:T(8,128)S(1)}, f32[1,4,1,32,8]{3,4,2,1,0:T(8,128)}, u32[]{:S(2)}) copy-start(f32[1,4,1,32,8]{3,4,2,1,0:T(8,128)} %param.20) | copy-start | bytes 12292
  7.2 123.3 %copy-start.11 = (s32[1,4,1,32,8]{3,4,2,1,0:T(8,128)S(1)}, s32[1,4,1,32,8]{3,4,2,1,0:T(8,128)}, u32[]{:S(2)}) copy-start(s32[1,4,1,32,8]{3,4,2,1,0:T(8,128)} %param.19) | copy-start | bytes 12292
  7.2 123.5 %copy-start.16 = (f32[1,2048]{1,0:T(1,128)S(1)}, f32[1,2048]{1,0:T(1,128)}, u32[]{:S(2)}) copy-start(f32[1,2048]{1,0:T(1,128)} %param.21) | copy-start | bytes 24580
  7.2 123.5 %copy-start.17 = (f32[1,2048]{1,0:T(1,128)S(1)}, f32[1,2048]{1,0:T(1,128)}, u32[]{:S(2)}) copy-start(f32[1,2048]{1,0:T(1,128)} %param.22) | copy-start | bytes 24580
  7.3 123.6 %copy-start.22 = (f32[1,128]{1,0:T(1,128)S(1)}, f32[1,128]{1,0:T(1,128)}, u32[]{:S(2)}) copy-start(f32[1,128]{1,0:T(1,128)} %param.23) | copy-start | bytes 1540
  7.3 123.6 %copy-start.23 = (f32[1,128]{1,0:T(1,128)S(1)}, f32[1,128]{1,0:T(1,128)}, u32[]{:S(2)}) copy-start(f32[1,128]{1,0:T(1,128)} %param.24) | copy-start | bytes 1540
  7.3 67.8 %all-gather.8.cloned.1.call-start = ((), (), s32[]{:S(2)}) async-start(), calls=%async_computation.4 | async-start | bytes 6553600 | tf_op jit(solution)/shard_map/all_gather | solution.py:1632
  10.9 118.6 %all-gather.10.cloned.1.call-start = ((), (), s32[]{:S(2)}) async-start(), calls=%async_computation.7 | async-start | bytes 5242880 | tf_op jit(solution)/shard_map/all_gather | solution.py:1633
  11.6 854.7 %reduce-scatter.3.cloned.1.call-start = ((), (), s32[]{:S(2)}) async-start(), calls=%async_computation.5 | async-start | bytes 6553600 | tf_op jit(solution)/shard_map/reduce_scatter | solution.py:1746
  75.1 81.9 %collective-permute-start = (bf16[2048,1280]{1,0:T(8,128)(2,1)}, bf16[2048,1280]{1,0:T(8,128)(2,1)}, u32[]{:S(2)}, u32[]{:S(2)}) collective-permute-start(bf16[2048,1280]{1,0:T(8,128)(2,1)} %all-gather.8.cloned.1.call-done.win_own), channel_id=1, source_target_pairs={{0,16},{16,0},{1,17},{17,1},{2,18},{18,2},{3,19},{19,3},{4,20},{20... | collective-permute-start | bytes 15728648 | tf_op jit(solution)/shard_map/ppermute | solution.py:92
  129.5 27.5 %collective-permute-start.1 = (bf16[2048,1024]{1,0:T(8,128)(2,1)}, bf16[2048,1024]{1,0:T(8,128)(2,1)}, u32[]{:S(2)}, u32[]{:S(2)}) collective-permute-start(bf16[2048,1024]{1,0:T(8,128)(2,1)} %bitcast.60), channel_id=1, source_target_pairs={{0,16},{16,0},{1,17},{17,1},{2,18},{18,2},{3,19},{19,3},{4,20},{20... | collective-permute-start | bytes 12582920 | tf_op jit(solution)/shard_map/ppermute | solution.py:92
  129.5 90.1 %collective-permute-start.2 = (bf16[2048,768]{1,0:T(8,128)(2,1)S(1)}, bf16[2048,768]{1,0:T(8,128)(2,1)}, u32[]{:S(2)}, u32[]{:S(2)}) collective-permute-start(bf16[2048,768]{1,0:T(8,128)(2,1)S(1)} %bitcast.69), channel_id=1, source_target_pairs={{0,16},{16,0},{1,17},{17,1},{2,18},{18,2},{3,19},{19,3},{4,20},{20... | collective-permute-start | bytes 9437192 | tf_op jit(solution)/shard_map/ppermute | solution.py:92
  130.0 89.6 %collective-permute-start.3 = (bf16[2048,768]{1,0:T(8,128)(2,1)}, bf16[2048,768]{1,0:T(8,128)(2,1)}, u32[]{:S(2)}, u32[]{:S(2)}) collective-permute-start(bf16[2048,768]{1,0:T(8,128)(2,1)} %bitcast.70), channel_id=1, source_target_pairs={{0,16},{16,0},{1,17},{17,1},{2,18},{18,2},{3,19},{19,3},{4,20},{20... | collective-permute-start | bytes 9437192 | tf_op jit(solution)/shard_map/ppermute | solution.py:92
  130.0 89.7 %collective-permute-start.4 = (bf16[768,2048]{1,0:T(8,128)(2,1)}, bf16[768,2048]{1,0:T(8,128)(2,1)}, u32[]{:S(2)}, u32[]{:S(2)}) collective-permute-start(bf16[768,2048]{1,0:T(8,128)(2,1)} %bitcast.75), channel_id=1, source_target_pairs={{0,16},{16,0},{1,17},{17,1},{2,18},{18,2},{3,19},{19,3},{4,20},{20... | collective-permute-start | bytes 9437192 | tf_op jit(solution)/shard_map/ppermute | solution.py:92
  605.0 144.8 %collective-permute-start.6 = (bf16[2048,1280]{1,0:T(8,128)(2,1)}, bf16[2048,1280]{1,0:T(8,128)(2,1)}, u32[]{:S(2)}, u32[]{:S(2)}) collective-permute-start(bf16[2048,1280]{1,0:T(8,128)(2,1)} %get-tuple-element.108), channel_id=1, source_target_pairs={{0,16},{1,17},{2,18},{3,19},{4,20},{5,21},{6,22},{7,23},{8,24},{9,... | collective-permute-start | bytes 15728648 | tf_op jit(solution)/shard_map/ppermute | solution.py:1736
  748.5 10.9 %collective-permute-start.5 = (bf16[2048,1280]{1,0:T(8,128)(2,1)}, bf16[2048,1280]{1,0:T(8,128)(2,1)}, u32[]{:S(2)}, u32[]{:S(2)}) collective-permute-start(bf16[2048,1280]{1,0:T(8,128)(2,1)} %get-tuple-element.107), channel_id=1, source_target_pairs={{16,0},{17,1},{18,2},{19,3},{20,4},{21,5},{22,6},{23,7},{24,8},{25... | collective-permute-start | bytes 15728648 | tf_op jit(solution)/shard_map/ppermute | solution.py:1736
  771.4 120.6 %reduce-scatter.5.cloned.1.call-start = ((), (), s32[]{:S(2)}) async-start(), calls=%async_computation.6 | async-start | bytes 5242880 | tf_op jit(solution)/shard_map/reduce_scatter | solution.py:1746
  771.4 9.0 collective-permute-start.8
  773.8 9.3 collective-permute-start.7
  789.3 13.2 %copy-start.3 = (bf16[768,2048]{1,0:T(8,128)(2,1)S(1)}, bf16[768,2048]{1,0:T(8,128)(2,1)}, u32[]{:S(2)}) copy-start(bf16[768,2048]{1,0:T(8,128)(2,1)} %get-tuple-element.116) | copy-start | bytes 9437188
  789.3 20.8 %copy-start.7 = (bf16[64,2048]{1,0:T(8,128)(2,1)S(1)}, bf16[64,2048]{1,0:T(8,128)(2,1)}, u32[]{:S(2)}) copy-start(bf16[64,2048]{1,0:T(8,128)(2,1)} %get-tuple-element.67.x_ref) | copy-start | bytes 786436
  789.3 35.1 %copy-start.12 = (f32[1,2048]{1,0:T(1,128)S(1)}, f32[1,2048]{1,0:T(1,128)}, u32[]{:S(2)}) copy-start(f32[1,2048]{1,0:T(1,128)} %get-tuple-element.104) | copy-start | bytes 24580
  789.4 35.1 %copy-start.13 = (f32[1,2048]{1,0:T(1,128)S(1)}, f32[1,2048]{1,0:T(1,128)}, u32[]{:S(2)}) copy-start(f32[1,2048]{1,0:T(1,128)} %get-tuple-element.103) | copy-start | bytes 24580
  789.4 35.1 %copy-start.14 = (f32[1,2048]{1,0:T(1,128)S(1)}, f32[1,2048]{1,0:T(1,128)}, u32[]{:S(2)}) copy-start(f32[1,2048]{1,0:T(1,128)} %get-tuple-element.100) | copy-start | bytes 24580
  789.4 35.1 %copy-start.15 = (f32[1,2048]{1,0:T(1,128)S(1)}, f32[1,2048]{1,0:T(1,128)}, u32[]{:S(2)}) copy-start(f32[1,2048]{1,0:T(1,128)} %get-tuple-element.99) | copy-start | bytes 24580
  789.4 35.1 %copy-start.18 = (f32[1,128]{1,0:T(1,128)S(1)}, f32[1,128]{1,0:T(1,128)}, u32[]{:S(2)}) copy-start(f32[1,128]{1,0:T(1,128)} %get-tuple-element.105) | copy-start | bytes 1540
  789.4 35.1 %copy-start.19 = (f32[1,128]{1,0:T(1,128)S(1)}, f32[1,128]{1,0:T(1,128)}, u32[]{:S(2)}) copy-start(f32[1,128]{1,0:T(1,128)} %get-tuple-element.106) | copy-start | bytes 1540
  789.4 35.1 %copy-start.20 = (f32[1,128]{1,0:T(1,128)S(1)}, f32[1,128]{1,0:T(1,128)}, u32[]{:S(2)}) copy-start(f32[1,128]{1,0:T(1,128)} %get-tuple-element.101) | copy-start | bytes 1540
  789.4 35.1 %copy-start.21 = (f32[1,128]{1,0:T(1,128)S(1)}, f32[1,128]{1,0:T(1,128)}, u32[]{:S(2)}) copy-start(f32[1,128]{1,0:T(1,128)} %get-tuple-element.102) | copy-start | bytes 1540
  789.4 147.0 %all-gather.12.cloned.1.call-start = ((), (), s32[]{:S(2)}) async-start(), calls=%async_computation.8 | async-start | bytes 2621440 | tf_op jit(solution)/shard_map/all_gather | solution.py:1755
  789.5 19.4 %collective-permute-start.10 = (bf16[2048,768]{1,0:T(8,128)(2,1)}, bf16[2048,768]{1,0:T(8,128)(2,1)}, u32[]{:S(2)}, u32[]{:S(2)}) collective-permute-start(bf16[2048,768]{1,0:T(8,128)(2,1)} %get-tuple-element.112), channel_id=1, source_target_pairs={{0,16},{1,17},{2,18},{3,19},{4,20},{5,21},{6,22},{7,23},{8,24},{9,... | collective-permute-start | bytes 9437192 | tf_op jit(solution)/shard_map/ppermute | solution.py:1736
  793.5 74.7 %collective-permute-start.9 = (bf16[2048,768]{1,0:T(8,128)(2,1)}, bf16[2048,768]{1,0:T(8,128)(2,1)}, u32[]{:S(2)}, u32[]{:S(2)}) collective-permute-start(bf16[2048,768]{1,0:T(8,128)(2,1)} %get-tuple-element.111), channel_id=1, source_target_pairs={{16,0},{17,1},{18,2},{19,3},{20,4},{21,5},{22,6},{23,7},{24,8},{25... | collective-permute-start | bytes 9437192 | tf_op jit(solution)/shard_map/ppermute | solution.py:1736
  794.8 82.3 %collective-permute-start.12 = (bf16[2048,768]{1,0:T(8,128)(2,1)}, bf16[2048,768]{1,0:T(8,128)(2,1)}, u32[]{:S(2)}, u32[]{:S(2)}) collective-permute-start(bf16[2048,768]{1,0:T(8,128)(2,1)} %get-tuple-element.114), channel_id=1, source_target_pairs={{0,16},{1,17},{2,18},{3,19},{4,20},{5,21},{6,22},{7,23},{8,24},{9,... | collective-permute-start | bytes 9437192 | tf_op jit(solution)/shard_map/ppermute | solution.py:1736
  801.2 75.9 %collective-permute-start.11 = (bf16[2048,768]{1,0:T(8,128)(2,1)}, bf16[2048,768]{1,0:T(8,128)(2,1)}, u32[]{:S(2)}, u32[]{:S(2)}) collective-permute-start(bf16[2048,768]{1,0:T(8,128)(2,1)} %get-tuple-element.113), channel_id=1, source_target_pairs={{16,0},{17,1},{18,2},{19,3},{20,4},{21,5},{22,6},{23,7},{24,8},{25... | collective-permute-start | bytes 9437192 | tf_op jit(solution)/shard_map/ppermute | solution.py:1736
  802.5 81.8 %collective-permute-start.14 = (bf16[768,2048]{1,0:T(8,128)(2,1)S(1)}, bf16[768,2048]{1,0:T(8,128)(2,1)}, u32[]{:S(2)}, u32[]{:S(2)}) collective-permute-start(bf16[768,2048]{1,0:T(8,128)(2,1)S(1)} %copy-done.3), channel_id=1, source_target_pairs={{0,16},{1,17},{2,18},{3,19},{4,20},{5,21},{6,22},{7,23},{8,24},{9,... | collective-permute-start | bytes 9437192 | tf_op jit(solution)/shard_map/ppermute | solution.py:1736
  808.9 75.4 %collective-permute-start.13 = (bf16[768,2048]{1,0:T(8,128)(2,1)}, bf16[768,2048]{1,0:T(8,128)(2,1)}, u32[]{:S(2)}, u32[]{:S(2)}) collective-permute-start(bf16[768,2048]{1,0:T(8,128)(2,1)} %get-tuple-element.115), channel_id=1, source_target_pairs={{16,0},{17,1},{18,2},{19,3},{20,4},{21,5},{22,6},{23,7},{24,8},{25... | collective-permute-start | bytes 9437192 | tf_op jit(solution)/shard_map/ppermute | solution.py:1736
  868.2 9.0 copy-start.4
  868.2 9.0 copy-start.6
  877.1 7.1 copy-start.5
  940.4 4.2 copy-start.8
  940.4 5.8 copy-start.1
  941.1 4.3 copy-start.9
Sparse Core Ops, SparseCore 0:
  11.0 64.0 all-gather.7
  76.9 52.5 all-gather.9
  771.5 60.7 reduce-scatter.2
  835.1 53.6 reduce-scatter.4
  890.8 45.6 all-gather.11

commit v2 on v1

--- a/solution.py
+++ b/solution.py
@@ -103,7 +103,7 @@
     )
 
 
-def hello(n, me, gy, with_plane):
+def hello(n, me, gy, with_plane, with_section=False):
     barrier = pltpu.get_barrier_semaphore()
     mesh_ids = pl.DeviceIdType.MESH
 
@@ -115,12 +115,17 @@
     def _():
         pl.semaphore_signal(barrier, 1, device_id={"gx": me - 1}, device_id_type=mesh_ids)
 
+    peers = 0
     if with_plane:
         for bit in (1, 2):
             pl.semaphore_signal(
                 barrier, 1, device_id={"gy": gy_flip(gy, bit)}, device_id_type=mesh_ids
             )
-    peers = 2 if with_plane else 0
+        peers += 2
+    if with_section:
+        other = 1 - lax.axis_index("section")
+        pl.semaphore_signal(barrier, 1, device_id={"section": other}, device_id_type=mesh_ids)
+        peers += 1
     at_end = (me == 0) | (me == n - 1)
 
     @pl.when(at_end)
@@ -607,11 +612,12 @@
     wg_other,
     wu_other,
     wd_other,
-    dmid_ref,
-    dgain_ref,
-    grad_gate_ref,
-    grad_up_ref,
-    grad_down_ref,
+    *rest,
+):
+    rest = rest[0 if layer else 6 :]
+    dmid_ref, dgain_ref = rest[:2]
+    keep_refs, give_refs = rest[2:5], rest[5:8]
+    (
     cots,
     wg,
     wu,
@@ -637,7 +643,8 @@
     isem,
     osem,
     *sems,
-):
+    ) = rest[8:]
+    section = lax.axis_index("section")
     r, d = mid_ref.shape
     ff = wg.shape[1]
     rows = n * r
@@ -713,13 +720,11 @@
     lax.fori_loop(0, 4, column, 0)
     plane.scatter_far()
 
-    def chunk_saves(i):
+    def saving(i, refs):
         at = pl.ds(pl.multiple_of(i * 256, 256), 256)
-        return (
-            pltpu.make_async_copy(out_gate.at[at], grad_gate_ref.at[at], osem.at[0, i]),
-            pltpu.make_async_copy(out_up.at[at], grad_up_ref.at[at], osem.at[1, i]),
-            pltpu.make_async_copy(out_down.at[:, at], grad_down_ref.at[:, at], osem.at[2, i]),
-        )
+        for k, (src, ref) in enumerate(zip((out_gate, out_up, out_down), refs)):
+            where = (slice(None), at) if k == 2 else (at, slice(None))
+            yield pltpu.make_async_copy(src.at[where], ref.at[where], osem.at[k, i])
 
     def weight_grads(first, last):
         def chunk(i, carry):
@@ -728,8 +733,17 @@
             out_gate[at] = dot32(left, gp[...], ROW_PAIR).astype(BF16)
             out_up[at] = dot32(left, up[...], ROW_PAIR).astype(BF16)
             out_down[:, at] = dot32(inner[...], de[:, at], ROW_PAIR).astype(BF16)
-            for save in chunk_saves(i):
-                save.start()
+
+            @pl.when(section == layer)
+            def _():
+                for copy in saving(i, keep_refs):
+                    copy.start()
+
+            @pl.when(section != layer)
+            def _():
+                for copy in saving(i, give_refs):
+                    copy.start()
+
             return carry
 
         lax.fori_loop(first, last, chunk, 0)
@@ -754,26 +768,30 @@
     dgain_ref[...] = jnp.sum(db * unit, axis=0, keepdims=True)
     dmid_ref[...] = cot_ref[...].astype(F32) + norm_back(db * gain_ref[...], unit, scale)
     plane.gather_drain(slot)
-    for i in range(chunks):
-        for save in chunk_saves(i):
-            save.wait()
-
-
-def moe_backward(layer, n, cot, mid, gain, weight, arrived, gp, up, inner, own, other, cid):
+
+    def settle(i, carry):
+        for copy in saving(i, keep_refs):
+            copy.wait()
+        return carry
+
+    lax.fori_loop(0, chunks, settle, 0)
+
+
+def moe_backward(layer, n, cot, mid, gain, weight, arrived, gp, up, inner, own, other, so_far, cid):
     r, d = mid.shape
     ff = own[0].shape[1]
     total_rows = 4 * n * r
+    sums = [jax.ShapeDtypeStruct(shape, BF16) for shape in ((d, ff), (d, ff), (ff, d))] * 2
     return pl.pallas_call(
         functools.partial(moe_backward_kernel, n, layer),
         out_shape=(
             jax.ShapeDtypeStruct((r, d), F32),
             jax.ShapeDtypeStruct((1, d), F32),
-            jax.ShapeDtypeStruct((d, ff), BF16),
-            jax.ShapeDtypeStruct((d, ff), BF16),
-            jax.ShapeDtypeStruct((ff, d), BF16),
+            *sums,
         ),
-        in_specs=in_vmem(4) + in_place(10),
-        out_specs=tuple(in_vmem(2) + in_place(3)),
+        in_specs=in_vmem(4) + in_place(10 + len(so_far)),
+        out_specs=tuple(in_vmem(2) + in_place(6)),
+        input_output_aliases={14 + k: 2 + k for k in range(len(so_far))},
         scratch_shapes=[
             pltpu.VMEM((total_rows, d), BF16),
             pltpu.VMEM((d, ff), BF16),
@@ -789,14 +807,314 @@
         + [
             pltpu.SemaphoreType.DMA((3,)),
             pltpu.SemaphoreType.DMA((4,)),
-            pltpu.SemaphoreType.DMA((3, d // 256)),
         ]
+        + [pltpu.SemaphoreType.DMA((3, d // 256))]
         + [pltpu.SemaphoreType.DMA((n,))] * 20,
         compiler_params=pltpu.CompilerParams(
             collective_id=cid, has_side_effects=True, vmem_limit_bytes=63 << 20
         ),
         name="moe_backward",
-    )(cot, mid, gain, weight, arrived, gp, up, inner, *own, *other)
+    )(cot, mid, gain, weight, arrived, gp, up, inner, *own, *other, *so_far)
+
+
+class Share:
+    def __init__(self, layer, shard, full, scratch):
+        self.shard, self.full = shard, full
+        self.held, self.plane_sems, self.to_sems, self.from_sems = scratch
+        self.section = lax.axis_index("section")
+        self.mine = self.section == layer
+        gy = lax.axis_index("gy")
+        self.cols = [gy_flip(gy, bits) if bits else gy for bits in range(4)]
+        self.rows = shard.shape[0]
+
+    def at(self, column, half=None):
+        rows = self.rows
+        if half is None:
+            return self.full.at[pl.ds(pl.multiple_of(column * rows, rows), rows)]
+        few = rows // 2
+        return self.full.at[pl.ds(pl.multiple_of(column * rows + half * few, few), few)]
+
+    def own(self, step):
+        src, dst = ((self.shard, self.held), (self.held, self.at(self.cols[0])))[step]
+        return pltpu.make_async_copy(src, dst, self.plane_sems.at[9 * step])
+
+    def direct(self, bit):
+        s = self.plane_sems
+        k = 1 if bit == 1 else 3
+        return remote(
+            self.shard, self.at(self.cols[0]), s.at[k], s.at[k + 1], gy=self.cols[bit]
+        )
+
+    def onward(self, bit):
+        s = self.plane_sems
+        k = 5 if bit == 1 else 7
+        half = 1 if bit == 1 else 0
+        ref = self.at(self.cols[3 - bit], half)
+        return remote(ref, ref, s.at[k], s.at[k + 1], gy=self.cols[bit])
+
+    def hand(self, k):
+        if k == 0:
+            src, dst = self.shard, self.at(self.cols[0])
+        elif k < 3:
+            src = dst = self.at(self.cols[k])
+        else:
+            src = dst = self.at(self.cols[3], k - 3)
+        return remote(src, dst, self.to_sems.at[k], self.from_sems.at[k], section=1 - self.section)
+
+    def start(self):
+        @pl.when(self.mine)
+        def _():
+            self.direct(1).start()
+            self.direct(2).start()
+            self.own(0).start()
+            self.hand(0).start()
+
+    def pass_on(self):
+        @pl.when(self.mine)
+        def _():
+            self.own(0).wait()
+            self.own(1).start()
+            self.direct(1).wait_recv()
+            self.onward(2).start()
+            self.hand(1).start()
+            self.direct(2).wait_recv()
+            self.onward(1).start()
+            self.hand(2).start()
+
+    def finish(self):
+        @pl.when(self.mine)
+        def _():
+            self.onward(2).wait_recv()
+            self.hand(3).start()
+            self.onward(1).wait_recv()
+            self.hand(4).start()
+            self.own(1).wait()
+
+        @pl.when(jnp.logical_not(self.mine))
+        def _():
+            for k in range(5):
+                self.hand(k).wait_recv()
+
+    def drain(self):
+        @pl.when(self.mine)
+        def _():
+            for bit in (1, 2):
+                self.direct(bit).wait_send()
+                self.onward(bit).wait_send()
+            for k in range(5):
+                self.hand(k).wait_send()
+
+
+def share_scratch(shard):
+    dma = pltpu.SemaphoreType.DMA
+    return [pltpu.VMEM(shard.shape, BF16), dma((10,)), dma((5,)), dma((5,))]
+
+
+def share_kernel(n, layer, count, *refs):
+    shards, fulls, scratch = refs[:count], refs[count : 2 * count], refs[2 * count :]
+    shares = [
+        Share(layer, shards[k], fulls[k], scratch[4 * k : 4 * k + 4]) for k in range(count)
+    ]
+    hello(n, lax.axis_index("gx"), lax.axis_index("gy"), True, True)
+    for share in shares:
+        share.start()
+    for share in shares:
+        share.pass_on()
+    for share in shares:
+        share.finish()
+    for share in shares:
+        share.drain()
+
+
+def share_weights(layer, n, shards, cid):
+    return pl.pallas_call(
+        functools.partial(share_kernel, n, layer, len(shards)),
+        out_shape=tuple(jax.ShapeDtypeStruct((4 * w.shape[0], w.shape[1]), BF16) for w in shards),
+        in_specs=in_place(len(shards)),
+        out_specs=tuple(in_place(len(shards))),
+        scratch_shapes=[item for shard in shards for item in share_scratch(shard)],
+        compiler_params=pltpu.CompilerParams(collective_id=cid, has_side_effects=True),
+        name="share_weights",
+    )(*shards)
+
+
+def finish_kernel(
+    n,
+    gains_ref,
+    kv_ref,
+    lo_ref,
+    ig_ref,
+    gain_ref,
+    kv_all_ref,
+    lo_all_ref,
+    ig_all_ref,
+    gbuf,
+    stage,
+    incoming,
+    lsem,
+    psem,
+    qsem,
+    rsem,
+    *sems,
+):
+    me = lax.axis_index("gx")
+    gy = lax.axis_index("gy")
+    section = lax.axis_index("section")
+    other = 1 - section
+    gbuf[me] = gains_ref[...]
+    kv_all_ref[me] = kv_ref[...]
+    hello(n, me, gy, True, True)
+    z_gather_steps(n, me, lambda z: gbuf.at[z], sems[:4], lambda z, k: None)
+    z_gather_steps(n, me, lambda z: kv_all_ref.at[z], sems[4:8], lambda z, k: None)
+    keeps = []
+    for k, (src, dst) in enumerate(((lo_ref, lo_all_ref), (ig_ref, ig_all_ref))):
+        keep = pltpu.make_async_copy(src.at[section], dst.at[section], lsem.at[k])
+        give = remote(src.at[other], dst.at[section], psem.at[k], qsem.at[k], section=other)
+        keep.start()
+        give.start()
+        keeps.append((keep, give))
+    total = gbuf[0]
+    for z in range(1, n):
+        total = total + gbuf[z]
+    for k, where in enumerate(({"gy": gy_flip(gy, 1)}, {"gy": gy_flip(gy, 2)}, {"section": other})):
+        stage[k] = total
+        swap = remote(stage.at[k], incoming.at[k], rsem.at[0, k], rsem.at[1, k], **where)
+        swap.start()
+        swap.wait()
+        total = total + incoming[k]
+
+    @pl.when(section == 0)
+    def _():
+        gain_ref[...] = total[0:1]
+
+    @pl.when(section == 1)
+    def _():
+        gain_ref[...] = total[1:2]
+
+    for keep, give in keeps:
+        keep.wait()
+        give.wait()
+    z_gather_drain(n, me, lambda z: gbuf.at[z], sems[:4])
+    z_gather_drain(n, me, lambda z: kv_all_ref.at[z], sems[4:8])
+
+
+def finish(n, gains, kv, lo, ig, cid):
+    dma = pltpu.SemaphoreType.DMA
+    shape = jax.ShapeDtypeStruct
+    return pl.pallas_call(
+        functools.partial(finish_kernel, n),
+        out_shape=(
+            shape((1, gains.shape[1]), F32),
+            shape((n,) + kv.shape, BF16),
+            shape(lo.shape, BF16),
+            shape(ig.shape, BF16),
+        ),
+        in_specs=in_vmem(4),
+        out_specs=tuple(in_vmem(4)),
+        scratch_shapes=[
+            pltpu.VMEM((n,) + gains.shape, F32),
+            pltpu.VMEM((3,) + gains.shape, F32),
+            pltpu.VMEM((3,) + gains.shape, F32),
+            dma((2,)),
+            dma((2,)),
+            dma((2,)),
+            dma((2, 3)),
+        ]
+        + [dma((n,))] * 8,
+        compiler_params=pltpu.CompilerParams(collective_id=cid, has_side_effects=True),
+        name="finish",
+    )(gains, kv, lo, ig)
+
+
+class Reduce:
+    def __init__(self, layer, part, inbox, xin, yin, din, sems):
+        self.part, self.inbox = part, inbox
+        self.xin, self.yin, self.din = xin, yin, din
+        self.give_sems, self.take_sems, self.send_sems, self.recv_sems = sems
+        self.section = lax.axis_index("section")
+        self.mine = self.section == layer
+        gy = lax.axis_index("gy")
+        self.cols = [gy_flip(gy, bits) if bits else gy for bits in range(4)]
+        self.few = xin.shape[0] // 2
+
+    def give(self, k, src):
+        return remote(
+            src,
+            self.inbox.at[self.cols[k]],
+            self.give_sems.at[k],
+            self.take_sems.at[k],
+            section=1 - self.section,
+        )
+
+    def half(self, ref, h):
+        return ref.at[pl.ds(h * self.few, self.few)]
+
+    def far(self, bit):
+        k = bit - 1
+        src = self.half(self.part(self.cols[3]), k)
+        return remote(
+            src, self.din.at[k], self.send_sems.at[k], self.recv_sems.at[k], gy=self.cols[bit]
+        )
+
+    def near(self, bit, h):
+        k = 2 * bit + h
+        into = self.xin if bit == 1 else self.yin
+        return remote(
+            self.half(self.part(self.cols[bit]), h),
+            self.half(into, h),
+            self.send_sems.at[k],
+            self.recv_sems.at[k],
+            gy=self.cols[bit],
+        )
+
+    def send_terms(self):
+        def add(k):
+            self.give(k, self.part(self.cols[k])).wait_recv()
+            ref = self.part(self.cols[k])
+            add_rows(ref, ref, self.inbox.at[self.cols[k]])
+
+        @pl.when(self.mine)
+        def _():
+            add(3)
+            self.far(1).start()
+            self.far(2).start()
+            add(1)
+            self.near(1, 0).start()
+            add(2)
+            self.near(2, 1).start()
+            add(0)
+
+    def pass_on(self):
+        @pl.when(self.mine)
+        def _():
+            self.far(1).wait_recv()
+            ref = self.half(self.part(self.cols[2]), 0)
+            add_rows(ref, ref, self.din.at[0])
+            self.near(2, 0).start()
+            self.far(2).wait_recv()
+            ref = self.half(self.part(self.cols[1]), 1)
+            add_rows(ref, ref, self.din.at[1])
+            self.near(1, 1).start()
+
+    def close(self, outs):
+        @pl.when(self.mine)
+        def _():
+            for bit in (1, 2):
+                for h in (0, 1):
+                    self.near(bit, h).wait_recv()
+            for ref, first, last in outs:
+                cols = slice(first, last)
+                own = self.part(self.cols[0])
+                add_rows(ref, own.at[:, cols], self.xin.at[:, cols], self.yin.at[:, cols])
+            for bit in (1, 2):
+                self.far(bit).wait_send()
+                for h in (0, 1):
+                    self.near(bit, h).wait_send()
+
+
+def reduce_sems():
+    dma = pltpu.SemaphoreType.DMA
+    return [dma((4,)), dma((4,)), dma((6,)), dma((6,))]
 
 
 class Line:
@@ -892,19 +1210,15 @@
     sin_ref,
     mask_ref,
     gates_ref,
-    win_own,
-    wout_own,
-    win_other,
-    wout_other,
-    mid_ref,
-    pay_ref,
-    normed_hbm,
-    proj_hbm,
-    qr_hbm,
-    kr_ref,
-    v_ref,
-    prob_hbm,
-    mixed_hbm,
+    win_hbm,
+    wout_hbm,
+    *rest,
+):
+    count = 2 if layer == 0 else 0
+    shards, rest = rest[:count], rest[count:]
+    mid_ref, pay_ref, normed_hbm, proj_hbm, qr_hbm, kr_ref, v_ref, prob_hbm, mixed_hbm = rest[:9]
+    fulls, rest = rest[9 : 9 + count], rest[9 + count :]
+    (
     win,
     wout,
     normed,
@@ -921,15 +1235,22 @@
     wsem,
     osem,
     *sems,
-):
+    ) = rest
     mb, length, d = normed.shape
     t = length // n
     r = mb * t
     span = heads * HD
     me = lax.axis_index("gx")
-    own, other, held = (win_own, wout_own), (win_other, wout_other), (win, wout)
-    fetch_layer(layer, own, other, held, wsem)
-    hello(n, me, None, False)
+    shares = [
+        Share(1, shards[k], fulls[k], sems[8 + 4 * k : 12 + 4 * k]) for k in range(count)
+    ]
+    fetch_in = pltpu.make_async_copy(win_hbm, win, wsem.at[0])
+    fetch_out = pltpu.make_async_copy(wout_hbm, wout, wsem.at[1])
+    fetch_in.start()
+    fetch_out.start()
+    hello(n, me, lax.axis_index("gy"), count > 0, count > 0)
+    for share in shares:
+        share.start()
     hidden = x_ref[...].astype(F32)
     unit, _ = unit_of(hidden)
     low = (unit * gain_attn[...]).astype(BF16)
@@ -947,7 +1268,7 @@
         pltpu.make_async_copy(mixed, mixed_hbm, osem.at[4]),
     ]
     saves[0].start()
-    fetch_wait(own, held, wsem, (0,))
+    fetch_in.wait()
     every = normed[...].reshape(mb * length, d)
     for j in range((span + 2 * HD) // 256):
         cols = slice(j * 256, (j + 1) * 256)
@@ -978,7 +1299,9 @@
     saves[2].start()
     saves[3].start()
     saves[4].start()
-    fetch_wait(own, held, wsem, (1,))
+    for share in shares:
+        share.pass_on()
+    fetch_out.wait()
     both = mixed[...]
 
     def out_cols(j, carry):
@@ -990,7 +1313,7 @@
         return carry
 
     lax.fori_loop(0, d // 256, out_cols, 0)
-    line = Line(n, sems[4:], zup, zdn, stage, acc)
+    line = Line(n, sems[4:8], zup, zdn, stage, acc)
     for z in line.z_list:
         add_rows(acc, col.at[z])
         line.move(z, total)
@@ -1000,6 +1323,10 @@
     unit, _ = unit_of(mid)
     pay_ref[:, :d] = (unit * gain_ffn[...]).astype(BF16)
     pay_ref[:, d:] = gates_ref[...]
+    for share in shares:
+        share.finish()
+    for share in shares:
+        share.drain()
     z_gather_drain(n, me, slot, sems[:4])
     for save in saves:
         save.wait()
@@ -1009,13 +1336,13 @@
     return [pltpu.VMEM((n, r, d), BF16)] * 4 + [pltpu.VMEM((r, d), F32)] * 2
 
 
-def attn_forward(layer, n, x, gains, tables, gate_cols, own, other, cid, mb):
+def attn_forward(layer, n, x, gains, tables, gate_cols, w_in, w_out, shards, cid, mb):
     r, d = x.shape
     cosine, sine, mask = tables
     total_rows = cosine.shape[0]
     length = total_rows // mb
-    width = own[0].shape[1]
-    heads = own[1].shape[1] // HD
+    width = w_in.shape[1]
+    heads = w_out.shape[1] // HD
     span = heads * HD
     shape = jax.ShapeDtypeStruct
     return pl.pallas_call(
@@ -1030,9 +1357,10 @@
             shape((total_rows, HD), BF16),
             shape((mb * heads, length, length), BF16),
             shape((total_rows, span), BF16),
+            *(shape((4 * w.shape[0], w.shape[1]), BF16) for w in shards),
         ),
-        in_specs=in_vmem(9) + in_place(4),
-        out_specs=tuple(in_vmem(2) + in_place(3) + in_vmem(2) + in_place(2)),
+        in_specs=in_vmem(9) + in_place(2 + len(shards)),
+        out_specs=tuple(in_vmem(2) + in_place(3) + in_vmem(2) + in_place(2 + len(shards))),
         scratch_shapes=[
             pltpu.VMEM((d, width), BF16),
             pltpu.VMEM((d, span), BF16),
@@ -1044,12 +1372,13 @@
         ]
         + line_buffers(n, r, d)
         + [pltpu.SemaphoreType.DMA((2,)), pltpu.SemaphoreType.DMA((5,))]
-        + [pltpu.SemaphoreType.DMA((n,))] * 8,
+        + [pltpu.SemaphoreType.DMA((n,))] * 8
+        + [item for shard in shards for item in share_scratch(shard)],
         compiler_params=pltpu.CompilerParams(
             collective_id=cid, has_side_effects=True, vmem_limit_bytes=60 << 20
         ),
         name="attn_forward",
-    )(x, *gains, cosine, sine, mask, gate_cols, *own, *other)
+    )(x, *gains, cosine, sine, mask, gate_cols, w_in, w_out, *shards)
 
 
 def attn_backward_kernel(
@@ -1070,16 +1399,16 @@
     qr_hbm,
     prob_hbm,
     mixed_hbm,
-    win_own,
-    wout_own,
-    win_other,
-    wout_other,
-    cot_ref,
-    dgain_attn,
-    dgain_query,
-    dgain_key,
-    grad_in_hbm,
-    grad_out_hbm,
+    win_hbm,
+    wout_hbm,
+    *rest,
+):
+    last = layer == 0
+    if last:
+        later_hbm, gives, rest = rest[0], rest[1:4], rest[4:]
+    cot_ref, dgain_attn, dgain_query, dgain_key = rest[:4]
+    outs, rest = rest[4 : 10 if last else 5], rest[10 if last else 5 :]
+    (
     win,
     wout,
     normed,
@@ -1092,8 +1421,7 @@
     dproj,
     dkey,
     dvalue,
-    grad_in,
-    grad_out,
+    grads,
     col,
     zup,
     zdn,
@@ -1104,14 +1432,18 @@
     isem,
     osem,
     *sems,
-):
+    ) = rest
     mb, length, d = normed.shape
     t = length // n
     span = heads * HD
     me = lax.axis_index("gx")
     inv_root = 1.0 / math.sqrt(HD)
-    own, other, held = (wout_own, win_own), (wout_other, win_other), (wout, win)
-    fetch_layer(layer, own, other, held, wsem)
+    gy = lax.axis_index("gy")
+    section = lax.axis_index("section")
+    fetch_out = pltpu.make_async_copy(wout_hbm, wout, wsem.at[0])
+    fetch_in = pltpu.make_async_copy(win_hbm, win, wsem.at[1])
+    fetch_out.start()
+    fetch_in.start()
     loads = [
         pltpu.make_async_copy(prob_hbm, prob, isem.at[0]),
         pltpu.make_async_copy(mixed_hbm, mixed, isem.at[1]),
@@ -1121,14 +1453,51 @@
     ]
     for load in loads:
         load.start()
-    hello(n, me, None, False)
+    if last:
+        later, inbox, xin, yin, din = sems[8:13]
+        block = d // 4
+        job_later = Reduce(
+            1, lambda c: later.at[pl.ds(c * block, block)], inbox, xin, yin, din, sems[13:17]
+        )
+        job = Reduce(
+            0, lambda c: grads.at[pl.ds(c * block, block)], inbox, xin, yin, din, sems[17:21]
+        )
+        swaps = [
+            remote(gives[k], outs[3 + k], sems[21].at[k], sems[22].at[k], section=1 - section)
+            for k in range(3)
+        ]
+        load_later = pltpu.make_async_copy(later_hbm, later, osem.at[0])
+
+        @pl.when(job_later.mine)
+        def _():
+            load_later.start()
+
+        hello(n, me, gy, True, True)
+
+        @pl.when(jnp.logical_not(job_later.mine))
+        def _():
+            for k in (3, 1, 2, 0):
+                c = job_later.cols[k]
+                job_later.give(k, later_hbm.at[pl.ds(c * block, block)]).start()
+
+        for swap in swaps:
+            swap.start()
+    else:
+        hello(n, me, None, False)
     dmids[:, pl.ds(pl.multiple_of(me * t, t), t)] = dmid_ref[...].astype(BF16).reshape(mb, t, d)
 
     def slot(z):
         return dmids.at[:, pl.ds(z * t, t)]
 
     z_gather_steps(n, me, slot, sems[:4], lambda z, k: None)
-    fetch_wait(own, held, wsem, (0,))
+    if last:
+
+        @pl.when(job_later.mine)
+        def _():
+            load_later.wait()
+
+        job_later.send_terms()
+    fetch_out.wait()
     every = dmids[...].reshape(mb * length, d)
     for j in range(span // 256):
         cols = slice(j * 256, (j + 1) * 256)
@@ -1161,13 +1530,15 @@
         return carry
 
     lax.fori_loop(0, heads, head, 0)
+    if last:
+        job_later.pass_on()
     dk = dkey[...]
     turned = dk * cosine - half_turn(dk) * sine
     unit, scale = unit_of(proj[:, span : span + HD])
     dgain_key[...] = jnp.sum(turned * unit, axis=0, keepdims=True)
     dproj[:, span : span + HD] = norm_back(turned * gain_key[...], unit, scale).astype(BF16)
     dproj[:, span + HD :] = dvalue[...].astype(BF16)
-    fetch_wait(own, held, wsem, (1,))
+    fetch_in.wait()
     both = dproj[...]
 
     def in_cols(j, carry):
@@ -1179,33 +1550,35 @@
         return carry
 
     lax.fori_loop(0, d // 256, in_cols, 0)
-    line = Line(n, sems[4:], zup, zdn, stage, acc)
-
-    def chunk_saves(i):
-        at = pl.ds(pl.multiple_of(i * 256, 256), 256)
-        return (
-            pltpu.make_async_copy(grad_in.at[at], grad_in_hbm.at[at], osem.at[0, i]),
-            pltpu.make_async_copy(grad_out.at[at], grad_out_hbm.at[at], osem.at[1, i]),
-        )
-
-    def weight_grads(first, last):
+    line = Line(n, sems[4:8], zup, zdn, stage, acc)
+
+    def weight_grads(begin, end):
         def chunk(i, carry):
             at = pl.ds(pl.multiple_of(i * 256, 256), 256)
             left = normed[:, :, at].reshape(mb * length, 256)
-            grad_in[at] = dot32(left, dproj[...], ROW_PAIR).astype(BF16)
+            grads[at, : span + 2 * HD] = dot32(left, dproj[...], ROW_PAIR).astype(BF16)
             left = dmids[:, :, at].reshape(mb * length, 256)
-            grad_out[at] = dot32(left, mixed[...], ROW_PAIR).astype(BF16)
-            for save in chunk_saves(i):
-                save.start()
+            grads[at, span + 2 * HD :] = dot32(left, mixed[...], ROW_PAIR).astype(BF16)
             return carry
 
-        lax.fori_loop(first, last, chunk, 0)
+        lax.fori_loop(begin, end, chunk, 0)
 
     chunks = d // 256
     for k, z in enumerate(line.z_list):
         add_rows(acc, col.at[z])
         line.move(z, total)
         weight_grads(chunks * k // len(line.z_list), chunks * (k + 1) // len(line.z_list))
+    if last:
+
+        @pl.when(jnp.logical_not(job.mine))
+        def _():
+            for k in (3, 1, 2, 0):
+                job.give(k, job.part(job.cols[k])).start()
+
+        job.send_terms()
+    else:
+        save = pltpu.make_async_copy(grads, outs[0], osem.at[0])
+        save.start()
     line.finish(total)
     hidden = x_ref[...].astype(F32)
     unit, scale = unit_of(hidden)
@@ -1213,21 +1586,56 @@
     dgain_attn[...] = jnp.sum(da * unit, axis=0, keepdims=True)
     cot_ref[...] = (dmid_ref[...] + norm_back(da * gain_attn[...], unit, scale)).astype(BF16)
     z_gather_drain(n, me, slot, sems[:4])
-    for i in range(chunks):
-        for save in chunk_saves(i):
-            save.wait()
-
-
-def attn_backward(layer, n, dmid, x, gains, tables, kept, own, other, cid, mb):
+    if not last:
+        save.wait()
+        return
+    job.pass_on()
+    closing = [(outs[0], 0, span), (outs[1], span, span + 2 * HD), (outs[2], span + 2 * HD, None)]
+    job_later.close(closing)
+    job.close(closing)
+    for swap in swaps:
+        swap.wait()
+
+    @pl.when(jnp.logical_not(job.mine))
+    def _():
+        for k in range(4):
+            job.give(k, job.part(job.cols[k])).wait_send()
+
+    @pl.when(jnp.logical_not(job_later.mine))
+    def _():
+        for k in range(4):
+            c = job_later.cols[k]
+            job_later.give(k, later_hbm.at[pl.ds(c * block, block)]).wait_send()
+
+
+def attn_backward(layer, n, dmid, x, gains, tables, kept, w_in, w_out, later, gives, cid, mb):
     r, d = x.shape
     cosine, sine, _ = tables
     normed, proj, qr, kr, v, prob, mixed = kept
     total_rows = cosine.shape[0]
     length = total_rows // mb
-    width = own[0].shape[1]
-    heads = own[1].shape[1] // HD
+    width = w_in.shape[1]
+    heads = w_out.shape[1] // HD
     span = heads * HD
     shape = jax.ShapeDtypeStruct
+    both = width + span
+    grad_shapes = [shape((d, both), BF16)]
+    extra = []
+    if later:
+        block = d // 4
+        grad_shapes = [
+            shape((block, span), F32),
+            shape((block, 2 * HD), BF16),
+            shape((block, span), F32),
+            *(shape(piece.shape, BF16) for piece in gives),
+        ]
+        extra = [
+            pltpu.VMEM((d, both), BF16),
+            pltpu.VMEM((4, block, both), BF16),
+            pltpu.VMEM((block, both), BF16),
+            pltpu.VMEM((block, both), BF16),
+            pltpu.VMEM((2, block // 2, both), BF16),
+        ] + reduce_sems() * 2 + [pltpu.SemaphoreType.DMA((3,))] * 2
     return pl.pallas_call(
         functools.partial(attn_backward_kernel, n, layer, heads),
         out_shape=(
@@ -1235,11 +1643,10 @@
             shape((1, d), F32),
             shape((1, HD), F32),
             shape((1, HD), F32),
-            shape((d, width), BF16),
-            shape((d, span), BF16),
+            *grad_shapes,
         ),
-        in_specs=in_vmem(9) + in_place(9),
-        out_specs=tuple(in_vmem(4) + in_place(2)),
+        in_specs=in_vmem(9) + in_place(7 + len(later) + len(gives)),
+        out_specs=tuple(in_vmem(4) + (in_vmem(3) + in_place(3) if later else in_place(1))),
         scratch_shapes=[
             pltpu.VMEM((d, width), BF16),
             pltpu.VMEM((d, span), BF16),
@@ -1253,18 +1660,18 @@
             pltpu.VMEM((total_rows, width), BF16),
             pltpu.VMEM((total_rows, HD), F32),
             pltpu.VMEM((total_rows, HD), F32),
-            pltpu.VMEM((d, width), BF16),
-            pltpu.VMEM((d, span), BF16),
+            pltpu.VMEM((d, both), BF16),
         ]
         + line_buffers(n, r, d)
         + [
             pltpu.SemaphoreType.DMA((2,)),
             pltpu.SemaphoreType.DMA((5,)),
-            pltpu.SemaphoreType.DMA((2, d // 256)),
+            pltpu.SemaphoreType.DMA((1,)),
         ]
-        + [pltpu.SemaphoreType.DMA((n,))] * 8,
+        + [pltpu.SemaphoreType.DMA((n,))] * 8
+        + extra,
         compiler_params=pltpu.CompilerParams(
-            collective_id=cid, has_side_effects=True, vmem_limit_bytes=60 << 20
+            collective_id=cid, has_side_effects=True, vmem_limit_bytes=63 << 20
         ),
         name="attn_backward",
     )(
@@ -1280,8 +1687,10 @@
         qr,
         prob,
         mixed,
-        *own,
-        *other,
+        w_in,
+        w_out,
+        *later,
+        *gives,
     )
 
 
@@ -1628,18 +2037,19 @@
     key_own = lax.dynamic_slice_in_dim(w_key[0], kv_head * HD, HD, 1)
     value_own = lax.dynamic_slice_in_dim(w_value[0], kv_head * HD, HD, 1)
     w_in_shard = jnp.concatenate([w_query[0], key_own, value_own], axis=1)
-    attn_own = (
-        lax.all_gather(w_in_shard, "gy", axis=0, tiled=True),
-        lax.all_gather(w_out[0], "gy", axis=0, tiled=True),
-    )
+    attn_shards = (w_in_shard, w_out[0])
+    attn_all = [share_weights(0, n_gx, attn_shards, 9)]
     moe_own = (w_gate[0, 0], w_up[0, 0], w_down[0, 0])
-    attn_other = tuple(swap_sections(w) for w in attn_own)
     moe_other = tuple(swap_sections(w) for w in moe_own)
     table = dense_gates(routes[0, :, 0], gates[0, :, 0], experts)
     small = jnp.concatenate(
         [table.reshape(-1), gain_attn[0], gain_ffn[0], gain_query[0], gain_key[0]]
     )
-    small_all = both_layers(small)
+    small_other = swap_sections(small)
+    is_first = section == 0
+    small_all = jnp.stack(
+        [jnp.where(is_first, small, small_other), jnp.where(is_first, small_other, small)]
+    )
     table_size = micro_count * local_rows * experts
     table_all = small_all[:, :table_size].reshape(n_sec, micro_count, local_rows, experts)
     gains_all = small_all[:, table_size:]
@@ -1674,18 +2084,19 @@
         tab_lo = (tab - tab_hi.astype(F32)).astype(BF16)
         pad = jnp.zeros((rows_own, 128 - 2 * experts), BF16)
         gate_cols = jnp.concatenate([tab_hi, tab_lo, pad], axis=1)
-        mid, payload, normed, proj, qr, kr, v, prob, mixed = attn_forward(
+        mid, payload, normed, proj, qr, kr, v, prob, mixed, *next_all = attn_forward(
             layer,
             n_gx,
             layer_in,
             split_gains(layer),
             tables,
             gate_cols,
-            attn_own,
-            attn_other,
+            *attn_all[layer],
+            attn_shards if layer == 0 else (),
             1 + layer,
             mb,
         )
+        attn_all.append(next_all)
         layer_out, *moe_kept = moe_forward(
             layer, n_gx, mid, payload, moe_own, moe_other, 3 + layer
         )
@@ -1694,13 +2105,13 @@
         layer_in = layer_out
 
     in_grads = [None] * n_sec
-    moe_grads = [None] * n_sec
-    attn_grads = [None] * n_sec
+    moe_sums = ()
+    later = ()
     gain_grads = [None] * n_sec
     for layer in reversed(range(n_sec)):
         g_attn, g_ffn, g_query, g_key = split_gains(layer)
         layer_in, mid, attn_kept, (arrived, weight, gp, up, inner) = kept[layer]
-        dmid, d_ffn, *moe_grads[layer] = moe_backward(
+        dmid, d_ffn, *moe_sums = moe_backward(
             layer,
             n_gx,
             cot,
@@ -1713,9 +2124,10 @@
             inner,
             moe_own,
             moe_other,
+            moe_sums,
             5 + layer,
         )
-        cot, d_attn, d_query, d_key, *attn_grads[layer] = attn_backward(
+        cot, d_attn, d_query, d_key, *later = attn_backward(
             layer,
             n_gx,
             dmid,
@@ -1723,51 +2135,35 @@
             (g_attn, g_query, g_key),
             tables,
             attn_kept,
-            attn_own,
-            attn_other,
+            *attn_all[layer],
+            later,
+            moe_sums[3:] if layer == 0 else (),
             7 + layer,
             mb,
         )
         in_grads[layer] = cot
         gain_grads[layer] = jnp.concatenate([d_attn, d_ffn, d_query, d_key], axis=1)
 
-    def own_layer_sum(pieces):
-        from_other = [
-            lax.ppermute(piece, "section", [(1 - layer, layer)])
-            for layer, piece in enumerate(pieces)
-        ]
-        sums = [a.astype(F32) + b.astype(F32) for a, b in zip(pieces, from_other)]
-        return jnp.where(section == 0, sums[0], sums[1])
-
+    query_grad, kv_shard, out_grad_w, *from_other = later
     grad_gate, grad_up, grad_down = (
-        own_layer_sum([moe_grads[layer][k] for layer in range(n_sec)])[None] for k in range(3)
+        (moe_sums[k].astype(F32) + from_other[k].astype(F32))[None] for k in range(3)
     )
-    grad_in, grad_out = (
-        lax.psum_scatter(
-            own_layer_sum([attn_grads[layer][k] for layer in range(n_sec)]).astype(BF16),
-            "gy",
-            scatter_dimension=0,
-            tiled=True,
-        ).astype(F32)
-        for k in range(2)
+    gain_sum, kv_all, out_rows, grad_rows = finish(
+        n_gx,
+        jnp.concatenate(gain_grads[::1], axis=0),
+        kv_shard,
+        jnp.stack(outs),
+        jnp.stack(in_grads),
+        10,
     )
-    query_grad = grad_in[:, :span]
-    kv_all = lax.all_gather(grad_in[:, span:], "gx", axis=0, tiled=False)
-    kv_all = jnp.sum(kv_all.reshape(KVH, n_gx // KVH, -1, 2, HD), axis=1)
+    kv_all = jnp.sum(kv_all.reshape(KVH, n_gx // KVH, -1, 2, HD).astype(F32), axis=1)
     key_part = jnp.swapaxes(kv_all[:, :, 0], 0, 1).reshape(-1, KVH * HD)
     value_part = jnp.swapaxes(kv_all[:, :, 1], 0, 1).reshape(-1, KVH * HD)
-    gain_sum = lax.psum(jnp.concatenate(gain_grads, axis=0), ("section", "gx", "gy"))
-    gain_sum = lax.dynamic_index_in_dim(gain_sum, section, 0, keepdims=True)
-
-    def own_layer_rows(pieces):
-        stacked = jnp.stack(pieces).reshape(n_sec, mb, local_rows, width)
-        return lax.all_to_all(stacked, "section", split_axis=0, concat_axis=0, tiled=True).reshape(
-            1, micro_count, 1, local_rows, width
-        )
+    whole_rows = (1, micro_count, 1, local_rows, width)
 
     return (
-        own_layer_rows(outs),
-        own_layer_rows(in_grads),
+        out_rows.reshape(whole_rows),
+        grad_rows.reshape(whole_rows),
         gain_sum[:, :width],
         gain_sum[:, width : 2 * width],
         gain_sum[:, 2 * width : 2 * width + HD],
@@ -1775,7 +2171,7 @@
         query_grad[None],
         key_part[None],
         value_part[None],
-        grad_out[None],
+        out_grad_w[None],
         grad_gate[:, None],
         grad_up[:, None],
         grad_down[:, None],

time: 961 us -> 811 us (0.84)
  waiting for transfers between devices: 175 us -> 0.01 us
  Pallas kernels: 588 us -> 746 us
  blocking collectives: 72.4 us -> 0 us
  other arithmetic: 54 us -> 23.3 us
  starting transfers between devices: 30.3 us -> 1.02 us
  between operations: 14.9 us -> 1.43 us
  local copies, waits for them, and re-layouts: 19 us -> 31.1 us
    all_gather x3 -> x0, waiting for transfers between devices: 156 us -> none  [the longest x1 63.4 us: local_fused(): lax.all_gather(w_in_shard, 'gy', axis=0, tiled=True)]
    pallas_call x0 -> x2, Pallas kernels: none -> 89.8 us  [the longest x1 47.4 us: share_weights(): pl.pallas_call(functools.partial(share_kernel, n, layer, len(shards)), ou...]
    pallas_call x2, Pallas kernels: 113 us -> 162 us  [attn_backward(): pl.pallas_call(functools.partial(attn_backward_kernel, n, layer, heads),...]
    psum x1 -> x0, blocking collectives: 40.5 us -> none  [local_fused(): lax.psum(jnp.concatenate(gain_grads, axis=0), ('section', 'gx', 'gy'))]
    ppermute x10 -> x0, starting transfers between devices: 29.1 us -> none  [own_layer_sum(): lax.ppermute(piece, 'section', [(1 - layer, layer)])]
    convert_element_type x3 -> x0, other arithmetic: 19.8 us -> none  [the longest x2 18.3 us: local_fused(): own_layer_sum([attn_grads[layer][k] for layer in range(n_sec)]).astype(BF16)]
    all_gather x1 -> x0, blocking collectives: 19.6 us -> none  [both_layers(): return lax.all_gather(tensor, 'section', axis=0, tiled=False)]
    ppermute x10 -> x0, waiting for transfers between devices: 17.6 us -> none  [own_layer_sum(): lax.ppermute(piece, 'section', [(1 - layer, layer)])]
  transfers between devices with their start and end apart: 20 -> 4, of which waited for: 6 -> 0; matrix products, arithmetic and copies ran while one was open for 5% -> 1% of each run, Pallas kernels for 21% -> 14%
where the time goes in v2:
time: 811 us; the launch traced here: 802 us
  Pallas kernels  746 us (92%)
  local copies, waits for them, and re-layouts  31.1 us (4%)
  other arithmetic  23.3 us (3%)
    pallas_call x2, Pallas kernels, moe_forward(): pl.pallas_call(functools.partial(moe_forward_kernel, n, layer), out_shape...  197 us
    pallas_call x2, Pallas kernels, moe_backward(): pl.pallas_call(functools.partial(moe_backward_kernel, n, layer), out_shap...  178 us
    pallas_call x2, Pallas kernels, attn_backward(): pl.pallas_call(functools.partial(attn_backward_kernel, n, layer, heads),...  162 us
    pallas_call x2, Pallas kernels, attn_forward(): pl.pallas_call(functools.partial(attn_forward_kernel, n, layer, heads), o...  118 us
    pallas_call x1, Pallas kernels, share_weights(): pl.pallas_call(functools.partial(share_kernel, n, layer, len(shards)), ou...  47.4 us
    pallas_call x1, Pallas kernels, finish(): pl.pallas_call(functools.partial(finish_kernel, n), out_shape=(shape((1,...  42.4 us
  transfers between devices with their start and end apart: 4, of which 0 were waited for; matrix products, arithmetic and copies ran while one was open for 1% of the time, Pallas kernels for 14%

profile of v2, /device:TPU:0, one launch (start us, length us, event | category | flops | bytes accessed | tf_op | source)
XLA Modules:
  0.0 802.4 jit_solution(2689606668356025730)
XLA Ops:
  0.7 0.9 select_reduce_fusion
  1.7 0.7 constant_dynamic-update-slice_fusion.3
  2.4 0.7 constant_dynamic-update-slice_fusion.2
  3.1 0.7 constant_dynamic-update-slice_fusion.1
  3.8 0.7 constant_dynamic-update-slice_fusion
  4.4 0.5 collective-permute-start
  5.0 0.5 collective-permute-start.2
  5.7 0.5 fusion.1
  6.3 0.8 fusion.mask_ref
  7.0 1.0 dynamic-slice_bitcast_fusion
  8.0 1.9 constant_dynamic-slice_fusion.3
  9.9 1.2 pad_maximum_fusion.refs_0_.rest_0_
  11.1 0.8 pad_maximum_fusion.3
  12.0 47.4 %share_weights.1 = (bf16[2048,1280]{1,0:T(8,128)(2,1)}, bf16[2048,1024]{1,0:T(8,128)(2,1)}) custom-call(bf16[512,1280]{1,0:T(8,128)(2,1)} %pad_maximum_fusion.refs_0_.rest_0_, bf16[512,1024]{1,0:T(8,128)(2,1)} %bitcast.73), custom_call_target="tpu_custom_call" | custom-call | tf_op jit(solution)/shard_map/share_weights/pallas_call | solution.py:930
  59.6 0.5 fusion.7
  60.1 0.7 maximum_maximum_fusion.2
  60.8 0.6 fusion.8
  61.4 62.3 %attn_forward.2 = (f32[64,2048]{1,0:T(8,128)}, bf16[64,2176]{1,0:T(8,128)(2,1)}, bf16[2,128,2048]{2,1,0:T(8,128)(2,1)}, f32[256,1280]{1,0:T(8,128)}, bf16[256,10...) custom-call(bf16[64,2048]{1,0:T(8,128)(2,1)} %bitcast.77, ...), custom_call_target="tpu_custom_call" | custom-call | tf_op jit(solution)/shard_map/attn_forward/pallas_call | solution.py:1348
  123.8 0.5 fusion.5
  124.3 0.6 fusion.6
  125.0 106.2 %moe_forward.2 = (bf16[64,2048]{1,0:T(8,128)(2,1)}, bf16[1024,2048]{1,0:T(8,128)(2,1)}, f32[1024,1]{1,0:T(8,128)}, bf16[1024,768]{1,0:T(8,128)(2,1)}, bf16[1024,...) custom-call(f32[64,2048]{1,0:T(8,128)} %get-tuple-element.84.mid_ref, bf16[64,2176]{1,0:T(8,128)(2,1)} %get-tuple-element.85.pay_ref, ...), custom_call_target="tpu_custom_call" | custom-call | tf_op jit(solution)/shard_map/moe_forward/pallas_call | solution.py:569
  231.2 55.8 %attn_forward.3 = (f32[64,2048]{1,0:T(8,128)}, bf16[64,2176]{1,0:T(8,128)(2,1)}, bf16[2,128,2048]{2,1,0:T(8,128)(2,1)}, f32[256,1280]{1,0:T(8,128)}, bf16[256,10...) custom-call(bf16[64,2048]{1,0:T(8,128)(2,1)} %get-tuple-element.86.x, ...), custom_call_target="tpu_custom_call" | custom-call | tf_op jit(solution)/shard_map/attn_forward/pallas_call | solution.py:1348
  287.0 90.6 %moe_forward.3 = (bf16[64,2048]{1,0:T(8,128)(2,1)}, bf16[1024,2048]{1,0:T(8,128)(2,1)}, f32[1024,1]{1,0:T(8,128)}, bf16[1024,768]{1,0:T(8,128)(2,1)}, bf16[1024,...) custom-call(f32[64,2048]{1,0:T(8,128)} %get-tuple-element.89.mid_ref, bf16[64,2176]{1,0:T(8,128)(2,1)} %get-tuple-element.90.pay_ref, ...), custom_call_target="tpu_custom_call" | custom-call | tf_op jit(solution)/shard_map/moe_forward/pallas_call | solution.py:569
  377.6 1.8 pad_maximum_fusion.1.lo_ref
  379.4 94.4 %moe_backward.2 = (f32[64,2048]{1,0:T(8,128)}, f32[1,2048]{1,0:T(1,128)}, bf16[2048,768]{1,0:T(8,128)(2,1)}, bf16[2048,768]{1,0:T(8,128)(2,1)}, bf16[768,2048]{1...) custom-call(bf16[64,2048]{1,0:T(8,128)(2,1)} %bitcast.82, ...), custom_call_target="tpu_custom_call" | custom-call | tf_op jit(solution)/shard_map/moe_backward/pallas_call | solution.py:785
  473.8 58.8 %attn_backward.2 = (bf16[64,2048]{1,0:T(8,128)(2,1)}, f32[1,2048]{1,0:T(1,128)}, f32[1,128]{1,0:T(1,128)}, f32[1,128]{1,0:T(1,128)}, bf16[2048,2304]{1,0:T(8,128)(2,1)}) custom-call(f32[64,2048]{1,0:T(8,128)} %get-tuple-element.96.dmid_ref, bf16[64,2048]{1,0:T(8,128)(2,1)} %get-tuple-element.86.x_ref, f32[1,2048]{1,0:T(1,128)} %get-tuple-element.203.gain_attn, ...), custom_call_target="tpu_custom_call" | custom-call | tf_op jit(solution)/shard_map/attn_backward/pallas_call | solution.py:1639
  532.6 84.1 %moe_backward.3 = (f32[64,2048]{1,0:T(8,128)}, f32[1,2048]{1,0:T(1,128)}, bf16[2048,768]{1,0:T(8,128)(2,1)}, bf16[2048,768]{1,0:T(8,128)(2,1)}, bf16[768,2048]{1...) custom-call(bf16[64,2048]{1,0:T(8,128)(2,1)} %get-tuple-element.104., ...), custom_call_target="tpu_custom_call", output_to_operand_aliasing={{2}: (14, {}), {3}: (15, {}), {4}: (16, {}), {5}: (17, {}),... | custom-call | tf_op jit(solution)/shard_map/moe_backward/pallas_call | solution.py:785
  616.8 103.5 %attn_backward.3 = (bf16[64,2048]{1,0:T(8,128)(2,1)}, f32[1,2048]{1,0:T(1,128)}, f32[1,128]{1,0:T(1,128)}, f32[1,128]{1,0:T(1,128)}, f32[512,1024]{1,0:T(8,128)}...) custom-call(f32[64,2048]{1,0:T(8,128)} %get-tuple-element.116.dmid_r, ...), custom_call_target="tpu_custom_call" | custom-call | tf_op jit(solution)/shard_map/attn_backward/pallas_call | solution.py:1639
  720.3 1.8 pad_maximum_fusion.2.ig_ref
  722.1 1.4 maximum_maximum_fusion.gains_ref
  723.5 42.4 %finish.1 = (f32[1,4352]{1,0:T(1,128)}, bf16[4,512,256]{2,1,0:T(8,128)(2,1)}, bf16[2,64,2048]{2,1,0:T(8,128)(2,1)}, bf16[2,64,2048]{2,1,0:T(8,128)(2,1)}) custom-call(f32[2,4352]{1,0:T(2,128)} %maximum_maximum_fusion.gains_ref, bf16[512,256]{1,0:T(8,128)(2,1)} %get-tuple-element.136.kv_ref, bf16[2,64,2048]{2,1,0:T(8,128)(2,1)} %pad_maximum_fusion.1.lo_ref, ...), custom_call_target="tpu_custom_call" | custom-call | tf_op jit(solution)/shard_map/finish/pallas_call | solution.py:1004
  765.9 1.2 fusion.9
  767.1 1.3 fusion.10
  768.4 2.1 reshape.114
  770.5 2.6 fusion.4
  773.1 1.6 copy.49
  774.8 2.8 broadcast_in_dim_reshape.7
  777.5 2.9 copy.48
  780.4 2.6 broadcast_in_dim_reshape.6
  783.0 5.4 add_bitcast_fusion.2
  788.4 3.9 add_bitcast_fusion.1
  792.3 1.2 copy-done.5
  793.5 4.0 add_bitcast_fusion
  797.5 0.8 copy.66
  798.3 0.8 copy.67
  799.1 0.2 copy-done.9
  799.3 1.3 copy.68
  800.6 1.3 copy.69
  (59 shorter events, 0.8 us)
Async XLA Ops:
  0.6 4.9 copy-start
  0.7 9.2 %copy-start.11 = (bf16[1,512,1024]{2,1,0:T(8,128)(2,1)S(1)}, bf16[1,512,1024]{2,1,0:T(8,128)(2,1)}, u32[]{:S(2)}) copy-start(bf16[1,512,1024]{2,1,0:T(8,128)(2,1)} %param.25) | copy-start | bytes 3145732
  4.4 54.9 %collective-permute-start = (f32[6400]{0:T(1024)S(1)}, f32[6400]{0:T(1024)S(1)}, u32[]{:S(2)}, u32[]{:S(2)}) collective-permute-start(f32[6400]{0:T(1024)S(1)} %constant_dynamic-update-slice_fusion), channel_id=1, source_target_pairs={{0,16},{16,0},{1,17},{17,1},{2,18},{18,2},{3,19},{19,3},{4,20},{20... | collective-permute-start | bytes 76808 | tf_op jit(solution)/shard_map/ppermute | solution.py:92
  4.9 120.0 %collective-permute-start.1 = (bf16[2048,768]{1,0:T(8,128)(2,1)}, bf16[2048,768]{1,0:T(8,128)(2,1)}, u32[]{:S(2)}, u32[]{:S(2)}) collective-permute-start(bf16[2048,768]{1,0:T(8,128)(2,1)} %bitcast.58), channel_id=1, source_target_pairs={{0,16},{16,0},{1,17},{17,1},{2,18},{18,2},{3,19},{19,3},{4,20},{20... | collective-permute-start | bytes 9437192 | tf_op jit(solution)/shard_map/ppermute | solution.py:92
  5.0 120.0 %collective-permute-start.2 = (bf16[2048,768]{1,0:T(8,128)(2,1)}, bf16[2048,768]{1,0:T(8,128)(2,1)}, u32[]{:S(2)}, u32[]{:S(2)}) collective-permute-start(bf16[2048,768]{1,0:T(8,128)(2,1)} %bitcast.63), channel_id=1, source_target_pairs={{0,16},{16,0},{1,17},{17,1},{2,18},{18,2},{3,19},{19,3},{4,20},{20... | collective-permute-start | bytes 9437192 | tf_op jit(solution)/shard_map/ppermute | solution.py:92
  5.4 119.5 %collective-permute-start.3 = (bf16[768,2048]{1,0:T(8,128)(2,1)}, bf16[768,2048]{1,0:T(8,128)(2,1)}, u32[]{:S(2)}, u32[]{:S(2)}) collective-permute-start(bf16[768,2048]{1,0:T(8,128)(2,1)} %bitcast.68), channel_id=1, source_target_pairs={{0,16},{16,0},{1,17},{17,1},{2,18},{18,2},{3,19},{19,3},{4,20},{20... | collective-permute-start | bytes 9437192 | tf_op jit(solution)/shard_map/ppermute | solution.py:92
  287.0 90.6 %copy-start.7 = (bf16[64,2048]{1,0:T(8,128)(2,1)S(1)}, bf16[64,2048]{1,0:T(8,128)(2,1)}, u32[]{:S(2)}) copy-start(bf16[64,2048]{1,0:T(8,128)(2,1)} %get-tuple-element.86.x_ref) | copy-start | bytes 786436
  616.7 103.6 %copy-start.10 = (bf16[64,2048]{1,0:T(8,128)(2,1)S(1)}, bf16[64,2048]{1,0:T(8,128)(2,1)}, u32[]{:S(2)}) copy-start(bf16[64,2048]{1,0:T(8,128)(2,1)} %get-tuple-element.104.cot_ref) | copy-start | bytes 786436
  616.7 105.4 %copy-start.14 = (f32[1,2048]{1,0:T(1,128)S(1)}, f32[1,2048]{1,0:T(1,128)}, u32[]{:S(2)}) copy-start(f32[1,2048]{1,0:T(1,128)} %get-tuple-element.133) | copy-start | bytes 24580
  616.7 105.4 %copy-start.15 = (f32[1,2048]{1,0:T(1,128)S(1)}, f32[1,2048]{1,0:T(1,128)}, u32[]{:S(2)}) copy-start(f32[1,2048]{1,0:T(1,128)} %get-tuple-element.132) | copy-start | bytes 24580
  616.7 105.4 %copy-start.16 = (f32[1,2048]{1,0:T(1,128)S(1)}, f32[1,2048]{1,0:T(1,128)}, u32[]{:S(2)}) copy-start(f32[1,2048]{1,0:T(1,128)} %get-tuple-element.129) | copy-start | bytes 24580
  616.8 105.4 %copy-start.17 = (f32[1,128]{1,0:T(1,128)S(1)}, f32[1,128]{1,0:T(1,128)}, u32[]{:S(2)}) copy-start(f32[1,128]{1,0:T(1,128)} %get-tuple-element.134) | copy-start | bytes 1540
  616.8 105.4 %copy-start.18 = (f32[1,128]{1,0:T(1,128)S(1)}, f32[1,128]{1,0:T(1,128)}, u32[]{:S(2)}) copy-start(f32[1,128]{1,0:T(1,128)} %get-tuple-element.135) | copy-start | bytes 1540
  774.8 8.3 %copy-start.2 = (bf16[2048,768]{1,0:T(8,128)(2,1)S(1)}, bf16[2048,768]{1,0:T(8,128)(2,1)}, u32[]{:S(2)}) copy-start(bf16[2048,768]{1,0:T(8,128)(2,1)} %get-tuple-element.145) | copy-start | bytes 9437188
  783.0 5.4 copy-start.3
  783.0 5.4 copy-start.6
  788.4 3.9 copy-start.4
  788.4 5.1 copy-start.5
  793.5 4.1 copy-start.13
  793.5 4.9 copy-start.12
  797.5 1.8 copy-start.9
  797.5 3.1 copy-start.8
  799.3 2.6 copy-start.1

commit v3 on v2

--- a/solution.py
+++ b/solution.py
@@ -222,10 +222,7 @@
         self.gy = lax.axis_index("gy")
         self.cx, self.cy, self.cd = (gy_flip(self.gy, bits) for bits in (1, 2, 3))
         self.gather_sems = sems[:10]
-        self.scatter_sems = sems[10:20]
-        self.z_list = []
-        for k in range((n + 1) // 2):
-            self.z_list += [n - 1 - k] + ([k] if k != n - 1 - k else [])
+        self.scatter_sems = sems[10:]
 
 
     def gather_own_column(self, slot):
@@ -284,109 +281,112 @@
             remote(one, one, sf.at[z], rf.at[z], gy=self.cx).wait_send()
 
 
-    def to_x(self, z):
-        sx, rx = self.scatter_sems[4:6]
-        return remote(self.part(z, self.cx), self.xin.at[z], sx.at[z], rx.at[z], gy=self.cx)
-
-    def to_y(self, z):
-        sy, ry = self.scatter_sems[6:8]
-        return remote(self.part(z, self.cy), self.yin.at[z], sy.at[z], ry.at[z], gy=self.cy)
+    def scatter_setup(self, part, sides, din, zup, zdn, stage, acc):
+        self.part, self.sides, self.din = part, sides, din
+        self.zup, self.zdn, self.stage, self.acc = zup, zdn, stage, acc
+
+    def column_of(self, side):
+        return self.cx * (1 - side) + self.cy * side
+
+    def near(self, side, z):
+        send, recv = self.scatter_sems[4:6]
+        column = self.column_of(side)
+        return remote(
+            self.part(z, column), self.sides.at[side, z], send.at[side, z], recv.at[side, z], gy=column
+        )
 
     def far(self, z):
-        sf, rf = self.scatter_sems[8:]
+        send, recv = self.scatter_sems[6:]
         return remote(
             self.part(z, self.cd),
             self.din.at[z],
-            sf.at[z],
-            rf.at[z],
-            gy=self.cx if z % 2 == 0 else self.cy,
-        )
-
-    def scatter_setup(self, part, xin, yin, din, zup, zdn, stage, acc):
-        self.part, self.xin, self.yin, self.din = part, xin, yin, din
-        self.zup, self.zdn, self.stage, self.acc = zup, zdn, stage, acc
-
-    def scatter_x(self):
-        for z in self.z_list:
-            if z % 2 == 0:
-                self.to_x(z).start()
-
-    def scatter_y(self):
-        for z in self.z_list:
-            if z % 2 == 1:
-                self.to_y(z).start()
+            send.at[z],
+            recv.at[z],
+            gy=self.column_of(lax.rem(z, 2)),
+        )
+
+    def each(self, call):
+        for k in [sign * far for far in reversed(range(1, self.n)) for sign in (-1, 1)] + [0]:
+
+            @pl.when((self.me + k >= 0) & (self.me + k < self.n))
+            def _():
+                call(self.me + k, k)
+
+    def scatter_near(self, side):
+        def send(z, k):
+            @pl.when(lax.rem(z, 2) == side)
+            def _():
+                self.near(side, z).start()
+
+        self.each(send)
 
     def scatter_far(self):
-        for z in self.z_list:
-            self.far(z).start()
-
-    def scatter_pass_on(self, z):
+        self.each(lambda z, k: self.far(z).start())
+
+    def scatter_pass_on(self, z, k):
         self.far(z).wait_recv()
-        mine = self.part(z, self.cy if z % 2 == 0 else self.cx)
+        side = 1 - lax.rem(z, 2)
+        mine = self.part(z, self.column_of(side))
         add_rows(mine, mine, self.din.at[z])
-        (self.to_y if z % 2 == 0 else self.to_x)(z).start()
-
-    def scatter_line(self, z, total):
+        self.near(side, z).start()
+
+    def along(self, z, up):
+        send, recv = self.scatter_sems[:2] if up else self.scatter_sems[2:4]
+        into = self.zup if up else self.zdn
+        return remote(
+            self.stage.at[z],
+            into.at[z],
+            send.at[z],
+            recv.at[z],
+            gx=self.me + 1 if up else self.me - 1,
+        )
+
+    def scatter_line(self, total, z, k):
         n, me, acc = self.n, self.me, self.acc
-        su, ru, sd, rd = self.scatter_sems[:4]
-        self.to_x(z).wait_recv()
-        self.to_y(z).wait_recv()
-        add_rows(acc, self.part(z, self.gy), self.xin.at[z], self.yin.at[z])
-        up = remote(self.stage.at[z], self.zup.at[z], su.at[z], ru.at[z], gx=me + 1)
-        down = remote(self.stage.at[z], self.zdn.at[z], sd.at[z], rd.at[z], gx=me - 1)
-
-        @pl.when((me < z) & (me > 0))
-        def _():
-            up.wait_recv()
-            add_rows(acc, acc, self.zup.at[z])
-
-        @pl.when((me > z) & (me < n - 1))
-        def _():
-            down.wait_recv()
-            add_rows(acc, acc, self.zdn.at[z])
-
-        @pl.when(me != z)
-        def _():
-            add_rows(self.stage.at[z], acc)
-
-        @pl.when(me < z)
-        def _():
-            up.start()
-
-        @pl.when(me > z)
-        def _():
-            down.start()
-
-        @pl.when(me == z)
-        def _():
-            add_rows(total, acc)
+        self.near(0, z).wait_recv()
+        self.near(1, z).wait_recv()
+        terms = (self.part(z, self.gy), self.sides.at[0, z], self.sides.at[1, z])
+        if k == 0:
+            add_rows(total, *terms)
+            return
+        came = me > 0 if k > 0 else me < n - 1
+
+        @pl.when(came)
+        def _():
+            self.along(z, k > 0).wait_recv()
+            add_rows(self.stage.at[z], *terms, (self.zup if k > 0 else self.zdn).at[z])
+
+        @pl.when(jnp.logical_not(came))
+        def _():
+            add_rows(self.stage.at[z], *terms)
+
+        self.along(z, k > 0).start()
 
     def scatter_finish(self, total):
         n, me = self.n, self.me
-        su, ru, sd, rd = self.scatter_sems[:4]
 
         @pl.when(me > 0)
         def _():
-            remote(self.stage.at[me], self.zup.at[me], su.at[me], ru.at[me], gx=me - 1).wait_recv()
+            self.along(me, True).wait_recv()
             add_rows(total, total, self.zup.at[me])
 
         @pl.when(me < n - 1)
         def _():
-            remote(self.stage.at[me], self.zdn.at[me], sd.at[me], rd.at[me], gx=me + 1).wait_recv()
+            self.along(me, False).wait_recv()
             add_rows(total, total, self.zdn.at[me])
 
-        for z in self.z_list:
-            self.to_x(z).wait_send()
-            self.to_y(z).wait_send()
+        for z in range(n):
+            self.near(0, z).wait_send()
+            self.near(1, z).wait_send()
             self.far(z).wait_send()
 
             @pl.when(me < z)
             def _():
-                remote(self.stage.at[z], self.zup.at[z], su.at[z], ru.at[z], gx=me + 1).wait_send()
+                self.along(z, True).wait_send()
 
             @pl.when(me > z)
             def _():
-                remote(self.stage.at[z], self.zdn.at[z], sd.at[z], rd.at[z], gx=me - 1).wait_send()
+                self.along(z, False).wait_send()
 
 
 def add_rows(out, *terms):
@@ -445,8 +445,7 @@
     wu,
     wd,
     part,
-    xin,
-    yin,
+    sides,
     din,
     zup,
     zdn,
@@ -478,7 +477,7 @@
     def slot(z, c):
         return pay.at[pl.ds((c * n + z) * r, r)]
 
-    plane.scatter_setup(lambda z, c: part.at[c * n + z], xin, yin, din, zup, zdn, stage, acc)
+    plane.scatter_setup(lambda z, c: part.at[c * n + z], sides, din, zup, zdn, stage, acc)
     plane.gather_own_column(slot)
     fetch_wait(own, held, wsem, range(3))
     expert = me * 4 + gy
@@ -518,11 +517,11 @@
 
         @pl.when(s == 1)
         def _():
-            plane.scatter_x()
+            plane.scatter_near(0)
 
         @pl.when(s == 2)
         def _():
-            plane.scatter_y()
+            plane.scatter_near(1)
 
         return carry
 
@@ -536,10 +535,8 @@
     ]
     for save in saves:
         save.start()
-    for z in plane.z_list:
-        plane.scatter_pass_on(z)
-    for z in plane.z_list:
-        plane.scatter_line(z, total)
+    plane.each(plane.scatter_pass_on)
+    plane.each(functools.partial(plane.scatter_line, total))
     plane.scatter_finish(total)
     add_rows(out_ref, mid_ref, total)
     plane.gather_drain(slot)
@@ -548,9 +545,13 @@
 
 
 def scatter_buffers(n, r, d):
-    return [pltpu.VMEM((4 * n, r, d), BF16)] + [pltpu.VMEM((n, r, d), BF16)] * 6 + [
-        pltpu.VMEM((r, d), F32)
-    ] * 2
+    block = pltpu.VMEM((n, r, d), BF16)
+    return [
+        pltpu.VMEM((4 * n, r, d), BF16),
+        pltpu.VMEM((2, n, r, d), BF16),
+        *[block] * 4,
+        *[pltpu.VMEM((r, d), F32)] * 2,
+    ]
 
 
 def in_vmem(count):
@@ -587,7 +588,9 @@
         + scatter_buffers(n, r, d)
         + [pltpu.VMEM((total_rows, ff), BF16)] * 3
         + [pltpu.SemaphoreType.DMA((3,)), pltpu.SemaphoreType.DMA((4,))]
-        + [pltpu.SemaphoreType.DMA((n,))] * 20,
+        + [pltpu.SemaphoreType.DMA((n,))] * 14
+        + [pltpu.SemaphoreType.DMA((2, n))] * 2
+        + [pltpu.SemaphoreType.DMA((n,))] * 2,
         compiler_params=pltpu.CompilerParams(
             collective_id=cid, has_side_effects=True, vmem_limit_bytes=63 << 20
         ),
@@ -623,8 +626,7 @@
     wu,
     wd,
     part,
-    xin,
-    yin,
+    sides,
     din,
     zup,
     zdn,
@@ -670,7 +672,7 @@
     def slot(z, c):
         return cots.at[pl.ds((c * n + z) * r, r)]
 
-    plane.scatter_setup(lambda z, c: part.at[c * n + z], xin, yin, din, zup, zdn, stage, acc)
+    plane.scatter_setup(lambda z, c: part.at[c * n + z], sides, din, zup, zdn, stage, acc)
     plane.gather_own_column(slot)
     fetch_wait(own, held, wsem, range(3))
     for load in loads:
@@ -709,11 +711,11 @@
 
         @pl.when(s == 1)
         def _():
-            plane.scatter_x()
+            plane.scatter_near(0)
 
         @pl.when(s == 2)
         def _():
-            plane.scatter_y()
+            plane.scatter_near(1)
 
         return carry
 
@@ -751,14 +753,14 @@
     chunks = d // 256
     cut = [0, chunks * 2 // 8, chunks * 4 // 8, chunks * 6 // 8, chunks]
     weight_grads(cut[0], cut[1])
-    for z in plane.z_list:
-        plane.scatter_pass_on(z)
+    plane.each(plane.scatter_pass_on)
     weight_grads(cut[1], cut[2])
-    for k, z in enumerate(plane.z_list):
-        plane.scatter_line(z, total)
-        if k == 0:
-            weight_grads(cut[2], cut[3])
-    weight_grads(cut[3], cut[4])
+
+    def line(z, k):
+        plane.scatter_line(total, z, k)
+
+    plane.each(line)
+    weight_grads(cut[2], cut[4])
     plane.scatter_finish(total)
 
     mid = mid_ref[...]
@@ -809,7 +811,9 @@
             pltpu.SemaphoreType.DMA((4,)),
         ]
         + [pltpu.SemaphoreType.DMA((3, d // 256))]
-        + [pltpu.SemaphoreType.DMA((n,))] * 20,
+        + [pltpu.SemaphoreType.DMA((n,))] * 14
+        + [pltpu.SemaphoreType.DMA((2, n))] * 2
+        + [pltpu.SemaphoreType.DMA((n,))] * 2,
         compiler_params=pltpu.CompilerParams(
             collective_id=cid, has_side_effects=True, vmem_limit_bytes=63 << 20
         ),
@@ -945,10 +949,12 @@
     lo_ref,
     ig_ref,
     gain_ref,
-    kv_all_ref,
+    key_ref,
+    value_ref,
     lo_all_ref,
     ig_all_ref,
     gbuf,
+    kv_all_ref,
     stage,
     incoming,
     lsem,
@@ -964,8 +970,10 @@
     gbuf[me] = gains_ref[...]
     kv_all_ref[me] = kv_ref[...]
     hello(n, me, gy, True, True)
-    z_gather_steps(n, me, lambda z: gbuf.at[z], sems[:4], lambda z, k: None)
-    z_gather_steps(n, me, lambda z: kv_all_ref.at[z], sems[4:8], lambda z, k: None)
+    few = Line(n, None, lambda z: gbuf.at[z], None, sems[:4])
+    many = Line(n, None, lambda z: kv_all_ref.at[z], None, sems[4:8])
+    many.gather_step(0)
+    few.gather_step(0)
     keeps = []
     for k, (src, dst) in enumerate(((lo_ref, lo_all_ref), (ig_ref, ig_all_ref))):
         keep = pltpu.make_async_copy(src.at[section], dst.at[section], lsem.at[k])
@@ -973,6 +981,11 @@
         keep.start()
         give.start()
         keeps.append((keep, give))
+    steps = [functools.partial(many.gather_step, k) for k in range(1, n)]
+    for k in range(1, n):
+        few.gather_step(k)
+        if k == n // 2:
+            steps.pop(0)()
     total = gbuf[0]
     for z in range(1, n):
         total = total + gbuf[z]
@@ -980,6 +993,8 @@
         stage[k] = total
         swap = remote(stage.at[k], incoming.at[k], rsem.at[0, k], rsem.at[1, k], **where)
         swap.start()
+        if k and steps:
+            steps.pop(0)()
         swap.wait()
         total = total + incoming[k]
 
@@ -991,11 +1006,17 @@
     def _():
         gain_ref[...] = total[1:2]
 
+    for step in steps:
+        step()
+    for z in range(n):
+        cols = slice(z * HD, (z + 1) * HD)
+        key_ref[:, cols] = kv_all_ref[z, :, :HD].astype(F32)
+        value_ref[:, cols] = kv_all_ref[z, :, HD:].astype(F32)
     for keep, give in keeps:
         keep.wait()
         give.wait()
-    z_gather_drain(n, me, lambda z: gbuf.at[z], sems[:4])
-    z_gather_drain(n, me, lambda z: kv_all_ref.at[z], sems[4:8])
+    few.gather_drain()
+    many.gather_drain()
 
 
 def finish(n, gains, kv, lo, ig, cid):
@@ -1005,14 +1026,16 @@
         functools.partial(finish_kernel, n),
         out_shape=(
             shape((1, gains.shape[1]), F32),
-            shape((n,) + kv.shape, BF16),
+            shape((kv.shape[0], n * HD), F32),
+            shape((kv.shape[0], n * HD), F32),
             shape(lo.shape, BF16),
             shape(ig.shape, BF16),
         ),
         in_specs=in_vmem(4),
-        out_specs=tuple(in_vmem(4)),
+        out_specs=tuple(in_vmem(5)),
         scratch_shapes=[
             pltpu.VMEM((n,) + gains.shape, F32),
+            pltpu.VMEM((n,) + kv.shape, BF16),
             pltpu.VMEM((3,) + gains.shape, F32),
             pltpu.VMEM((3,) + gains.shape, F32),
             dma((2,)),
@@ -1067,22 +1090,17 @@
             gy=self.cols[bit],
         )
 
-    def send_terms(self):
-        def add(k):
-            self.give(k, self.part(self.cols[k])).wait_recv()
+    def send_term(self, k):
+        @pl.when(self.mine)
+        def _():
             ref = self.part(self.cols[k])
+            self.give(k, ref).wait_recv()
             add_rows(ref, ref, self.inbox.at[self.cols[k]])
-
-        @pl.when(self.mine)
-        def _():
-            add(3)
-            self.far(1).start()
-            self.far(2).start()
-            add(1)
-            self.near(1, 0).start()
-            add(2)
-            self.near(2, 1).start()
-            add(0)
+            if k == 3:
+                self.far(1).start()
+                self.far(2).start()
+            elif k:
+                self.near(k, k - 1).start()
 
     def pass_on(self):
         @pl.when(self.mine)
@@ -1118,54 +1136,82 @@
 
 
 class Line:
-    def __init__(self, n, sems, zup, zdn, stage, acc):
-        self.n = n
+    def __init__(self, n, m, slot, terms, sems):
+        self.n, self.m, self.slot = n, m, slot
         self.me = lax.axis_index("gx")
-        self.sems = sems
-        self.zup, self.zdn, self.stage, self.acc = zup, zdn, stage, acc
-        self.z_list = []
-        for k in range((n + 1) // 2):
-            self.z_list += [n - 1 - k] + ([k] if k != n - 1 - k else [])
+        if terms is not None:
+            self.col, self.zup, self.zdn, self.stage = (ref.at[m] for ref in terms)
+        self.sems = [sem if m is None else sem.at[m] for sem in sems]
+
+    def gather_up(self, k):
+        ref = self.slot(self.me - k)
+        return remote(ref, ref, self.sems[0].at[k], self.sems[1].at[k], gx=self.me + 1)
+
+    def gather_down(self, k):
+        ref = self.slot(self.me + k)
+        return remote(ref, ref, self.sems[2].at[k], self.sems[3].at[k], gx=self.me - 1)
+
+    def gather_step(self, k):
+        n, me = self.n, self.me
+
+        @pl.when(me - k >= 0)
+        def _():
+            if k:
+                ref = self.slot(me - k)
+                sems = self.sems
+                remote(ref, ref, sems[0].at[k - 1], sems[1].at[k - 1], gx=me + 1).wait_recv()
+            if k < n - 1:
+
+                @pl.when(me + 1 < n)
+                def _():
+                    self.gather_up(k).start()
+
+        @pl.when(me + k < n)
+        def _():
+            if k:
+                ref = self.slot(me + k)
+                sems = self.sems
+                remote(ref, ref, sems[2].at[k - 1], sems[3].at[k - 1], gx=me - 1).wait_recv()
+            if k < n - 1:
+
+                @pl.when(me > 0)
+                def _():
+                    self.gather_down(k).start()
 
     def up(self, z):
-        su, ru = self.sems[:2]
-        return remote(self.stage.at[z], self.zup.at[z], su.at[z], ru.at[z], gx=self.me + 1)
+        send, recv = self.sems[4:6]
+        return remote(self.stage.at[z], self.zup.at[z], send.at[z], recv.at[z], gx=self.me + 1)
 
     def down(self, z):
-        sd, rd = self.sems[2:]
-        return remote(self.stage.at[z], self.zdn.at[z], sd.at[z], rd.at[z], gx=self.me - 1)
-
-    def move(self, z, total):
-        n, me, acc = self.n, self.me, self.acc
-
-        @pl.when((me < z) & (me > 0))
-        def _():
-            self.up(z).wait_recv()
-            add_rows(acc, acc, self.zup.at[z])
-
-        @pl.when((me > z) & (me < n - 1))
-        def _():
-            self.down(z).wait_recv()
-            add_rows(acc, acc, self.zdn.at[z])
-
-        @pl.when(me != z)
-        def _():
-            add_rows(self.stage.at[z], acc)
-
-        @pl.when(me < z)
-        def _():
-            self.up(z).start()
-
-        @pl.when(me > z)
-        def _():
-            self.down(z).start()
-
-        @pl.when(me == z)
-        def _():
-            add_rows(total, acc)
-
-    def finish(self, total):
+        send, recv = self.sems[6:8]
+        return remote(self.stage.at[z], self.zdn.at[z], send.at[z], recv.at[z], gx=self.me - 1)
+
+    def scatter_tick(self, hop):
         n, me = self.n, self.me
+
+        @pl.when(me == hop)
+        def _():
+            for z in reversed(range(hop + 1, n)):
+                if hop:
+                    self.up(z).wait_recv()
+                    add_rows(self.stage.at[z], self.col.at[z], self.zup.at[z])
+                else:
+                    add_rows(self.stage.at[z], self.col.at[z])
+                self.up(z).start()
+
+        @pl.when(me == n - 1 - hop)
+        def _():
+            for z in range(n - 1 - hop):
+                if hop:
+                    self.down(z).wait_recv()
+                    add_rows(self.stage.at[z], self.col.at[z], self.zdn.at[z])
+                else:
+                    add_rows(self.stage.at[z], self.col.at[z])
+                self.down(z).start()
+
+    def scatter_finish(self, total):
+        n, me = self.n, self.me
+        add_rows(total, self.col.at[me])
 
         @pl.when(me > 0)
         def _():
@@ -1177,7 +1223,22 @@
             self.down(me).wait_recv()
             add_rows(total, total, self.zdn.at[me])
 
-        for z in self.z_list:
+    def gather_drain(self):
+        n, me = self.n, self.me
+        for k in range(n - 1):
+
+            @pl.when((me - k >= 0) & (me + 1 < n))
+            def _():
+                self.gather_up(k).wait_send()
+
+            @pl.when((me + k < n) & (me > 0))
+            def _():
+                self.gather_down(k).wait_send()
+
+    def drain(self):
+        n, me = self.n, self.me
+        self.gather_drain()
+        for z in range(n):
 
             @pl.when(me < z)
             def _():
@@ -1230,7 +1291,6 @@
     zup,
     zdn,
     stage,
-    acc,
     total,
     wsem,
     osem,
@@ -1255,11 +1315,78 @@
     unit, _ = unit_of(hidden)
     low = (unit * gain_attn[...]).astype(BF16)
     normed[:, pl.ds(pl.multiple_of(me * t, t), t)] = low.reshape(mb, t, d)
-
-    def slot(z):
-        return normed.at[:, pl.ds(z * t, t)]
-
-    z_gather_steps(n, me, slot, sems[:4], lambda z, k: None)
+    lines = [
+        Line(
+            n,
+            m,
+            lambda z, m=m: normed.at[m, pl.ds(z * t, t)],
+            (col, zup, zdn, stage),
+            sems[:8],
+        )
+        for m in range(mb)
+    ]
+    waiting = []
+
+    def tick():
+        if waiting:
+            waiting.pop(0)()
+
+    for k in range(n):
+        lines[0].gather_step(k)
+        if k == min(1, n - 1):
+            for line in lines[1:]:
+                line.gather_step(0)
+    fetch_in.wait()
+    cosine, sine = cos_ref[...], sin_ref[...]
+    for m, line in enumerate(lines):
+        first = m * length
+        rows = slice(first, first + length)
+        if m + 1 < mb:
+            waiting += [functools.partial(lines[m + 1].gather_step, k) for k in range(1, n)]
+        for j in range((span + 2 * HD) // 256):
+            cols = slice(j * 256, (j + 1) * 256)
+            proj[rows, cols] = jnp.dot(normed[m], win[:, cols], preferred_element_type=F32)
+            if j == 2:
+                tick()
+        tick()
+        key_unit, _ = unit_of(proj[rows, span : span + HD])
+        key = key_unit * gain_key[...]
+        kr_ref[rows] = (key * cosine[rows] + half_turn(key) * sine[rows]).astype(BF16)
+        v_ref[rows] = proj[rows, span + HD :].astype(BF16)
+
+        def head(h, carry, m=m, rows=rows):
+            at = pl.ds(pl.multiple_of(h * HD, HD), HD)
+            query_unit, _ = unit_of(proj[rows, at])
+            query = query_unit * gain_query[...]
+            turned = (query * cosine[rows] + half_turn(query) * sine[rows]).astype(BF16)
+            qr[rows, at] = turned
+            scores = dot32(turned, kr_ref[rows], COL_PAIR) * (1.0 / math.sqrt(HD))
+            exponent = jnp.where(mask_ref[m] > 0.5, jnp.exp(scores), 0.0)
+            p = (exponent / jnp.sum(exponent, axis=-1, keepdims=True)).astype(BF16)
+            prob[m * heads + h] = p
+            mixed[rows, at] = jnp.dot(p, v_ref[rows], preferred_element_type=F32).astype(BF16)
+            return carry
+
+        lax.fori_loop(0, heads // 2, head, 0, unroll=2)
+        tick()
+        lax.fori_loop(heads // 2, heads, head, 0, unroll=2)
+        while waiting:
+            tick()
+        if m == 0:
+            for share in shares:
+                share.pass_on()
+            fetch_out.wait()
+
+        def out_cols(j, carry, m=m, rows=rows):
+            at = pl.ds(pl.multiple_of(j * 256, 256), 256)
+            res = dot32(mixed[rows], wout[at], COL_PAIR).astype(BF16)
+            for z in range(n):
+                col[m, z, :, at] = res[z * t : (z + 1) * t]
+            return carry
+
+        lax.fori_loop(0, d // 256, out_cols, 0)
+        line.scatter_tick(0)
+        waiting += [functools.partial(line.scatter_tick, hop) for hop in range(1, n - 1)]
     saves = [
         pltpu.make_async_copy(normed, normed_hbm, osem.at[0]),
         pltpu.make_async_copy(proj, proj_hbm, osem.at[1]),
@@ -1267,57 +1394,12 @@
         pltpu.make_async_copy(prob, prob_hbm, osem.at[3]),
         pltpu.make_async_copy(mixed, mixed_hbm, osem.at[4]),
     ]
-    saves[0].start()
-    fetch_in.wait()
-    every = normed[...].reshape(mb * length, d)
-    for j in range((span + 2 * HD) // 256):
-        cols = slice(j * 256, (j + 1) * 256)
-        proj[:, cols] = jnp.dot(every, win[:, cols], preferred_element_type=F32)
-    saves[1].start()
-    cosine, sine = cos_ref[...], sin_ref[...]
-    key_unit, _ = unit_of(proj[:, span : span + HD])
-    key = key_unit * gain_key[...]
-    kr_ref[...] = (key * cosine + half_turn(key) * sine).astype(BF16)
-    v_ref[...] = proj[:, span + HD :].astype(BF16)
-
-    def head(h, carry):
-        at = pl.ds(pl.multiple_of(h * HD, HD), HD)
-        query_unit, _ = unit_of(proj[:, at])
-        query = query_unit * gain_query[...]
-        turned = (query * cosine + half_turn(query) * sine).astype(BF16)
-        qr[:, at] = turned
-        for m in range(mb):
-            rows = slice(m * length, (m + 1) * length)
-            scores = dot32(turned[rows], kr_ref[rows], COL_PAIR) * (1.0 / math.sqrt(HD))
-            exponent = jnp.where(mask_ref[m] > 0.5, jnp.exp(scores), 0.0)
-            p = (exponent / jnp.sum(exponent, axis=-1, keepdims=True)).astype(BF16)
-            prob[m * heads + h] = p
-            mixed[rows, at] = jnp.dot(p, v_ref[rows], preferred_element_type=F32).astype(BF16)
-        return carry
-
-    lax.fori_loop(0, heads, head, 0)
-    saves[2].start()
-    saves[3].start()
-    saves[4].start()
-    for share in shares:
-        share.pass_on()
-    fetch_out.wait()
-    both = mixed[...]
-
-    def out_cols(j, carry):
-        at = pl.ds(pl.multiple_of(j * 256, 256), 256)
-        res = dot32(both, wout[at], COL_PAIR).astype(BF16)
-        for m in range(mb):
-            for z in range(n):
-                col[z, m * t : (m + 1) * t, at] = res[m * length + z * t : m * length + (z + 1) * t]
-        return carry
-
-    lax.fori_loop(0, d // 256, out_cols, 0)
-    line = Line(n, sems[4:8], zup, zdn, stage, acc)
-    for z in line.z_list:
-        add_rows(acc, col.at[z])
-        line.move(z, total)
-    line.finish(total)
+    for save in saves:
+        save.start()
+    while waiting:
+        tick()
+    for m, line in enumerate(lines):
+        line.scatter_finish(total.at[m * t : (m + 1) * t])
     mid = x_ref[...].astype(F32) + total[...]
     mid_ref[...] = mid
     unit, _ = unit_of(mid)
@@ -1327,13 +1409,14 @@
         share.finish()
     for share in shares:
         share.drain()
-    z_gather_drain(n, me, slot, sems[:4])
+    for line in lines:
+        line.drain()
     for save in saves:
         save.wait()
 
 
-def line_buffers(n, r, d):
-    return [pltpu.VMEM((n, r, d), BF16)] * 4 + [pltpu.VMEM((r, d), F32)] * 2
+def line_buffers(mb, n, r, d):
+    return [pltpu.VMEM((mb, n, r // mb, d), BF16)] * 4 + [pltpu.VMEM((r, d), F32)]
 
 
 def attn_forward(layer, n, x, gains, tables, gate_cols, w_in, w_out, shards, cid, mb):
@@ -1370,9 +1453,9 @@
             pltpu.VMEM((mb * heads, length, length), BF16),
             pltpu.VMEM((total_rows, span), BF16),
         ]
-        + line_buffers(n, r, d)
+        + line_buffers(mb, n, r, d)
         + [pltpu.SemaphoreType.DMA((2,)), pltpu.SemaphoreType.DMA((5,))]
-        + [pltpu.SemaphoreType.DMA((n,))] * 8
+        + [pltpu.SemaphoreType.DMA((mb, n))] * 8
         + [item for shard in shards for item in share_scratch(shard)],
         compiler_params=pltpu.CompilerParams(
             collective_id=cid, has_side_effects=True, vmem_limit_bytes=60 << 20
@@ -1426,7 +1509,6 @@
     zup,
     zdn,
     stage,
-    acc,
     total,
     wsem,
     isem,
@@ -1485,34 +1567,61 @@
     else:
         hello(n, me, None, False)
     dmids[:, pl.ds(pl.multiple_of(me * t, t), t)] = dmid_ref[...].astype(BF16).reshape(mb, t, d)
-
-    def slot(z):
-        return dmids.at[:, pl.ds(z * t, t)]
-
-    z_gather_steps(n, me, slot, sems[:4], lambda z, k: None)
+    lines = [
+        Line(
+            n,
+            m,
+            lambda z, m=m: dmids.at[m, pl.ds(z * t, t)],
+            (col, zup, zdn, stage),
+            sems[:8],
+        )
+        for m in range(mb)
+    ]
+    waiting = []
+    sums = []
+
+    def tick():
+        if waiting:
+            waiting.pop(0)()
+        if sums:
+            sums.pop(0)()
+
+    for k in range(n):
+        lines[0].gather_step(k)
+        if k == min(1, n - 1):
+            for line in lines[1:]:
+                line.gather_step(0)
     if last:
 
         @pl.when(job_later.mine)
         def _():
             load_later.wait()
 
-        job_later.send_terms()
+        sums += [functools.partial(job_later.send_term, k) for k in (3, 1, 2, 0)]
+        sums += [job_later.pass_on]
+    tick()
     fetch_out.wait()
-    every = dmids[...].reshape(mb * length, d)
-    for j in range(span // 256):
-        cols = slice(j * 256, (j + 1) * 256)
-        dheads[:, cols] = jnp.dot(every, wout[:, cols], preferred_element_type=F32).astype(BF16)
     for load in loads:
         load.wait()
     cosine, sine = cos_ref[...], sin_ref[...]
     dkey[...] = jnp.zeros_like(dkey)
     dvalue[...] = jnp.zeros_like(dvalue)
     dgain_query[...] = jnp.zeros_like(dgain_query)
-
-    def head(h, carry):
-        at = pl.ds(pl.multiple_of(h * HD, HD), HD)
-        for m in range(mb):
-            rows = slice(m * length, (m + 1) * length)
+    dgain_key[...] = jnp.zeros_like(dgain_key)
+    for m, line in enumerate(lines):
+        first = m * length
+        rows = slice(first, first + length)
+        if m + 1 < mb:
+            waiting += [functools.partial(lines[m + 1].gather_step, k) for k in range(1, n)]
+        for j in range(span // 256):
+            cols = slice(j * 256, (j + 1) * 256)
+            dheads[rows, cols] = jnp.dot(
+                dmids[m], wout[:, cols], preferred_element_type=F32
+            ).astype(BF16)
+        tick()
+
+        def head(h, carry, m=m, rows=rows):
+            at = pl.ds(pl.multiple_of(h * HD, HD), HD)
             p = prob[m * heads + h]
             dh = dheads[rows, at]
             dvalue[rows] += dot32(p, dh, ROW_PAIR)
@@ -1527,65 +1636,74 @@
             unit, scale = unit_of(proj[rows, at])
             dgain_query[...] += jnp.sum(turned * unit, axis=0, keepdims=True)
             dproj[rows, at] = norm_back(turned * gain_query[...], unit, scale).astype(BF16)
-        return carry
-
-    lax.fori_loop(0, heads, head, 0)
-    if last:
-        job_later.pass_on()
-    dk = dkey[...]
-    turned = dk * cosine - half_turn(dk) * sine
-    unit, scale = unit_of(proj[:, span : span + HD])
-    dgain_key[...] = jnp.sum(turned * unit, axis=0, keepdims=True)
-    dproj[:, span : span + HD] = norm_back(turned * gain_key[...], unit, scale).astype(BF16)
-    dproj[:, span + HD :] = dvalue[...].astype(BF16)
-    fetch_in.wait()
-    both = dproj[...]
-
-    def in_cols(j, carry):
-        at = pl.ds(pl.multiple_of(j * 256, 256), 256)
-        res = dot32(both, win[at], COL_PAIR).astype(BF16)
-        for m in range(mb):
+            return carry
+
+        lax.fori_loop(0, heads // 2, head, 0, unroll=2)
+        tick()
+        lax.fori_loop(heads // 2, heads, head, 0, unroll=2)
+        tick()
+        dk = dkey[rows]
+        turned = dk * cosine[rows] - half_turn(dk) * sine[rows]
+        unit, scale = unit_of(proj[rows, span : span + HD])
+        dgain_key[...] += jnp.sum(turned * unit, axis=0, keepdims=True)
+        dproj[rows, span : span + HD] = norm_back(turned * gain_key[...], unit, scale).astype(BF16)
+        dproj[rows, span + HD :] = dvalue[rows].astype(BF16)
+        if m == 0:
+            fetch_in.wait()
+        while waiting:
+            tick()
+
+        def in_cols(j, carry, m=m, rows=rows):
+            at = pl.ds(pl.multiple_of(j * 256, 256), 256)
+            res = dot32(dproj[rows], win[at], COL_PAIR).astype(BF16)
             for z in range(n):
-                col[z, m * t : (m + 1) * t, at] = res[m * length + z * t : m * length + (z + 1) * t]
-        return carry
-
-    lax.fori_loop(0, d // 256, in_cols, 0)
-    line = Line(n, sems[4:8], zup, zdn, stage, acc)
-
-    def weight_grads(begin, end):
+                col[m, z, :, at] = res[z * t : (z + 1) * t]
+            return carry
+
+        lax.fori_loop(0, d // 256, in_cols, 0)
+        line.scatter_tick(0)
+        waiting += [functools.partial(line.scatter_tick, hop) for hop in range(1, n - 1)]
+    while sums:
+        sums.pop(0)()
+
+    def weight_grads(c):
         def chunk(i, carry):
-            at = pl.ds(pl.multiple_of(i * 256, 256), 256)
+            at = pl.ds(pl.multiple_of(c * (d // 4) + i * 256, 256), 256)
             left = normed[:, :, at].reshape(mb * length, 256)
             grads[at, : span + 2 * HD] = dot32(left, dproj[...], ROW_PAIR).astype(BF16)
             left = dmids[:, :, at].reshape(mb * length, 256)
             grads[at, span + 2 * HD :] = dot32(left, mixed[...], ROW_PAIR).astype(BF16)
             return carry
 
-        lax.fori_loop(begin, end, chunk, 0)
-
-    chunks = d // 256
-    for k, z in enumerate(line.z_list):
-        add_rows(acc, col.at[z])
-        line.move(z, total)
-        weight_grads(chunks * k // len(line.z_list), chunks * (k + 1) // len(line.z_list))
+        lax.fori_loop(0, d // 4 // 256, chunk, 0)
+
+    for bits in (3, 1, 2, 0):
+        c = gy_flip(gy, bits)
+        weight_grads(c)
+        if last:
+
+            @pl.when(jnp.logical_not(job.mine))
+            def _():
+                job.give(bits, job.part(c)).start()
+
+        tick()
+    while waiting:
+        tick()
     if last:
-
-        @pl.when(jnp.logical_not(job.mine))
-        def _():
-            for k in (3, 1, 2, 0):
-                job.give(k, job.part(job.cols[k])).start()
-
-        job.send_terms()
+        for k in (3, 1, 2, 0):
+            job.send_term(k)
     else:
         save = pltpu.make_async_copy(grads, outs[0], osem.at[0])
         save.start()
-    line.finish(total)
+    for m, line in enumerate(lines):
+        line.scatter_finish(total.at[m * t : (m + 1) * t])
     hidden = x_ref[...].astype(F32)
     unit, scale = unit_of(hidden)
     da = total[...]
     dgain_attn[...] = jnp.sum(da * unit, axis=0, keepdims=True)
     cot_ref[...] = (dmid_ref[...] + norm_back(da * gain_attn[...], unit, scale)).astype(BF16)
-    z_gather_drain(n, me, slot, sems[:4])
+    for line in lines:
+        line.drain()
     if not last:
         save.wait()
         return
@@ -1662,13 +1780,13 @@
             pltpu.VMEM((total_rows, HD), F32),
             pltpu.VMEM((d, both), BF16),
         ]
-        + line_buffers(n, r, d)
+        + line_buffers(mb, n, r, d)
         + [
             pltpu.SemaphoreType.DMA((2,)),
             pltpu.SemaphoreType.DMA((5,)),
             pltpu.SemaphoreType.DMA((1,)),
         ]
-        + [pltpu.SemaphoreType.DMA((n,))] * 8
+        + [pltpu.SemaphoreType.DMA((mb, n))] * 8
         + extra,
         compiler_params=pltpu.CompilerParams(
             collective_id=cid, has_side_effects=True, vmem_limit_bytes=63 << 20
@@ -2148,7 +2266,7 @@
     grad_gate, grad_up, grad_down = (
         (moe_sums[k].astype(F32) + from_other[k].astype(F32))[None] for k in range(3)
     )
-    gain_sum, kv_all, out_rows, grad_rows = finish(
+    gain_sum, key_part, value_part, out_rows, grad_rows = finish(
         n_gx,
         jnp.concatenate(gain_grads[::1], axis=0),
         kv_shard,
@@ -2156,9 +2274,6 @@
         jnp.stack(in_grads),
         10,
     )
-    kv_all = jnp.sum(kv_all.reshape(KVH, n_gx // KVH, -1, 2, HD).astype(F32), axis=1)
-    key_part = jnp.swapaxes(kv_all[:, :, 0], 0, 1).reshape(-1, KVH * HD)
-    value_part = jnp.swapaxes(kv_all[:, :, 1], 0, 1).reshape(-1, KVH * HD)
     whole_rows = (1, micro_count, 1, local_rows, width)
 
     return (
@@ -2182,7 +2297,7 @@
     inputs = args[0]
     n = lax.axis_size("gx")
     rows_own = inputs.shape[0] // lax.axis_size("section") * inputs.shape[2]
-    if 4 * n * rows_own > MOST_ROWS:
+    if 4 * n * rows_own > MOST_ROWS or n != KVH:
         return local_wide(*args)
     return local_fused(*args)
 

time: 811 us -> 724 us (0.89)
  Pallas kernels: 746 us -> 671 us
  local copies, waits for them, and re-layouts: 31.1 us -> 18.5 us
    pallas_call x2, Pallas kernels: 197 us -> 177 us  [moe_forward(): pl.pallas_call(functools.partial(moe_forward_kernel, n, layer), out_shape...]
    pallas_call x2, Pallas kernels: 162 us -> 147 us  [attn_backward(): pl.pallas_call(functools.partial(attn_backward_kernel, n, layer, heads),...]
    pallas_call x2, Pallas kernels: 178 us -> 163 us  [moe_backward(): pl.pallas_call(functools.partial(moe_backward_kernel, n, layer), out_shap...]
    pallas_call x1, Pallas kernels: 42.4 us -> 28.7 us  [finish(): pl.pallas_call(functools.partial(finish_kernel, n), out_shape=(shape((1,...]
    pallas_call x2, Pallas kernels: 118 us -> 108 us  [attn_forward(): pl.pallas_call(functools.partial(attn_forward_kernel, n, layer, heads), o...]
  transfers between devices with their start and end apart: 4 -> 4, of which waited for: 0 -> 0; matrix products, arithmetic and copies ran while one was open for 1% -> 1% of each run, Pallas kernels for 14% -> 15%
where the time goes in v3:
time: 724 us; the launch traced here: 716 us
  Pallas kernels  671 us (93%)
  other arithmetic  24.4 us (3%)
  local copies, waits for them, and re-layouts  18.5 us (3%)
    pallas_call x2, Pallas kernels, moe_forward(): pl.pallas_call(functools.partial(moe_forward_kernel, n, layer), out_shape...  177 us
    pallas_call x2, Pallas kernels, moe_backward(): pl.pallas_call(functools.partial(moe_backward_kernel, n, layer), out_shap...  163 us
    pallas_call x2, Pallas kernels, attn_backward(): pl.pallas_call(functools.partial(attn_backward_kernel, n, layer, heads),...  147 us
    pallas_call x2, Pallas kernels, attn_forward(): pl.pallas_call(functools.partial(attn_forward_kernel, n, layer, heads), o...  108 us
    pallas_call x1, Pallas kernels, share_weights(): pl.pallas_call(functools.partial(share_kernel, n, layer, len(shards)), ou...  47.4 us
    pallas_call x1, Pallas kernels, finish(): pl.pallas_call(functools.partial(finish_kernel, n), out_shape=(shape((1,...  28.7 us
  transfers between devices with their start and end apart: 4, of which 0 were waited for; matrix products, arithmetic and copies ran while one was open for 1% of the time, Pallas kernels for 15%

profile of v3, /device:TPU:0, one launch (start us, length us, event | category | flops | bytes accessed | tf_op | source)
XLA Modules:
  0.0 716.1 jit_solution(2468484732947981719)
XLA Ops:
  0.7 0.9 select_reduce_fusion
  1.6 0.1 reshape.102
  1.7 0.7 constant_dynamic-update-slice_fusion.3
  2.4 0.7 constant_dynamic-update-slice_fusion.2
  3.1 0.7 constant_dynamic-update-slice_fusion.1
  3.8 0.7 constant_dynamic-update-slice_fusion
  4.4 0.5 collective-permute-start
  5.0 0.5 collective-permute-start.2
  5.5 0.2 convert_reduce_fusion
  5.7 0.5 fusion.1
  6.3 0.8 fusion.mask_ref
  7.0 1.0 dynamic-slice_bitcast_fusion
  8.0 1.9 constant_dynamic-slice_fusion.3
  9.9 1.2 pad_maximum_fusion.refs_0_.rest_0_
  11.1 0.8 pad_maximum_fusion.3
  12.0 47.4 %share_weights.1 = (bf16[2048,1280]{1,0:T(8,128)(2,1)}, bf16[2048,1024]{1,0:T(8,128)(2,1)}) custom-call(bf16[512,1280]{1,0:T(8,128)(2,1)} %pad_maximum_fusion.refs_0_.rest_0_, bf16[512,1024]{1,0:T(8,128)(2,1)} %bitcast.69), custom_call_target="tpu_custom_call" | custom-call | tf_op jit(solution)/shard_map/share_weights/pallas_call | solution.py:934
  59.5 0.1 reshape.103
  59.6 0.5 fusion.6
  60.1 0.7 maximum_maximum_fusion.2
  60.8 0.6 fusion.7
  61.4 58.8 %attn_forward.2 = (f32[64,2048]{1,0:T(8,128)}, bf16[64,2176]{1,0:T(8,128)(2,1)}, bf16[2,128,2048]{2,1,0:T(8,128)(2,1)}, f32[256,1280]{1,0:T(8,128)}, bf16[256,10...) custom-call(bf16[64,2048]{1,0:T(8,128)(2,1)} %bitcast.71, ...), custom_call_target="tpu_custom_call" | custom-call | tf_op jit(solution)/shard_map/attn_forward/pallas_call | solution.py:1431
  120.3 0.5 fusion.4
  120.8 0.6 fusion.5
  121.4 95.3 %moe_forward.2 = (bf16[64,2048]{1,0:T(8,128)(2,1)}, bf16[1024,2048]{1,0:T(8,128)(2,1)}, f32[1024,1]{1,0:T(8,128)}, bf16[1024,768]{1,0:T(8,128)(2,1)}, bf16[1024,...) custom-call(f32[64,2048]{1,0:T(8,128)} %get-tuple-element.85.mid_ref, bf16[64,2176]{1,0:T(8,128)(2,1)} %get-tuple-element.86.pay_ref, ...), custom_call_target="tpu_custom_call" | custom-call | tf_op jit(solution)/shard_map/moe_forward/pallas_call | solution.py:570
  216.8 49.2 %attn_forward.3 = (f32[64,2048]{1,0:T(8,128)}, bf16[64,2176]{1,0:T(8,128)(2,1)}, bf16[2,128,2048]{2,1,0:T(8,128)(2,1)}, f32[256,1280]{1,0:T(8,128)}, bf16[256,10...) custom-call(bf16[64,2048]{1,0:T(8,128)(2,1)} %get-tuple-element.87.x, ...), custom_call_target="tpu_custom_call" | custom-call | tf_op jit(solution)/shard_map/attn_forward/pallas_call | solution.py:1431
  266.0 81.5 %moe_forward.3 = (bf16[64,2048]{1,0:T(8,128)(2,1)}, bf16[1024,2048]{1,0:T(8,128)(2,1)}, f32[1024,1]{1,0:T(8,128)}, bf16[1024,768]{1,0:T(8,128)(2,1)}, bf16[1024,...) custom-call(f32[64,2048]{1,0:T(8,128)} %get-tuple-element.90.mid_ref, bf16[64,2176]{1,0:T(8,128)(2,1)} %get-tuple-element.91.pay_ref, ...), custom_call_target="tpu_custom_call" | custom-call | tf_op jit(solution)/shard_map/moe_forward/pallas_call | solution.py:570
  347.6 1.8 pad_maximum_fusion.1.lo_ref
  349.4 85.3 %moe_backward.2 = (f32[64,2048]{1,0:T(8,128)}, f32[1,2048]{1,0:T(1,128)}, bf16[2048,768]{1,0:T(8,128)(2,1)}, bf16[2048,768]{1,0:T(8,128)(2,1)}, bf16[768,2048]{1...) custom-call(bf16[64,2048]{1,0:T(8,128)(2,1)} %bitcast.76, ...), custom_call_target="tpu_custom_call" | custom-call | tf_op jit(solution)/shard_map/moe_backward/pallas_call | solution.py:787
  434.7 48.5 %attn_backward.2 = (bf16[64,2048]{1,0:T(8,128)(2,1)}, f32[1,2048]{1,0:T(1,128)}, f32[1,128]{1,0:T(1,128)}, f32[1,128]{1,0:T(1,128)}, bf16[2048,2304]{1,0:T(8,128)(2,1)}) custom-call(f32[64,2048]{1,0:T(8,128)} %get-tuple-element.97.dmid_ref, bf16[64,2048]{1,0:T(8,128)(2,1)} %get-tuple-element.87.x_ref, f32[1,2048]{1,0:T(1,128)} %get-tuple-element.203.gain_attn, ...), custom_call_target="tpu_custom_call" | custom-call | tf_op jit(solution)/shard_map/attn_backward/pallas_call | solution.py:1757
  483.2 77.8 %moe_backward.3 = (f32[64,2048]{1,0:T(8,128)}, f32[1,2048]{1,0:T(1,128)}, bf16[2048,768]{1,0:T(8,128)(2,1)}, bf16[2048,768]{1,0:T(8,128)(2,1)}, bf16[768,2048]{1...) custom-call(bf16[64,2048]{1,0:T(8,128)(2,1)} %get-tuple-element.105., ...), custom_call_target="tpu_custom_call", output_to_operand_aliasing={{2}: (14, {}), {3}: (15, {}), {4}: (16, {}), {5}: (17, {}),... | custom-call | tf_op jit(solution)/shard_map/moe_backward/pallas_call | solution.py:787
  561.1 98.1 %attn_backward.3 = (bf16[64,2048]{1,0:T(8,128)(2,1)}, f32[1,2048]{1,0:T(1,128)}, f32[1,128]{1,0:T(1,128)}, f32[1,128]{1,0:T(1,128)}, f32[512,1024]{1,0:T(8,128)}...) custom-call(f32[64,2048]{1,0:T(8,128)} %get-tuple-element.117.dmid_r, ...), custom_call_target="tpu_custom_call" | custom-call | tf_op jit(solution)/shard_map/attn_backward/pallas_call | solution.py:1757
  659.2 1.8 pad_maximum_fusion.2.ig_ref
  661.0 1.4 maximum_maximum_fusion.gains_ref
  662.3 28.7 %finish.1 = (f32[1,4352]{1,0:T(1,128)}, f32[512,512]{1,0:T(8,128)}, f32[512,512]{1,0:T(8,128)}, bf16[2,64,2048]{2,1,0:T(8,128)(2,1)}, bf16[2,64,2048]{2,1,0:T(8,128)(2,1)}) custom-call(f32[2,4352]{1,0:T(2,128)} %maximum_maximum_fusion.gains_ref, bf16[512,256]{1,0:T(8,128)(2,1)} %get-tuple-element.137.kv_ref, bf16[2,64,2048]{2,1,0:T(8,128)(2,1)} %pad_maximum_fusion.1.lo_ref, ...), custom_call_target="tpu_custom_call" | custom-call | tf_op jit(solution)/shard_map/finish/pallas_call | solution.py:1025
  691.1 1.1 fusion.8
  692.2 1.3 fusion.9
  693.5 6.4 add_bitcast_fusion.2
  699.9 3.9 add_bitcast_fusion.1
  703.8 1.2 copy-done.4
  705.0 4.0 add_bitcast_fusion
  709.1 0.8 copy.62
  709.9 0.8 copy.63
  710.7 0.2 copy-done.8
  710.9 1.3 copy.64
  712.2 1.0 copy.65
  713.2 1.0 copy.66
  714.1 0.1 copy-done.7
  714.3 1.3 copy.67
  (57 shorter events, 0.4 us)
Async XLA Ops:
  0.6 4.9 copy-start
  0.7 9.2 %copy-start.10 = (bf16[1,512,1024]{2,1,0:T(8,128)(2,1)S(1)}, bf16[1,512,1024]{2,1,0:T(8,128)(2,1)}, u32[]{:S(2)}) copy-start(bf16[1,512,1024]{2,1,0:T(8,128)(2,1)} %param.25) | copy-start | bytes 3145732
  4.4 54.9 %collective-permute-start = (f32[6400]{0:T(1024)S(1)}, f32[6400]{0:T(1024)S(1)}, u32[]{:S(2)}, u32[]{:S(2)}) collective-permute-start(f32[6400]{0:T(1024)S(1)} %constant_dynamic-update-slice_fusion), channel_id=1, source_target_pairs={{0,16},{16,0},{1,17},{17,1},{2,18},{18,2},{3,19},{19,3},{4,20},{20... | collective-permute-start | bytes 76808 | tf_op jit(solution)/shard_map/ppermute | solution.py:92
  4.9 116.5 %collective-permute-start.1 = (bf16[2048,768]{1,0:T(8,128)(2,1)}, bf16[2048,768]{1,0:T(8,128)(2,1)}, u32[]{:S(2)}, u32[]{:S(2)}) collective-permute-start(bf16[2048,768]{1,0:T(8,128)(2,1)} %bitcast.54), channel_id=1, source_target_pairs={{0,16},{16,0},{1,17},{17,1},{2,18},{18,2},{3,19},{19,3},{4,20},{20... | collective-permute-start | bytes 9437192 | tf_op jit(solution)/shard_map/ppermute | solution.py:92
  5.0 116.5 %collective-permute-start.2 = (bf16[2048,768]{1,0:T(8,128)(2,1)}, bf16[2048,768]{1,0:T(8,128)(2,1)}, u32[]{:S(2)}, u32[]{:S(2)}) collective-permute-start(bf16[2048,768]{1,0:T(8,128)(2,1)} %bitcast.59), channel_id=1, source_target_pairs={{0,16},{16,0},{1,17},{17,1},{2,18},{18,2},{3,19},{19,3},{4,20},{20... | collective-permute-start | bytes 9437192 | tf_op jit(solution)/shard_map/ppermute | solution.py:92
  5.4 116.0 %collective-permute-start.3 = (bf16[768,2048]{1,0:T(8,128)(2,1)}, bf16[768,2048]{1,0:T(8,128)(2,1)}, u32[]{:S(2)}, u32[]{:S(2)}) collective-permute-start(bf16[768,2048]{1,0:T(8,128)(2,1)} %bitcast.64), channel_id=1, source_target_pairs={{0,16},{16,0},{1,17},{17,1},{2,18},{18,2},{3,19},{19,3},{4,20},{20... | collective-permute-start | bytes 9437192 | tf_op jit(solution)/shard_map/ppermute | solution.py:92
  266.0 81.5 %copy-start.6 = (bf16[64,2048]{1,0:T(8,128)(2,1)S(1)}, bf16[64,2048]{1,0:T(8,128)(2,1)}, u32[]{:S(2)}) copy-start(bf16[64,2048]{1,0:T(8,128)(2,1)} %get-tuple-element.87.x_ref) | copy-start | bytes 786436
  561.0 98.1 %copy-start.9 = (bf16[64,2048]{1,0:T(8,128)(2,1)S(1)}, bf16[64,2048]{1,0:T(8,128)(2,1)}, u32[]{:S(2)}) copy-start(bf16[64,2048]{1,0:T(8,128)(2,1)} %get-tuple-element.105.cot_ref) | copy-start | bytes 786436
  561.0 99.9 %copy-start.15 = (f32[1,2048]{1,0:T(1,128)S(1)}, f32[1,2048]{1,0:T(1,128)}, u32[]{:S(2)}) copy-start(f32[1,2048]{1,0:T(1,128)} %get-tuple-element.134) | copy-start | bytes 24580
  561.0 99.9 %copy-start.16 = (f32[1,2048]{1,0:T(1,128)S(1)}, f32[1,2048]{1,0:T(1,128)}, u32[]{:S(2)}) copy-start(f32[1,2048]{1,0:T(1,128)} %get-tuple-element.133) | copy-start | bytes 24580
  561.1 99.9 %copy-start.17 = (f32[1,2048]{1,0:T(1,128)S(1)}, f32[1,2048]{1,0:T(1,128)}, u32[]{:S(2)}) copy-start(f32[1,2048]{1,0:T(1,128)} %get-tuple-element.130) | copy-start | bytes 24580
  561.1 99.9 %copy-start.18 = (f32[1,128]{1,0:T(1,128)S(1)}, f32[1,128]{1,0:T(1,128)}, u32[]{:S(2)}) copy-start(f32[1,128]{1,0:T(1,128)} %get-tuple-element.135) | copy-start | bytes 1540
  561.1 99.9 %copy-start.19 = (f32[1,128]{1,0:T(1,128)S(1)}, f32[1,128]{1,0:T(1,128)}, u32[]{:S(2)}) copy-start(f32[1,128]{1,0:T(1,128)} %get-tuple-element.136) | copy-start | bytes 1540
  693.5 6.4 copy-start.2
  693.5 6.4 copy-start.5
  699.9 3.9 copy-start.3
  699.9 5.1 copy-start.4
  705.0 4.1 copy-start.14
  705.0 4.9 copy-start.13
  709.1 1.8 copy-start.8
  709.1 3.1 copy-start.12
  710.9 2.3 copy-start.11
  712.2 2.1 copy-start.7
  712.2 3.4 copy-start.1

commit v4 on v3

--- a/solution.py
+++ b/solution.py
@@ -392,12 +392,14 @@
 def add_rows(out, *terms):
     rows = out.shape[0]
     step = 16
+    short = len(terms) == 2 and all(ref.dtype == BF16 for ref in (out, *terms))
+    kind = BF16 if short else F32
 
     def body(i, carry):
         at = pl.ds(pl.multiple_of(i * step, step), step)
-        value = terms[0][at].astype(F32)
+        value = terms[0][at].astype(kind)
         for term in terms[1:]:
-            value = value + term[at].astype(F32)
+            value = value + term[at].astype(kind)
         out[at] = value.astype(out.dtype)
         return carry
 
@@ -500,20 +502,28 @@
         weight = jnp.sum(jnp.where(hit, gate_cols, 0.0), axis=1, keepdims=True)
         weight_ref[at] = weight
         block = pay[at, :d]
-        for j in range(ff // 256):
-            cols = slice(j * 256, (j + 1) * 256)
+
+        def mid_cols(j, carry):
+            cols = pl.ds(pl.multiple_of(j * 256, 256), 256)
             g = jnp.dot(block, wg[:, cols], preferred_element_type=F32)
             u = jnp.dot(block, wu[:, cols], preferred_element_type=F32)
             gp[at, cols] = g.astype(BF16)
             up[at, cols] = u.astype(BF16)
             inner[at, cols] = (g / (1.0 + jnp.exp(-g)) * u).astype(BF16)
+            return carry
+
+        lax.fori_loop(0, ff // 256, mid_cols, 0)
         act = inner[at]
-        for j in range(d // 256):
-            cols = slice(j * 256, (j + 1) * 256)
+
+        def out_cols(j, carry):
+            cols = pl.ds(pl.multiple_of(j * 256, 256), 256)
             res = jnp.dot(act, wd[:, cols], preferred_element_type=F32) * weight
             part[pl.ds(pl.multiple_of(c * n, n), n), :, cols] = (
                 res.astype(BF16).reshape(n, r, 256)
             )
+            return carry
+
+        lax.fori_loop(0, d // 256, out_cols, 0)
 
         @pl.when(s == 1)
         def _():
@@ -692,22 +702,30 @@
         at = pl.ds(pl.multiple_of(c * rows, rows), rows)
         de[at] = (cots[at].astype(F32) * weight_ref[at]).astype(BF16)
         block = de[at]
-        for j in range(ff // 256):
-            cols = slice(j * 256, (j + 1) * 256)
+
+        def mid_cols(j, carry):
+            cols = pl.ds(pl.multiple_of(j * 256, 256), 256)
             dz = dot32(block, wd[cols], COL_PAIR)
             g = gp[at, cols].astype(F32)
             u = up[at, cols].astype(F32)
             sg = 1.0 / (1.0 + jnp.exp(-g))
             gp[at, cols] = (dz * u * sg * (1.0 + g * (1.0 - sg))).astype(BF16)
             up[at, cols] = (dz * g * sg).astype(BF16)
+            return carry
+
+        lax.fori_loop(0, ff // 256, mid_cols, 0)
         dgp = gp[at]
         dup = up[at]
-        for j in range(d // 256):
-            cols = slice(j * 256, (j + 1) * 256)
+
+        def in_cols(j, carry):
+            cols = pl.ds(pl.multiple_of(j * 256, 256), 256)
             res = dot32(dgp, wg[cols], COL_PAIR) + dot32(dup, wu[cols], COL_PAIR)
             part[pl.ds(pl.multiple_of(c * n, n), n), :, cols] = (
                 res.astype(BF16).reshape(n, r, 256)
             )
+            return carry
+
+        lax.fori_loop(0, d // 256, in_cols, 0)
 
         @pl.when(s == 1)
         def _():
@@ -728,39 +746,36 @@
             where = (slice(None), at) if k == 2 else (at, slice(None))
             yield pltpu.make_async_copy(src.at[where], ref.at[where], osem.at[k, i])
 
-    def weight_grads(first, last):
-        def chunk(i, carry):
-            at = pl.ds(pl.multiple_of(i * 256, 256), 256)
-            left = arrived[:, at]
-            out_gate[at] = dot32(left, gp[...], ROW_PAIR).astype(BF16)
-            out_up[at] = dot32(left, up[...], ROW_PAIR).astype(BF16)
-            out_down[:, at] = dot32(inner[...], de[:, at], ROW_PAIR).astype(BF16)
-
-            @pl.when(section == layer)
-            def _():
-                for copy in saving(i, keep_refs):
-                    copy.start()
-
-            @pl.when(section != layer)
-            def _():
-                for copy in saving(i, give_refs):
-                    copy.start()
-
-            return carry
-
-        lax.fori_loop(first, last, chunk, 0)
-
     chunks = d // 256
-    cut = [0, chunks * 2 // 8, chunks * 4 // 8, chunks * 6 // 8, chunks]
-    weight_grads(cut[0], cut[1])
-    plane.each(plane.scatter_pass_on)
-    weight_grads(cut[1], cut[2])
-
-    def line(z, k):
-        plane.scatter_line(total, z, k)
-
-    plane.each(line)
-    weight_grads(cut[2], cut[4])
+
+    def weight_grads(i, carry):
+        at = pl.ds(pl.multiple_of(i * 256, 256), 256)
+        left = arrived[:, at]
+        out_gate[at] = dot32(left, gp[...], ROW_PAIR).astype(BF16)
+        out_up[at] = dot32(left, up[...], ROW_PAIR).astype(BF16)
+        out_down[:, at] = dot32(inner[...], de[:, at], ROW_PAIR).astype(BF16)
+
+        @pl.when(section == layer)
+        def _():
+            for copy in saving(i, keep_refs):
+                copy.start()
+
+        @pl.when(section != layer)
+        def _():
+            for copy in saving(i, give_refs):
+                copy.start()
+
+        @pl.when(i == chunks // 4 - 1)
+        def _():
+            plane.each(plane.scatter_pass_on)
+
+        @pl.when(i == chunks // 2 - 1)
+        def _():
+            plane.each(functools.partial(plane.scatter_line, total))
+
+        return carry
+
+    lax.fori_loop(0, chunks, weight_grads, 0)
     plane.scatter_finish(total)
 
     mid = mid_ref[...]
@@ -822,14 +837,20 @@
 
 
 class Share:
-    def __init__(self, layer, shard, full, scratch):
-        self.shard, self.full = shard, full
-        self.held, self.plane_sems, self.to_sems, self.from_sems = scratch
+    def __init__(self, layer, pieces, full, scratch):
+        self.full = full
+        self.held, self.load_sems, self.plane_sems, self.to_sems, self.from_sems = scratch
+        self.loads, first = [], 0
+        for k, piece in enumerate(pieces):
+            last = first + piece.shape[1]
+            into = self.held.at[:, first:last]
+            self.loads.append(pltpu.make_async_copy(piece, into, self.load_sems.at[k]))
+            first = last
         self.section = lax.axis_index("section")
         self.mine = self.section == layer
         gy = lax.axis_index("gy")
         self.cols = [gy_flip(gy, bits) if bits else gy for bits in range(4)]
-        self.rows = shard.shape[0]
+        self.rows = self.held.shape[0]
 
     def at(self, column, half=None):
         rows = self.rows
@@ -838,15 +859,14 @@
         few = rows // 2
         return self.full.at[pl.ds(pl.multiple_of(column * rows + half * few, few), few)]
 
-    def own(self, step):
-        src, dst = ((self.shard, self.held), (self.held, self.at(self.cols[0])))[step]
-        return pltpu.make_async_copy(src, dst, self.plane_sems.at[9 * step])
+    def own(self):
+        return pltpu.make_async_copy(self.held, self.at(self.cols[0]), self.plane_sems.at[0])
 
     def direct(self, bit):
         s = self.plane_sems
         k = 1 if bit == 1 else 3
         return remote(
-            self.shard, self.at(self.cols[0]), s.at[k], s.at[k + 1], gy=self.cols[bit]
+            self.held, self.at(self.cols[0]), s.at[k], s.at[k + 1], gy=self.cols[bit]
         )
 
     def onward(self, bit):
@@ -858,7 +878,7 @@
 
     def hand(self, k):
         if k == 0:
-            src, dst = self.shard, self.at(self.cols[0])
+            src, dst = self.held, self.at(self.cols[0])
         elif k < 3:
             src = dst = self.at(self.cols[k])
         else:
@@ -868,16 +888,18 @@
     def start(self):
         @pl.when(self.mine)
         def _():
+            for load in self.loads:
+                load.start()
+            for load in self.loads:
+                load.wait()
             self.direct(1).start()
             self.direct(2).start()
-            self.own(0).start()
+            self.own().start()
             self.hand(0).start()
 
     def pass_on(self):
         @pl.when(self.mine)
         def _():
-            self.own(0).wait()
-            self.own(1).start()
             self.direct(1).wait_recv()
             self.onward(2).start()
             self.hand(1).start()
@@ -892,7 +914,7 @@
             self.hand(3).start()
             self.onward(1).wait_recv()
             self.hand(4).start()
-            self.own(1).wait()
+            self.own().wait()
 
         @pl.when(jnp.logical_not(self.mine))
         def _():
@@ -909,15 +931,32 @@
                 self.hand(k).wait_send()
 
 
-def share_scratch(shard):
+def share_scratch(shape):
     dma = pltpu.SemaphoreType.DMA
-    return [pltpu.VMEM(shard.shape, BF16), dma((10,)), dma((5,)), dma((5,))]
-
-
-def share_kernel(n, layer, count, *refs):
-    shards, fulls, scratch = refs[:count], refs[count : 2 * count], refs[2 * count :]
+    return [pltpu.VMEM(shape, BF16), dma((3,)), dma((9,)), dma((5,)), dma((5,))]
+
+
+def shard_pieces(query, key, value, out):
+    heads = query.shape[2] // HD
+    kv_head = lax.axis_index("gx") * heads // (HQ // KVH)
+    own = pl.ds(pl.multiple_of(kv_head * HD, HD), HD)
+    return [(query.at[0], key.at[0, :, own], value.at[0, :, own]), (out.at[0],)]
+
+
+def shard_shapes(shards):
+    rows, span = shards[0].shape[1:]
+    return [(rows, span + 2 * HD), (rows, span)]
+
+
+def full_shapes(shards):
+    return [jax.ShapeDtypeStruct((4 * rows, cols), BF16) for rows, cols in shard_shapes(shards)]
+
+
+def share_kernel(n, layer, *refs):
+    fulls, scratch = refs[4:6], refs[6:]
     shares = [
-        Share(layer, shards[k], fulls[k], scratch[4 * k : 4 * k + 4]) for k in range(count)
+        Share(layer, pieces, fulls[k], scratch[5 * k : 5 * k + 5])
+        for k, pieces in enumerate(shard_pieces(*refs[:4]))
     ]
     hello(n, lax.axis_index("gx"), lax.axis_index("gy"), True, True)
     for share in shares:
@@ -932,55 +971,33 @@
 
 def share_weights(layer, n, shards, cid):
     return pl.pallas_call(
-        functools.partial(share_kernel, n, layer, len(shards)),
-        out_shape=tuple(jax.ShapeDtypeStruct((4 * w.shape[0], w.shape[1]), BF16) for w in shards),
-        in_specs=in_place(len(shards)),
-        out_specs=tuple(in_place(len(shards))),
-        scratch_shapes=[item for shard in shards for item in share_scratch(shard)],
+        functools.partial(share_kernel, n, layer),
+        out_shape=tuple(full_shapes(shards)),
+        in_specs=in_place(4),
+        out_specs=tuple(in_place(2)),
+        scratch_shapes=[item for shape in shard_shapes(shards) for item in share_scratch(shape)],
         compiler_params=pltpu.CompilerParams(collective_id=cid, has_side_effects=True),
         name="share_weights",
     )(*shards)
 
 
-def finish_kernel(
-    n,
-    gains_ref,
-    kv_ref,
-    lo_ref,
-    ig_ref,
-    gain_ref,
-    key_ref,
-    value_ref,
-    lo_all_ref,
-    ig_all_ref,
-    gbuf,
-    kv_all_ref,
-    stage,
-    incoming,
-    lsem,
-    psem,
-    qsem,
-    rsem,
-    *sems,
-):
+def finish_line_kernel(n, *refs):
+    gains, rest = refs[:8], refs[8:]
+    kv_ref, gain_ref, key_ref, value_ref, gbuf, kv_all, stage, incoming, rsem, *sems = rest
     me = lax.axis_index("gx")
     gy = lax.axis_index("gy")
-    section = lax.axis_index("section")
-    other = 1 - section
-    gbuf[me] = gains_ref[...]
-    kv_all_ref[me] = kv_ref[...]
-    hello(n, me, gy, True, True)
+    kv_all[me] = kv_ref[...]
+    for k in range(2):
+        first = 0
+        for ref in gains[4 * k : 4 * k + 4]:
+            last = first + ref.shape[1]
+            gbuf[me, k : k + 1, first:last] = ref[...]
+            first = last
+    hello(n, me, gy, True)
     few = Line(n, None, lambda z: gbuf.at[z], None, sems[:4])
-    many = Line(n, None, lambda z: kv_all_ref.at[z], None, sems[4:8])
+    many = Line(n, None, lambda z: kv_all.at[z], None, sems[4:8])
+    few.gather_step(0)
     many.gather_step(0)
-    few.gather_step(0)
-    keeps = []
-    for k, (src, dst) in enumerate(((lo_ref, lo_all_ref), (ig_ref, ig_all_ref))):
-        keep = pltpu.make_async_copy(src.at[section], dst.at[section], lsem.at[k])
-        give = remote(src.at[other], dst.at[section], psem.at[k], qsem.at[k], section=other)
-        keep.start()
-        give.start()
-        keeps.append((keep, give))
     steps = [functools.partial(many.gather_step, k) for k in range(1, n)]
     for k in range(1, n):
         few.gather_step(k)
@@ -989,64 +1006,102 @@
     total = gbuf[0]
     for z in range(1, n):
         total = total + gbuf[z]
-    for k, where in enumerate(({"gy": gy_flip(gy, 1)}, {"gy": gy_flip(gy, 2)}, {"section": other})):
+    for k, where in enumerate(({"gy": gy_flip(gy, 1)}, {"gy": gy_flip(gy, 2)})):
         stage[k] = total
         swap = remote(stage.at[k], incoming.at[k], rsem.at[0, k], rsem.at[1, k], **where)
         swap.start()
-        if k and steps:
+        if steps:
             steps.pop(0)()
         swap.wait()
         total = total + incoming[k]
-
-    @pl.when(section == 0)
-    def _():
-        gain_ref[...] = total[0:1]
-
-    @pl.when(section == 1)
-    def _():
-        gain_ref[...] = total[1:2]
-
+    gain_ref[...] = total
     for step in steps:
         step()
     for z in range(n):
         cols = slice(z * HD, (z + 1) * HD)
-        key_ref[:, cols] = kv_all_ref[z, :, :HD].astype(F32)
-        value_ref[:, cols] = kv_all_ref[z, :, HD:].astype(F32)
-    for keep, give in keeps:
-        keep.wait()
-        give.wait()
+        key_ref[:, cols] = kv_all[z, :, :HD].astype(F32)
+        value_ref[:, cols] = kv_all[z, :, HD:].astype(F32)
     few.gather_drain()
     many.gather_drain()
 
 
-def finish(n, gains, kv, lo, ig, cid):
+def finish_line(n, gains, kv, cid):
     dma = pltpu.SemaphoreType.DMA
     shape = jax.ShapeDtypeStruct
+    width = sum(gain.shape[1] for gain in gains[:4])
     return pl.pallas_call(
-        functools.partial(finish_kernel, n),
+        functools.partial(finish_line_kernel, n),
         out_shape=(
-            shape((1, gains.shape[1]), F32),
+            shape((2, width), F32),
             shape((kv.shape[0], n * HD), F32),
             shape((kv.shape[0], n * HD), F32),
-            shape(lo.shape, BF16),
-            shape(ig.shape, BF16),
         ),
-        in_specs=in_vmem(4),
-        out_specs=tuple(in_vmem(5)),
+        in_specs=in_vmem(9),
+        out_specs=tuple(in_vmem(3)),
         scratch_shapes=[
-            pltpu.VMEM((n,) + gains.shape, F32),
+            pltpu.VMEM((n, 2, width), F32),
             pltpu.VMEM((n,) + kv.shape, BF16),
-            pltpu.VMEM((3,) + gains.shape, F32),
-            pltpu.VMEM((3,) + gains.shape, F32),
-            dma((2,)),
-            dma((2,)),
-            dma((2,)),
-            dma((2, 3)),
+            pltpu.VMEM((2, 2, width), F32),
+            pltpu.VMEM((2, 2, width), F32),
+            dma((2, 2)),
         ]
         + [dma((n,))] * 8,
         compiler_params=pltpu.CompilerParams(collective_id=cid, has_side_effects=True),
-        name="finish",
-    )(gains, kv, lo, ig)
+        name="finish_line",
+    )(*gains, kv)
+
+
+def finish_pair_kernel(*refs):
+    gain_ref, *rows = refs[:5]
+    out_rows, out_gains = refs[5:7], refs[7:11]
+    incoming, send, recv = refs[11:]
+    section = lax.axis_index("section")
+    other = 1 - section
+    barrier = pltpu.get_barrier_semaphore()
+    mesh_ids = pl.DeviceIdType.MESH
+    pl.semaphore_signal(barrier, 1, device_id={"section": other}, device_id_type=mesh_ids)
+    pl.semaphore_wait(barrier, 1)
+    swap = remote(gain_ref, incoming, send.at[2], recv.at[2], section=other)
+    swap.start()
+    for mine in range(2):
+
+        @pl.when(section == mine)
+        def _():
+            for k in range(2):
+                src, dst = rows[2 * k + 1 - mine], out_rows[k].at[mine]
+                remote(src, dst, send.at[k], recv.at[k], section=other).start()
+            for k in range(2):
+                out_rows[k][mine] = rows[2 * k + mine][...]
+
+    swap.wait()
+    for mine in range(2):
+
+        @pl.when(section == mine)
+        def _():
+            first = 0
+            for ref in out_gains:
+                last = first + ref.shape[1]
+                at = (slice(mine, mine + 1), slice(first, last))
+                ref[...] = gain_ref[at] + incoming[at]
+                first = last
+            for k in range(2):
+                src, dst = rows[2 * k + 1 - mine], out_rows[k].at[mine]
+                remote(src, dst, send.at[k], recv.at[k], section=other).wait()
+
+
+def finish_pair(gains, widths, lo, ig, cid):
+    dma = pltpu.SemaphoreType.DMA
+    shape = jax.ShapeDtypeStruct
+    both = shape((2,) + lo[0].shape, BF16)
+    return pl.pallas_call(
+        finish_pair_kernel,
+        out_shape=(both, both, *(shape((1, width), F32) for width in widths)),
+        in_specs=in_vmem(5),
+        out_specs=tuple(in_vmem(6)),
+        scratch_shapes=[pltpu.VMEM(gains.shape, F32), dma((3,)), dma((3,))],
+        compiler_params=pltpu.CompilerParams(collective_id=cid, has_side_effects=True),
+        name="finish_pair",
+    )(gains, *lo, *ig)
 
 
 class Reduce:
@@ -1275,10 +1330,10 @@
     wout_hbm,
     *rest,
 ):
-    count = 2 if layer == 0 else 0
-    shards, rest = rest[:count], rest[count:]
+    ahead = layer == 0
+    shards, rest = (rest[:4], rest[4:]) if ahead else ((), rest)
     mid_ref, pay_ref, normed_hbm, proj_hbm, qr_hbm, kr_ref, v_ref, prob_hbm, mixed_hbm = rest[:9]
-    fulls, rest = rest[9 : 9 + count], rest[9 + count :]
+    fulls, rest = (rest[9:11], rest[11:]) if ahead else ((), rest[9:])
     (
     win,
     wout,
@@ -1301,14 +1356,17 @@
     r = mb * t
     span = heads * HD
     me = lax.axis_index("gx")
-    shares = [
-        Share(1, shards[k], fulls[k], sems[8 + 4 * k : 12 + 4 * k]) for k in range(count)
-    ]
+    shares = []
+    if ahead:
+        shares = [
+            Share(1, pieces, fulls[k], sems[8 + 5 * k : 13 + 5 * k])
+            for k, pieces in enumerate(shard_pieces(*shards))
+        ]
     fetch_in = pltpu.make_async_copy(win_hbm, win, wsem.at[0])
     fetch_out = pltpu.make_async_copy(wout_hbm, wout, wsem.at[1])
     fetch_in.start()
     fetch_out.start()
-    hello(n, me, lax.axis_index("gy"), count > 0, count > 0)
+    hello(n, me, lax.axis_index("gy"), ahead, ahead)
     for share in shares:
         share.start()
     hidden = x_ref[...].astype(F32)
@@ -1343,11 +1401,16 @@
         rows = slice(first, first + length)
         if m + 1 < mb:
             waiting += [functools.partial(lines[m + 1].gather_step, k) for k in range(1, n)]
-        for j in range((span + 2 * HD) // 256):
-            cols = slice(j * 256, (j + 1) * 256)
+
+        def project(j, carry, m=m, rows=rows):
+            cols = pl.ds(pl.multiple_of(j * 256, 256), 256)
             proj[rows, cols] = jnp.dot(normed[m], win[:, cols], preferred_element_type=F32)
-            if j == 2:
-                tick()
+            return carry
+
+        blocks = (span + 2 * HD) // 256
+        lax.fori_loop(0, blocks // 2, project, 0)
+        tick()
+        lax.fori_loop(blocks // 2, blocks, project, 0)
         tick()
         key_unit, _ = unit_of(proj[rows, span : span + HD])
         key = key_unit * gain_key[...]
@@ -1362,7 +1425,7 @@
             qr[rows, at] = turned
             scores = dot32(turned, kr_ref[rows], COL_PAIR) * (1.0 / math.sqrt(HD))
             exponent = jnp.where(mask_ref[m] > 0.5, jnp.exp(scores), 0.0)
-            p = (exponent / jnp.sum(exponent, axis=-1, keepdims=True)).astype(BF16)
+            p = (exponent * (1.0 / jnp.sum(exponent, axis=-1, keepdims=True))).astype(BF16)
             prob[m * heads + h] = p
             mixed[rows, at] = jnp.dot(p, v_ref[rows], preferred_element_type=F32).astype(BF16)
             return carry
@@ -1372,9 +1435,10 @@
         lax.fori_loop(heads // 2, heads, head, 0, unroll=2)
         while waiting:
             tick()
-        if m == 0:
+        if m == mb - 1:
             for share in shares:
                 share.pass_on()
+        if m == 0:
             fetch_out.wait()
 
         def out_cols(j, carry, m=m, rows=rows):
@@ -1440,10 +1504,10 @@
             shape((total_rows, HD), BF16),
             shape((mb * heads, length, length), BF16),
             shape((total_rows, span), BF16),
-            *(shape((4 * w.shape[0], w.shape[1]), BF16) for w in shards),
+            *(full_shapes(shards) if shards else ()),
         ),
         in_specs=in_vmem(9) + in_place(2 + len(shards)),
-        out_specs=tuple(in_vmem(2) + in_place(3) + in_vmem(2) + in_place(2 + len(shards))),
+        out_specs=tuple(in_vmem(2) + in_place(3) + in_vmem(2) + in_place(4 if shards else 2)),
         scratch_shapes=[
             pltpu.VMEM((d, width), BF16),
             pltpu.VMEM((d, span), BF16),
@@ -1456,7 +1520,11 @@
         + line_buffers(mb, n, r, d)
         + [pltpu.SemaphoreType.DMA((2,)), pltpu.SemaphoreType.DMA((5,))]
         + [pltpu.SemaphoreType.DMA((mb, n))] * 8
-        + [item for shard in shards for item in share_scratch(shard)],
+        + [
+            item
+            for size in (shard_shapes(shards) if shards else ())
+            for item in share_scratch(size)
+        ],
         compiler_params=pltpu.CompilerParams(
             collective_id=cid, has_side_effects=True, vmem_limit_bytes=60 << 20
         ),
@@ -1538,14 +1606,18 @@
     if last:
         later, inbox, xin, yin, din = sems[8:13]
         block = d // 4
-        job_later = Reduce(
-            1, lambda c: later.at[pl.ds(c * block, block)], inbox, xin, yin, din, sems[13:17]
-        )
-        job = Reduce(
-            0, lambda c: grads.at[pl.ds(c * block, block)], inbox, xin, yin, din, sems[17:21]
-        )
+
+        def reduce(layer, terms, first, last, sems):
+            cols = slice(first, last)
+            buffers = [ref.at[..., cols] for ref in (inbox, xin, yin, din)]
+            return Reduce(layer, lambda c: terms.at[pl.ds(c * block, block), cols], *buffers, sems)
+
+        wide = span + 2 * HD
+        job_later = reduce(1, later, 0, wide + span, sems[13:17])
+        job = reduce(0, grads, 0, wide, sems[17:21])
+        job_out = reduce(0, grads, wide, wide + span, sems[21:25])
         swaps = [
-            remote(gives[k], outs[3 + k], sems[21].at[k], sems[22].at[k], section=1 - section)
+            remote(gives[k], outs[3 + k], sems[25].at[k], sems[26].at[k], section=1 - section)
             for k in range(3)
         ]
         load_later = pltpu.make_async_copy(later_hbm, later, osem.at[0])
@@ -1608,16 +1680,50 @@
     dvalue[...] = jnp.zeros_like(dvalue)
     dgain_query[...] = jnp.zeros_like(dgain_query)
     dgain_key[...] = jnp.zeros_like(dgain_key)
+    per = d // 4 // 256
+
+    def out_grads(at):
+        left = dmids[:, :, at].reshape(mb * length, 256)
+        grads[at, span + 2 * HD :] = dot32(left, mixed[...], ROW_PAIR).astype(BF16)
+
+    def in_grads(at):
+        left = normed[:, :, at].reshape(mb * length, 256)
+        grads[at, : span + 2 * HD] = dot32(left, dproj[...], ROW_PAIR).astype(BF16)
+
+    def chunked(compute, job):
+        def chunk(i, carry):
+            first = flip_by(gy, 3 - i // per) * (d // 4) + lax.rem(i, per) * 256
+            compute(pl.ds(pl.multiple_of(first, 256), 256))
+            for q in range(4):
+
+                @pl.when(i == per * (q + 1) - 1)
+                def _():
+                    if job is not None:
+
+                        @pl.when(jnp.logical_not(job.mine))
+                        def _():
+                            job.give(3 - q, job.part(job.cols[3 - q])).start()
+
+                    tick()
+
+            return carry
+
+        lax.fori_loop(0, 4 * per, chunk, 0)
+
     for m, line in enumerate(lines):
         first = m * length
         rows = slice(first, first + length)
         if m + 1 < mb:
             waiting += [functools.partial(lines[m + 1].gather_step, k) for k in range(1, n)]
-        for j in range(span // 256):
-            cols = slice(j * 256, (j + 1) * 256)
+
+        def to_heads(j, carry, m=m, rows=rows):
+            cols = pl.ds(pl.multiple_of(j * 256, 256), 256)
             dheads[rows, cols] = jnp.dot(
                 dmids[m], wout[:, cols], preferred_element_type=F32
             ).astype(BF16)
+            return carry
+
+        lax.fori_loop(0, span // 256, to_heads, 0)
         tick()
 
         def head(h, carry, m=m, rows=rows):
@@ -1663,34 +1769,20 @@
         lax.fori_loop(0, d // 256, in_cols, 0)
         line.scatter_tick(0)
         waiting += [functools.partial(line.scatter_tick, hop) for hop in range(1, n - 1)]
+        if m == 0 and last:
+            chunked(out_grads, job_out)
+            sums += [functools.partial(job_out.send_term, k) for k in (3, 2, 1, 0)]
+            sums += [job_out.pass_on]
     while sums:
         sums.pop(0)()
 
-    def weight_grads(c):
-        def chunk(i, carry):
-            at = pl.ds(pl.multiple_of(c * (d // 4) + i * 256, 256), 256)
-            left = normed[:, :, at].reshape(mb * length, 256)
-            grads[at, : span + 2 * HD] = dot32(left, dproj[...], ROW_PAIR).astype(BF16)
-            left = dmids[:, :, at].reshape(mb * length, 256)
-            grads[at, span + 2 * HD :] = dot32(left, mixed[...], ROW_PAIR).astype(BF16)
-            return carry
-
-        lax.fori_loop(0, d // 4 // 256, chunk, 0)
-
-    for bits in (3, 1, 2, 0):
-        c = gy_flip(gy, bits)
-        weight_grads(c)
-        if last:
-
-            @pl.when(jnp.logical_not(job.mine))
-            def _():
-                job.give(bits, job.part(c)).start()
-
-        tick()
+    if not last:
+        chunked(out_grads, None)
+    chunked(in_grads, job if last else None)
     while waiting:
         tick()
     if last:
-        for k in (3, 1, 2, 0):
+        for k in (3, 2, 1, 0):
             job.send_term(k)
     else:
         save = pltpu.make_async_copy(grads, outs[0], osem.at[0])
@@ -1708,9 +1800,10 @@
         save.wait()
         return
     job.pass_on()
-    closing = [(outs[0], 0, span), (outs[1], span, span + 2 * HD), (outs[2], span + 2 * HD, None)]
+    closing = [(outs[0], 0, span), (outs[1], span, wide), (outs[2], wide, wide + span)]
     job_later.close(closing)
-    job.close(closing)
+    job_out.close([(outs[2], 0, span)])
+    job.close(closing[:2])
     for swap in swaps:
         swap.wait()
 
@@ -1718,6 +1811,7 @@
     def _():
         for k in range(4):
             job.give(k, job.part(job.cols[k])).wait_send()
+            job_out.give(k, job_out.part(job_out.cols[k])).wait_send()
 
     @pl.when(jnp.logical_not(job_later.mine))
     def _():
@@ -1753,7 +1847,7 @@
             pltpu.VMEM((block, both), BF16),
             pltpu.VMEM((block, both), BF16),
             pltpu.VMEM((2, block // 2, both), BF16),
-        ] + reduce_sems() * 2 + [pltpu.SemaphoreType.DMA((3,))] * 2
+        ] + reduce_sems() * 3 + [pltpu.SemaphoreType.DMA((3,))] * 2
     return pl.pallas_call(
         functools.partial(attn_backward_kernel, n, layer, heads),
         out_shape=(
@@ -2148,14 +2242,9 @@
     rows_own = mb * local_rows
     rows_attn = mb * group_len
     section = lax.axis_index("section")
-    gx = lax.axis_index("gx")
     first = section * mb
 
-    kv_head = gx * heads // (HQ // KVH)
-    key_own = lax.dynamic_slice_in_dim(w_key[0], kv_head * HD, HD, 1)
-    value_own = lax.dynamic_slice_in_dim(w_value[0], kv_head * HD, HD, 1)
-    w_in_shard = jnp.concatenate([w_query[0], key_own, value_own], axis=1)
-    attn_shards = (w_in_shard, w_out[0])
+    attn_shards = (w_query, w_key, w_value, w_out)
     attn_all = [share_weights(0, n_gx, attn_shards, 9)]
     moe_own = (w_gate[0, 0], w_up[0, 0], w_down[0, 0])
     moe_other = tuple(swap_sections(w) for w in moe_own)
@@ -2260,29 +2349,24 @@
             mb,
         )
         in_grads[layer] = cot
-        gain_grads[layer] = jnp.concatenate([d_attn, d_ffn, d_query, d_key], axis=1)
+        gain_grads[layer] = [d_attn, d_ffn, d_query, d_key]
 
     query_grad, kv_shard, out_grad_w, *from_other = later
     grad_gate, grad_up, grad_down = (
         (moe_sums[k].astype(F32) + from_other[k].astype(F32))[None] for k in range(3)
     )
-    gain_sum, key_part, value_part, out_rows, grad_rows = finish(
-        n_gx,
-        jnp.concatenate(gain_grads[::1], axis=0),
-        kv_shard,
-        jnp.stack(outs),
-        jnp.stack(in_grads),
-        10,
+    gain_sum, key_part, value_part = finish_line(
+        n_gx, [grad for grads in gain_grads for grad in grads], kv_shard, 10
+    )
+    out_rows, grad_rows, *gain_sums = finish_pair(
+        gain_sum, [grad.shape[1] for grad in gain_grads[0]], outs, in_grads, 11
     )
     whole_rows = (1, micro_count, 1, local_rows, width)
 
     return (
         out_rows.reshape(whole_rows),
         grad_rows.reshape(whole_rows),
-        gain_sum[:, :width],
-        gain_sum[:, width : 2 * width],
-        gain_sum[:, 2 * width : 2 * width + HD],
-        gain_sum[:, 2 * width + HD :],
+        *gain_sums,
         query_grad[None],
         key_part[None],
         value_part[None],

time: 724 us -> 709 us (0.979)
    pallas_call x2 -> x3, Pallas kernels: 76.1 us -> 75.4 us  [the longest x1 48.4 us: share_weights(): pl.pallas_call(functools.partial(share_kernel, n, layer), out_shape=tuple...]
where the time goes in v4:
time: 709 us; the launch traced here: 708 us
  Pallas kernels  671 us (95%)
  other arithmetic  18.2 us (3%)
  local copies, waits for them, and re-layouts  17.1 us (2%)
    pallas_call x2, Pallas kernels, moe_forward(): pl.pallas_call(functools.partial(moe_forward_kernel, n, layer), out_shape...  181 us
    pallas_call x2, Pallas kernels, moe_backward(): pl.pallas_call(functools.partial(moe_backward_kernel, n, layer), out_shap...  162 us
    pallas_call x2, Pallas kernels, attn_backward(): pl.pallas_call(functools.partial(attn_backward_kernel, n, layer, heads),...  145 us
    pallas_call x2, Pallas kernels, attn_forward(): pl.pallas_call(functools.partial(attn_forward_kernel, n, layer, heads), o...  107 us
    pallas_call x1, Pallas kernels, share_weights(): pl.pallas_call(functools.partial(share_kernel, n, layer), out_shape=tuple...  48.4 us
    pallas_call x1, Pallas kernels, finish_line(): pl.pallas_call(functools.partial(finish_line_kernel, n), out_shape=(shape...  22.7 us
  transfers between devices with their start and end apart: 4, of which 0 were waited for; matrix products, arithmetic and copies ran while one was open for 1% of the time, Pallas kernels for 15%

profile of v4, /device:TPU:0, one launch (start us, length us, event | category | flops | bytes accessed | tf_op | source)
XLA Modules:
  0.0 708.0 jit_solution(5742997024761070652)
XLA Ops:
  0.7 0.8 select_reduce_fusion
  1.4 0.1 copy.43
  1.5 0.1 reshape.100
  1.6 0.7 constant_dynamic-update-slice_fusion.3
  2.3 0.7 constant_dynamic-update-slice_fusion.2
  3.0 0.7 constant_dynamic-update-slice_fusion.1
  3.7 0.7 constant_dynamic-update-slice_fusion
  4.3 0.5 collective-permute-start
  4.8 0.0 collective-permute-start.1
  4.9 0.5 collective-permute-start.2
  5.4 0.2 convert_reduce_fusion
  5.6 0.8 fusion.mask_ref
  6.4 0.5 fusion.1
  6.9 1.9 constant_dynamic-slice_fusion.3
  8.8 0.8 pad_maximum_fusion
  9.6 0.1 pad.5.clone
  9.7 48.4 %share_weights.1 = (bf16[2048,1280]{1,0:T(8,128)(2,1)}, bf16[2048,1024]{1,0:T(8,128)(2,1)}) custom-call(bf16[1,512,1024]{2,1,0:T(8,128)(2,1)} %rest_0_.1, bf16[1,512,512]{2,1,0:T(8,128)(2,1)} %rest_1_.1, bf16[1,512,512]{2,1,0:T(8,128)(2,1)} %rest_2_.1, bf16[1,512,1024]{2,1,0:T(8,128)(2,1)} %rest_3_.1), custom_call_target="tpu_custom_call" | custom-call | tf_op jit(solution)/shard_map/share_weights/pallas_call | solution.py:973
  58.3 0.1 reshape.101
  58.4 0.5 fusion.6
  58.9 0.7 maximum_maximum_fusion.1
  59.6 0.6 fusion.7
  60.2 58.7 %attn_forward.2 = (f32[64,2048]{1,0:T(8,128)}, bf16[64,2176]{1,0:T(8,128)(2,1)}, bf16[2,128,2048]{2,1,0:T(8,128)(2,1)}, f32[256,1280]{1,0:T(8,128)}, bf16[256,10...) custom-call(bf16[64,2048]{1,0:T(8,128)(2,1)} %bitcast.59, ...), custom_call_target="tpu_custom_call" | custom-call | tf_op jit(solution)/shard_map/attn_forward/pallas_call | solution.py:1495
  119.0 0.6 fusion.4
  119.6 0.6 fusion.5
  120.2 96.9 %moe_forward.2 = (bf16[64,2048]{1,0:T(8,128)(2,1)}, bf16[1024,2048]{1,0:T(8,128)(2,1)}, f32[1024,1]{1,0:T(8,128)}, bf16[1024,768]{1,0:T(8,128)(2,1)}, bf16[1024,...) custom-call(f32[64,2048]{1,0:T(8,128)} %get-tuple-element.89.mid_ref, bf16[64,2176]{1,0:T(8,128)(2,1)} %get-tuple-element.90.pay_ref, ...), custom_call_target="tpu_custom_call" | custom-call | tf_op jit(solution)/shard_map/moe_forward/pallas_call | solution.py:580
  217.1 48.6 %attn_forward.3 = (f32[64,2048]{1,0:T(8,128)}, bf16[64,2176]{1,0:T(8,128)(2,1)}, bf16[2,128,2048]{2,1,0:T(8,128)(2,1)}, f32[256,1280]{1,0:T(8,128)}, bf16[256,10...) custom-call(bf16[64,2048]{1,0:T(8,128)(2,1)} %get-tuple-element.91.x, ...), custom_call_target="tpu_custom_call" | custom-call | tf_op jit(solution)/shard_map/attn_forward/pallas_call | solution.py:1495
  265.7 84.4 %moe_forward.3 = (bf16[64,2048]{1,0:T(8,128)(2,1)}, bf16[1024,2048]{1,0:T(8,128)(2,1)}, f32[1024,1]{1,0:T(8,128)}, bf16[1024,768]{1,0:T(8,128)(2,1)}, bf16[1024,...) custom-call(f32[64,2048]{1,0:T(8,128)} %get-tuple-element.94.mid_ref, bf16[64,2176]{1,0:T(8,128)(2,1)} %get-tuple-element.95.pay_ref, ...), custom_call_target="tpu_custom_call" | custom-call | tf_op jit(solution)/shard_map/moe_forward/pallas_call | solution.py:580
  350.1 80.1 %moe_backward.2 = (f32[64,2048]{1,0:T(8,128)}, f32[1,2048]{1,0:T(1,128)}, bf16[2048,768]{1,0:T(8,128)(2,1)}, bf16[2048,768]{1,0:T(8,128)(2,1)}, bf16[768,2048]{1...) custom-call(bf16[64,2048]{1,0:T(8,128)(2,1)} %bitcast.63, ...), custom_call_target="tpu_custom_call" | custom-call | tf_op jit(solution)/shard_map/moe_backward/pallas_call | solution.py:802
  430.2 47.7 %attn_backward.2 = (bf16[64,2048]{1,0:T(8,128)(2,1)}, f32[1,2048]{1,0:T(1,128)}, f32[1,128]{1,0:T(1,128)}, f32[1,128]{1,0:T(1,128)}, bf16[2048,2304]{1,0:T(8,128)(2,1)}) custom-call(f32[64,2048]{1,0:T(8,128)} %get-tuple-element.101.dmid_ref, bf16[64,2048]{1,0:T(8,128)(2,1)} %get-tuple-element.91.x_ref.refs_1_, f32[1,2048]{1,0:T(1,128)} %get-tuple-element.211.gain_attn, ...), custom_call_target="tpu_custom_call" | custom-call | tf_op jit(solution)/shard_map/attn_backward/pallas_call | solution.py:1851
  477.9 81.7 %moe_backward.3 = (f32[64,2048]{1,0:T(8,128)}, f32[1,2048]{1,0:T(1,128)}, bf16[2048,768]{1,0:T(8,128)(2,1)}, bf16[2048,768]{1,0:T(8,128)(2,1)}, bf16[768,2048]{1...) custom-call(bf16[64,2048]{1,0:T(8,128)(2,1)} %get-tuple-element.109., ...), custom_call_target="tpu_custom_call", output_to_operand_aliasing={{2}: (14, {}), {3}: (15, {}), {4}: (16, {}), {5}: (17, {}),... | custom-call | tf_op jit(solution)/shard_map/moe_backward/pallas_call | solution.py:802
  559.6 97.2 %attn_backward.3 = (bf16[64,2048]{1,0:T(8,128)(2,1)}, f32[1,2048]{1,0:T(1,128)}, f32[1,128]{1,0:T(1,128)}, f32[1,128]{1,0:T(1,128)}, f32[512,1024]{1,0:T(8,128)}...) custom-call(f32[64,2048]{1,0:T(8,128)} %get-tuple-element.121.dmid_r, ...), custom_call_target="tpu_custom_call" | custom-call | tf_op jit(solution)/shard_map/attn_backward/pallas_call | solution.py:1851
  656.8 22.7 %finish_line.1 = (f32[2,4352]{1,0:T(2,128)}, f32[512,512]{1,0:T(8,128)}, f32[512,512]{1,0:T(8,128)}) custom-call(f32[1,2048]{1,0:T(1,128)} %get-tuple-element.133.refs_0_, f32[1,2048]{1,0:T(1,128)} %get-tuple-element.134.refs_1_, f32[1,128]{1,0:T(1,128)} %get-tuple-element.135.refs_2_, f32[1,128]{1,0:T(1,128)} %get-tuple-element.136.refs_3_, ...), custom_call_target="tpu_custom_call" | custom-call | tf_op jit(solution)/shard_map/finish_line/pallas_call | solution.py:1032
  679.5 4.3 finish_pair.1
  683.8 6.4 add_bitcast_fusion.2
  690.2 3.9 add_bitcast_fusion.1
  694.1 1.2 copy-done.4
  695.3 4.0 add_bitcast_fusion
  699.4 0.8 copy.66
  700.2 0.8 copy.67
  701.0 0.6 copy.68
  701.6 0.6 copy.69
  702.2 0.5 copy.70
  702.7 0.5 copy.71
  703.2 1.3 copy.72
  704.5 1.0 copy.73
  705.5 1.0 copy.74
  706.5 0.1 copy-done.6
  706.6 1.3 copy.75
  (47 shorter events, 0.2 us)
Async XLA Ops:
  0.6 4.8 copy-start
  4.3 53.8 %collective-permute-start = (f32[6400]{0:T(1024)S(1)}, f32[6400]{0:T(1024)S(1)}, u32[]{:S(2)}, u32[]{:S(2)}) collective-permute-start(f32[6400]{0:T(1024)S(1)} %constant_dynamic-update-slice_fusion), channel_id=1, source_target_pairs={{0,16},{16,0},{1,17},{17,1},{2,18},{18,2},{3,19},{19,3},{4,20},{20... | collective-permute-start | bytes 76808 | tf_op jit(solution)/shard_map/ppermute | solution.py:92
  4.8 115.3 %collective-permute-start.1 = (bf16[2048,768]{1,0:T(8,128)(2,1)}, bf16[2048,768]{1,0:T(8,128)(2,1)}, u32[]{:S(2)}, u32[]{:S(2)}) collective-permute-start(bf16[2048,768]{1,0:T(8,128)(2,1)} %bitcast.44), channel_id=1, source_target_pairs={{0,16},{16,0},{1,17},{17,1},{2,18},{18,2},{3,19},{19,3},{4,20},{20... | collective-permute-start | bytes 9437192 | tf_op jit(solution)/shard_map/ppermute | solution.py:92
  4.9 115.3 %collective-permute-start.2 = (bf16[2048,768]{1,0:T(8,128)(2,1)}, bf16[2048,768]{1,0:T(8,128)(2,1)}, u32[]{:S(2)}, u32[]{:S(2)}) collective-permute-start(bf16[2048,768]{1,0:T(8,128)(2,1)} %bitcast.49), channel_id=1, source_target_pairs={{0,16},{16,0},{1,17},{17,1},{2,18},{18,2},{3,19},{19,3},{4,20},{20... | collective-permute-start | bytes 9437192 | tf_op jit(solution)/shard_map/ppermute | solution.py:92
  5.4 114.8 %collective-permute-start.3 = (bf16[768,2048]{1,0:T(8,128)(2,1)}, bf16[768,2048]{1,0:T(8,128)(2,1)}, u32[]{:S(2)}, u32[]{:S(2)}) collective-permute-start(bf16[768,2048]{1,0:T(8,128)(2,1)} %bitcast.54), channel_id=1, source_target_pairs={{0,16},{16,0},{1,17},{17,1},{2,18},{18,2},{3,19},{19,3},{4,20},{20... | collective-permute-start | bytes 9437192 | tf_op jit(solution)/shard_map/ppermute | solution.py:92
  683.8 6.4 copy-start.2
  683.8 6.4 copy-start.5
  690.2 3.9 copy-start.3
  690.2 5.1 copy-start.4
  695.3 4.1 copy-start.11
  695.3 4.9 copy-start.10
  695.3 5.7 copy-start.13
  695.3 6.3 copy-start.12
  695.3 6.9 copy-start.15
  695.3 7.4 %copy-start.14 = (f32[1,128]{1,0:T(1,128)S(1)}, f32[1,128]{1,0:T(1,128)}, u32[]{:S(2)}) copy-start(f32[1,128]{1,0:T(1,128)} %get-tuple-element.245) | copy-start | bytes 1540
  699.4 3.8 copy-start.7
  699.4 5.1 copy-start.9
  703.2 2.3 copy-start.8
  704.5 2.1 copy-start.6
  704.5 3.4 copy-start.1

commit v5 on v4

--- a/solution.py
+++ b/solution.py
@@ -314,9 +314,11 @@
 
     def scatter_near(self, side):
         def send(z, k):
-            @pl.when(lax.rem(z, 2) == side)
-            def _():
-                self.near(side, z).start()
+            if abs(k) > 1:
+
+                @pl.when(lax.rem(z, 2) == side)
+                def _():
+                    self.near(side, z).start()
 
         self.each(send)
 
@@ -329,6 +331,8 @@
         mine = self.part(z, self.column_of(side))
         add_rows(mine, mine, self.din.at[z])
         self.near(side, z).start()
+        if abs(k) < 2:
+            self.near(1 - side, z).start()
 
     def along(self, z, up):
         send, recv = self.scatter_sems[:2] if up else self.scatter_sems[2:4]
@@ -952,33 +956,48 @@
     return [jax.ShapeDtypeStruct((4 * rows, cols), BF16) for rows, cols in shard_shapes(shards)]
 
 
-def share_kernel(n, layer, *refs):
-    fulls, scratch = refs[4:6], refs[6:]
+def share_kernel(n, layer, few, *refs):
+    shards, smalls = refs[:4], refs[4 : 4 + few]
+    fulls, others = refs[4 + few : 6 + few], refs[6 + few : 6 + 2 * few]
+    send, recv, *scratch = refs[6 + 2 * few :]
+    other = 1 - lax.axis_index("section")
+    swaps = [
+        remote(smalls[k], others[k], send.at[k], recv.at[k], section=other) for k in range(few)
+    ]
     shares = [
         Share(layer, pieces, fulls[k], scratch[5 * k : 5 * k + 5])
-        for k, pieces in enumerate(shard_pieces(*refs[:4]))
+        for k, pieces in enumerate(shard_pieces(*shards))
     ]
     hello(n, lax.axis_index("gx"), lax.axis_index("gy"), True, True)
     for share in shares:
         share.start()
+    for swap in swaps:
+        swap.start()
     for share in shares:
         share.pass_on()
     for share in shares:
         share.finish()
     for share in shares:
         share.drain()
-
-
-def share_weights(layer, n, shards, cid):
+    for swap in swaps:
+        swap.wait()
+
+
+def share_weights(layer, n, shards, smalls, cid):
+    few = len(smalls)
     return pl.pallas_call(
-        functools.partial(share_kernel, n, layer),
-        out_shape=tuple(full_shapes(shards)),
-        in_specs=in_place(4),
-        out_specs=tuple(in_place(2)),
-        scratch_shapes=[item for shape in shard_shapes(shards) for item in share_scratch(shape)],
+        functools.partial(share_kernel, n, layer, few),
+        out_shape=(
+            *full_shapes(shards),
+            *(jax.ShapeDtypeStruct(small.shape, small.dtype) for small in smalls),
+        ),
+        in_specs=in_place(4 + few),
+        out_specs=tuple(in_place(2 + few)),
+        scratch_shapes=[pltpu.SemaphoreType.DMA((few,))] * 2
+        + [item for shape in shard_shapes(shards) for item in share_scratch(shape)],
         compiler_params=pltpu.CompilerParams(collective_id=cid, has_side_effects=True),
         name="share_weights",
-    )(*shards)
+    )(*shards, *smalls)
 
 
 def finish_line_kernel(n, *refs):
@@ -1658,20 +1677,22 @@
         if sums:
             sums.pop(0)()
 
+    if last:
+        sums += [functools.partial(job_later.send_term, k) for k in (3, 1, 2, 0)]
+        sums += [job_later.pass_on]
     for k in range(n):
         lines[0].gather_step(k)
         if k == min(1, n - 1):
             for line in lines[1:]:
                 line.gather_step(0)
-    if last:
-
-        @pl.when(job_later.mine)
-        def _():
-            load_later.wait()
-
-        sums += [functools.partial(job_later.send_term, k) for k in (3, 1, 2, 0)]
-        sums += [job_later.pass_on]
-    tick()
+        if k == 0 and last:
+
+            @pl.when(job_later.mine)
+            def _():
+                load_later.wait()
+
+        if k < n - 1:
+            tick()
     fetch_out.wait()
     for load in loads:
         load.wait()
@@ -1757,7 +1778,7 @@
         if m == 0:
             fetch_in.wait()
         while waiting:
-            tick()
+            waiting.pop(0)()
 
         def in_cols(j, carry, m=m, rows=rows):
             at = pl.ds(pl.multiple_of(j * 256, 256), 256)
@@ -1773,13 +1794,11 @@
             chunked(out_grads, job_out)
             sums += [functools.partial(job_out.send_term, k) for k in (3, 2, 1, 0)]
             sums += [job_out.pass_on]
-    while sums:
-        sums.pop(0)()
 
     if not last:
         chunked(out_grads, None)
     chunked(in_grads, job if last else None)
-    while waiting:
+    while waiting or sums:
         tick()
     if last:
         for k in (3, 2, 1, 0):
@@ -2245,24 +2264,21 @@
     first = section * mb
 
     attn_shards = (w_query, w_key, w_value, w_out)
-    attn_all = [share_weights(0, n_gx, attn_shards, 9)]
+    table = dense_gates(routes[0, :, 0], gates[0, :, 0], experts)
+    smalls = (table, gain_attn, gain_ffn, gain_query, gain_key)
+    full_in, full_out, *others = share_weights(0, n_gx, attn_shards, smalls, 9)
+    attn_all = [(full_in, full_out)]
+    is_first = section == 0
+    by_layer = [
+        (jnp.where(is_first, own, other), jnp.where(is_first, other, own))
+        for own, other in zip(smalls, others)
+    ]
     moe_own = (w_gate[0, 0], w_up[0, 0], w_down[0, 0])
     moe_other = tuple(swap_sections(w) for w in moe_own)
-    table = dense_gates(routes[0, :, 0], gates[0, :, 0], experts)
-    small = jnp.concatenate(
-        [table.reshape(-1), gain_attn[0], gain_ffn[0], gain_query[0], gain_key[0]]
-    )
-    small_other = swap_sections(small)
-    is_first = section == 0
-    small_all = jnp.stack(
-        [jnp.where(is_first, small, small_other), jnp.where(is_first, small_other, small)]
-    )
-    table_size = micro_count * local_rows * experts
-    table_all = small_all[:, :table_size].reshape(n_sec, micro_count, local_rows, experts)
-    gains_all = small_all[:, table_size:]
-    table_mine = lax.dynamic_slice_in_dim(table_all, first, mb, 1).reshape(
-        n_sec, rows_own, experts
-    )
+    table_mine = [
+        lax.dynamic_slice_in_dim(part, first, mb, 0).reshape(rows_own, experts)
+        for part in by_layer[0]
+    ]
     x_mine = lax.dynamic_slice_in_dim(inputs[:, 0], first, mb, 0).reshape(rows_own, width)
     cot = lax.dynamic_slice_in_dim(out_grad[:, 0], first, mb, 0).reshape(rows_own, width)
     segs = lax.dynamic_slice_in_dim(segments[:, 0], first, mb, 0)
@@ -2274,13 +2290,7 @@
     )
 
     def split_gains(layer):
-        g = gains_all[layer : layer + 1]
-        return (
-            g[:, :width],
-            g[:, width : 2 * width],
-            g[:, 2 * width : 2 * width + HD],
-            g[:, 2 * width + HD :],
-        )
+        return tuple(pair[layer] for pair in by_layer[1:])
 
     kept = []
     outs = []

time: 709 us -> 683 us (0.963)
  Pallas kernels: 671 us -> 647 us
    pallas_call x2, Pallas kernels: 181 us -> 172 us  [moe_forward(): pl.pallas_call(functools.partial(moe_forward_kernel, n, layer), out_shape...]
  transfers between devices with their start and end apart: 4 -> 3, of which waited for: 0 -> 0; matrix products, arithmetic and copies ran while one was open for 1% -> 1% of each run, Pallas kernels for 15% -> 16%
where the time goes in v5:
time: 683 us; the launch traced here: 682 us
  Pallas kernels  647 us (95%)
  other arithmetic  21.5 us (3%)
  local copies, waits for them, and re-layouts  11.5 us (2%)
    pallas_call x2, Pallas kernels, moe_forward(): pl.pallas_call(functools.partial(moe_forward_kernel, n, layer), out_shape...  172 us
    pallas_call x2, Pallas kernels, moe_backward(): pl.pallas_call(functools.partial(moe_backward_kernel, n, layer), out_shap...  155 us
    pallas_call x2, Pallas kernels, attn_backward(): pl.pallas_call(functools.partial(attn_backward_kernel, n, layer, heads),...  140 us
    pallas_call x2, Pallas kernels, attn_forward(): pl.pallas_call(functools.partial(attn_forward_kernel, n, layer, heads), o...  107 us
    pallas_call x1, Pallas kernels, share_weights(): pl.pallas_call(functools.partial(share_kernel, n, layer, few), out_shape=...  48.1 us
    pallas_call x1, Pallas kernels, finish_line(): pl.pallas_call(functools.partial(finish_line_kernel, n), out_shape=(shape...  21.1 us
  transfers between devices with their start and end apart: 3, of which 0 were waited for; matrix products, arithmetic and copies ran while one was open for 1% of the time, Pallas kernels for 16%

profile of v5, /device:TPU:0, one launch (start us, length us, event | category | flops | bytes accessed | tf_op | source)
XLA Modules:
  0.0 681.9 jit_solution(9762390310374305140)
XLA Ops:
  0.6 0.0 copy-start
  0.7 0.0 copy-start.20
  0.7 0.0 copy-start.19
  0.7 0.0 copy-start.16
  0.7 0.0 copy-start.15
  0.7 0.6 collective-permute-start
  1.3 0.1 collective-permute-start.1
  1.4 0.4 collective-permute-start.2
  1.8 0.8 select_reduce_fusion
  2.6 0.7 copy.39.refs_4_
  3.3 0.1 pad.5.clone
  3.4 48.1 %share_weights.1 = (bf16[2048,1280]{1,0:T(8,128)(2,1)}, bf16[2048,1024]{1,0:T(8,128)(2,1)}, f32[4,32,16]{2,1,0:T(8,128)}, f32[1,2048]{1,0:T(1,128)}, f32[1,2048]...) custom-call(bf16[1,512,1024]{2,1,0:T(8,128)(2,1)} %rest_0_.1, bf16[1,512,512]{2,1,0:T(8,128)(2,1)} %rest_1_.1, ...), custom_call_target="tpu_custom_call" | custom-call | tf_op jit(solution)/shard_map/share_weights/pallas_call | solution.py:988
  51.6 0.8 dynamic-slice_select_fusion
  52.3 0.2 convert_reduce_fusion
  52.5 0.5 fusion.1
  53.1 0.8 pad_maximum_fusion
  53.9 1.2 broadcast_select_fusion.4
  55.1 0.7 maximum_maximum_fusion.1
  55.8 0.8 fusion.mask_ref
  56.6 0.8 constant_dynamic-slice_fusion.1
  57.4 1.3 broadcast_select_fusion
  58.8 58.8 %attn_forward.2 = (f32[64,2048]{1,0:T(8,128)}, bf16[64,2176]{1,0:T(8,128)(2,1)}, bf16[2,128,2048]{2,1,0:T(8,128)(2,1)}, f32[256,1280]{1,0:T(8,128)}, bf16[256,10...) custom-call(bf16[64,2048]{1,0:T(8,128)(2,1)} %bitcast.53, ...), custom_call_target="tpu_custom_call" | custom-call | tf_op jit(solution)/shard_map/attn_forward/pallas_call | solution.py:1514
  117.6 0.0 collective-permute-done.wg_other
  117.6 0.0 collective-permute-done.1.wu_other
  117.6 91.2 %moe_forward.2 = (bf16[64,2048]{1,0:T(8,128)(2,1)}, bf16[1024,2048]{1,0:T(8,128)(2,1)}, f32[1024,1]{1,0:T(8,128)}, bf16[1024,768]{1,0:T(8,128)(2,1)}, bf16[1024,...) custom-call(f32[64,2048]{1,0:T(8,128)} %get-tuple-element.99.mid_ref, bf16[64,2176]{1,0:T(8,128)(2,1)} %get-tuple-element.100.pay_ref, ...), custom_call_target="tpu_custom_call" | custom-call | tf_op jit(solution)/shard_map/moe_forward/pallas_call | solution.py:584
  208.9 47.8 %attn_forward.3 = (f32[64,2048]{1,0:T(8,128)}, bf16[64,2176]{1,0:T(8,128)(2,1)}, bf16[2,128,2048]{2,1,0:T(8,128)(2,1)}, f32[256,1280]{1,0:T(8,128)}, bf16[256,10...) custom-call(bf16[64,2048]{1,0:T(8,128)(2,1)} %get-tuple-element.101., ...), custom_call_target="tpu_custom_call" | custom-call | tf_op jit(solution)/shard_map/attn_forward/pallas_call | solution.py:1514
  256.7 80.4 %moe_forward.3 = (bf16[64,2048]{1,0:T(8,128)(2,1)}, bf16[1024,2048]{1,0:T(8,128)(2,1)}, f32[1024,1]{1,0:T(8,128)}, bf16[1024,768]{1,0:T(8,128)(2,1)}, bf16[1024,...) custom-call(f32[64,2048]{1,0:T(8,128)} %get-tuple-element.104.mid_ref, bf16[64,2176]{1,0:T(8,128)(2,1)} %get-tuple-element.105.pay_ref, ...), custom_call_target="tpu_custom_call" | custom-call | tf_op jit(solution)/shard_map/moe_forward/pallas_call | solution.py:584
  337.1 76.4 %moe_backward.2 = (f32[64,2048]{1,0:T(8,128)}, f32[1,2048]{1,0:T(1,128)}, bf16[2048,768]{1,0:T(8,128)(2,1)}, bf16[2048,768]{1,0:T(8,128)(2,1)}, bf16[768,2048]{1...) custom-call(bf16[64,2048]{1,0:T(8,128)(2,1)} %bitcast.57, ...), custom_call_target="tpu_custom_call" | custom-call | tf_op jit(solution)/shard_map/moe_backward/pallas_call | solution.py:806
  413.5 49.3 %attn_backward.2 = (bf16[64,2048]{1,0:T(8,128)(2,1)}, f32[1,2048]{1,0:T(1,128)}, f32[1,128]{1,0:T(1,128)}, f32[1,128]{1,0:T(1,128)}, bf16[2048,2304]{1,0:T(8,128)(2,1)}) custom-call(f32[64,2048]{1,0:T(8,128)} %get-tuple-element.111.dmid_ref, bf16[64,2048]{1,0:T(8,128)(2,1)} %get-tuple-element.101.x_ref.refs_1_, f32[1,2048]{1,0:T(1,128)} %get-tuple-element.219.gain_attn, ...), custom_call_target="tpu_custom_call" | custom-call | tf_op jit(solution)/shard_map/attn_backward/pallas_call | solution.py:1870
  462.9 78.3 %moe_backward.3 = (f32[64,2048]{1,0:T(8,128)}, f32[1,2048]{1,0:T(1,128)}, bf16[2048,768]{1,0:T(8,128)(2,1)}, bf16[2048,768]{1,0:T(8,128)(2,1)}, bf16[768,2048]{1...) custom-call(bf16[64,2048]{1,0:T(8,128)(2,1)} %get-tuple-element.119., ...), custom_call_target="tpu_custom_call", output_to_operand_aliasing={{2}: (14, {}), {3}: (15, {}), {4}: (16, {}), {5}: (17, {}),... | custom-call | tf_op jit(solution)/shard_map/moe_backward/pallas_call | solution.py:806
  541.2 91.1 %attn_backward.3 = (bf16[64,2048]{1,0:T(8,128)(2,1)}, f32[1,2048]{1,0:T(1,128)}, f32[1,128]{1,0:T(1,128)}, f32[1,128]{1,0:T(1,128)}, f32[512,1024]{1,0:T(8,128)}...) custom-call(f32[64,2048]{1,0:T(8,128)} %get-tuple-element.131.dmid_r, ...), custom_call_target="tpu_custom_call" | custom-call | tf_op jit(solution)/shard_map/attn_backward/pallas_call | solution.py:1870
  632.4 21.1 %finish_line.1 = (f32[2,4352]{1,0:T(2,128)}, f32[512,512]{1,0:T(8,128)}, f32[512,512]{1,0:T(8,128)}) custom-call(f32[1,2048]{1,0:T(1,128)} %get-tuple-element.143.refs_0_, f32[1,2048]{1,0:T(1,128)} %get-tuple-element.144.refs_1_, f32[1,128]{1,0:T(1,128)} %get-tuple-element.145.refs_2_, f32[1,128]{1,0:T(1,128)} %get-tuple-element.146.refs_3_, ...), custom_call_target="tpu_custom_call" | custom-call | tf_op jit(solution)/shard_map/finish_line/pallas_call | solution.py:1051
  653.5 4.2 finish_pair.1
  657.8 6.4 add_bitcast_fusion.2
  664.2 3.9 add_bitcast_fusion.1
  668.1 1.2 copy-done.4
  669.3 4.0 add_bitcast_fusion
  673.3 0.8 copy.60
  674.1 0.8 copy.61
  674.9 0.6 copy.62
  675.5 0.6 copy.63
  676.1 0.5 copy.64
  676.7 0.5 copy.65
  677.2 1.3 copy.66
  678.5 1.0 copy.67
  679.5 1.0 copy.68
  680.4 0.1 copy-done.6
  680.6 1.3 copy.69
  (46 shorter events, 0.1 us)
Async XLA Ops:
  0.6 50.9 %copy-start = (s32[4,1,128]{2,1,0:T(1,128)S(1)}, s32[4,1,128]{2,1,0:T(1,128)}, u32[]{:S(2)}) copy-start(s32[4,1,128]{2,1,0:T(1,128)} %param.18) | copy-start | bytes 6148
  0.7 53.3 %copy-start.20 = (f32[1,128]{1,0:T(1,128)S(1)}, f32[1,128]{1,0:T(1,128)}, u32[]{:S(2)}) copy-start(f32[1,128]{1,0:T(1,128)} %refs_8_.1) | copy-start | bytes 1540
  0.7 53.3 %copy-start.19 = (f32[1,128]{1,0:T(1,128)S(1)}, f32[1,128]{1,0:T(1,128)}, u32[]{:S(2)}) copy-start(f32[1,128]{1,0:T(1,128)} %refs_7_.1) | copy-start | bytes 1540
  0.7 56.7 %copy-start.16 = (f32[1,2048]{1,0:T(1,128)S(1)}, f32[1,2048]{1,0:T(1,128)}, u32[]{:S(2)}) copy-start(f32[1,2048]{1,0:T(1,128)} %refs_6_.1) | copy-start | bytes 24580
  0.7 56.7 %copy-start.15 = (f32[1,2048]{1,0:T(1,128)S(1)}, f32[1,2048]{1,0:T(1,128)}, u32[]{:S(2)}) copy-start(f32[1,2048]{1,0:T(1,128)} %refs_5_.1) | copy-start | bytes 24580
  0.7 55.9 %copy-start.14 = (bf16[4,1,32,2048]{3,2,1,0:T(8,128)(2,1)S(1)}, bf16[4,1,32,2048]{3,2,1,0:T(8,128)(2,1)}, u32[]{:S(2)}) copy-start(bf16[4,1,32,2048]{3,2,1,0:T(8,128)(2,1)} %param.17) | copy-start | bytes 1572868
  0.7 55.9 %copy-start.13 = (bf16[4,1,32,2048]{3,2,1,0:T(8,128)(2,1)S(1)}, bf16[4,1,32,2048]{3,2,1,0:T(8,128)(2,1)}, u32[]{:S(2)}) copy-start(bf16[4,1,32,2048]{3,2,1,0:T(8,128)(2,1)} %param.16) | copy-start | bytes 1572868
  0.7 116.9 %collective-permute-start = (bf16[2048,768]{1,0:T(8,128)(2,1)}, bf16[2048,768]{1,0:T(8,128)(2,1)}, u32[]{:S(2)}, u32[]{:S(2)}) collective-permute-start(bf16[2048,768]{1,0:T(8,128)(2,1)} %bitcast.38), channel_id=1, source_target_pairs={{0,16},{16,0},{1,17},{17,1},{2,18},{18,2},{3,19},{19,3},{4,20},{20... | collective-permute-start | bytes 9437192 | tf_op jit(solution)/shard_map/ppermute | solution.py:92
  1.3 116.3 %collective-permute-start.1 = (bf16[2048,768]{1,0:T(8,128)(2,1)}, bf16[2048,768]{1,0:T(8,128)(2,1)}, u32[]{:S(2)}, u32[]{:S(2)}) collective-permute-start(bf16[2048,768]{1,0:T(8,128)(2,1)} %bitcast.43), channel_id=1, source_target_pairs={{0,16},{16,0},{1,17},{17,1},{2,18},{18,2},{3,19},{19,3},{4,20},{20... | collective-permute-start | bytes 9437192 | tf_op jit(solution)/shard_map/ppermute | solution.py:92
  1.4 116.3 %collective-permute-start.2 = (bf16[768,2048]{1,0:T(8,128)(2,1)}, bf16[768,2048]{1,0:T(8,128)(2,1)}, u32[]{:S(2)}, u32[]{:S(2)}) collective-permute-start(bf16[768,2048]{1,0:T(8,128)(2,1)} %bitcast.48), channel_id=1, source_target_pairs={{0,16},{16,0},{1,17},{17,1},{2,18},{18,2},{3,19},{19,3},{4,20},{20... | collective-permute-start | bytes 9437192 | tf_op jit(solution)/shard_map/ppermute | solution.py:92
  3.3 48.3 %copy-start.12 = (f32[4,32,16]{2,1,0:T(8,128)S(1)}, f32[4,32,16]{2,1,0:T(8,128)}, u32[]{:S(2)}) copy-start(f32[4,32,16]{2,1,0:T(8,128)} %copy.39.refs_4_) | copy-start | bytes 24580
  657.7 6.4 copy-start.2
  657.8 6.4 copy-start.5
  664.1 3.9 copy-start.3
  664.2 5.1 copy-start.4
  669.3 4.1 copy-start.11
  669.3 4.9 copy-start.10
  669.3 5.7 copy-start.18
  669.3 6.3 copy-start.17
  669.3 6.9 %copy-start.22 = (f32[1,128]{1,0:T(1,128)S(1)}, f32[1,128]{1,0:T(1,128)}, u32[]{:S(2)}) copy-start(f32[1,128]{1,0:T(1,128)} %get-tuple-element.243) | copy-start | bytes 1540
  669.3 7.4 %copy-start.21 = (f32[1,128]{1,0:T(1,128)S(1)}, f32[1,128]{1,0:T(1,128)}, u32[]{:S(2)}) copy-start(f32[1,128]{1,0:T(1,128)} %get-tuple-element.244) | copy-start | bytes 1540
  673.3 3.8 copy-start.7
  673.3 5.1 copy-start.9
  677.2 2.3 copy-start.8
  678.5 2.1 copy-start.6
  678.5 3.4 copy-start.1

commit v6 on v5

--- a/solution.py
+++ b/solution.py
@@ -305,18 +305,23 @@
             gy=self.column_of(lax.rem(z, 2)),
         )
 
-    def each(self, call):
-        for k in [sign * far for far in reversed(range(1, self.n)) for sign in (-1, 1)] + [0]:
+    def each(self, call, nearest=0, farthest=None):
+        hops = reversed(range(nearest, self.n if farthest is None else farthest + 1))
+        for k in [sign * far for far in hops for sign in ((-1, 1) if far else (1,))]:
 
             @pl.when((self.me + k >= 0) & (self.me + k < self.n))
             def _():
                 call(self.me + k, k)
 
+    def early(self, z, k):
+        at_end = (z == 0) | (z == self.n - 1)
+        return (abs(k) > 1) | (at_end & (k != 0))
+
     def scatter_near(self, side):
         def send(z, k):
-            if abs(k) > 1:
-
-                @pl.when(lax.rem(z, 2) == side)
+            if k:
+
+                @pl.when((lax.rem(z, 2) == side) & self.early(z, k))
                 def _():
                     self.near(side, z).start()
 
@@ -331,8 +336,13 @@
         mine = self.part(z, self.column_of(side))
         add_rows(mine, mine, self.din.at[z])
         self.near(side, z).start()
-        if abs(k) < 2:
-            self.near(1 - side, z).start()
+        pl.when(jnp.logical_not(self.early(z, k)))(lambda: self.near(1 - side, z).start())
+
+    def closing_steps(self, total):
+        pass_on, line = self.scatter_pass_on, functools.partial(self.scatter_line, total)
+        order = [(pass_on, 2, None), (pass_on, 1, 1), (line, 2, None)]
+        order += [(pass_on, 0, 0), (line, 1, 1), (line, 0, 0)]
+        return [functools.partial(self.each, *step) for step in order]
 
     def along(self, z, up):
         send, recv = self.scatter_sems[:2] if up else self.scatter_sems[2:4]
@@ -549,8 +559,8 @@
     ]
     for save in saves:
         save.start()
-    plane.each(plane.scatter_pass_on)
-    plane.each(functools.partial(plane.scatter_line, total))
+    for step in plane.closing_steps(total):
+        step()
     plane.scatter_finish(total)
     add_rows(out_ref, mid_ref, total)
     plane.gather_drain(slot)
@@ -769,13 +779,8 @@
             for copy in saving(i, give_refs):
                 copy.start()
 
-        @pl.when(i == chunks // 4 - 1)
-        def _():
-            plane.each(plane.scatter_pass_on)
-
-        @pl.when(i == chunks // 2 - 1)
-        def _():
-            plane.each(functools.partial(plane.scatter_line, total))
+        for k, step in enumerate(plane.closing_steps(total)):
+            pl.when(i == min(k + 1, chunks - 1))(step)
 
         return carry
 

time: 683 us -> 682 us (level)
  no operation moved by 1% of the time
where the time goes in v6:
time: 682 us; the launch traced here: 681 us
  Pallas kernels  646 us (95%)
  other arithmetic  21.5 us (3%)
  local copies, waits for them, and re-layouts  11.5 us (2%)
    pallas_call x2, Pallas kernels, moe_forward(): pl.pallas_call(functools.partial(moe_forward_kernel, n, layer), out_shape...  170 us
    pallas_call x2, Pallas kernels, moe_backward(): pl.pallas_call(functools.partial(moe_backward_kernel, n, layer), out_shap...  157 us
    pallas_call x2, Pallas kernels, attn_backward(): pl.pallas_call(functools.partial(attn_backward_kernel, n, layer, heads),...  137 us
    pallas_call x2, Pallas kernels, attn_forward(): pl.pallas_call(functools.partial(attn_forward_kernel, n, layer, heads), o...  109 us
    pallas_call x1, Pallas kernels, share_weights(): pl.pallas_call(functools.partial(share_kernel, n, layer, few), out_shape=...  48.1 us
    pallas_call x1, Pallas kernels, finish_line(): pl.pallas_call(functools.partial(finish_line_kernel, n), out_shape=(shape...  21.2 us
  transfers between devices with their start and end apart: 3, of which 0 were waited for; matrix products, arithmetic and copies ran while one was open for 1% of the time, Pallas kernels for 16%

profile of v6, /device:TPU:0, one launch (start us, length us, event | category | flops | bytes accessed | tf_op | source)
XLA Modules:
  0.0 681.3 jit_solution(16822558589370944642)
XLA Ops:
  0.6 0.0 copy-start
  0.7 0.0 copy-start.20
  0.7 0.0 copy-start.19
  0.7 0.0 copy-start.16
  0.7 0.0 copy-start.15
  0.7 0.6 collective-permute-start
  1.3 0.1 collective-permute-start.1
  1.4 0.4 collective-permute-start.2
  1.8 0.8 select_reduce_fusion
  2.6 0.7 copy.39.refs_4_
  3.3 0.1 pad.5.clone
  3.4 48.1 %share_weights.1 = (bf16[2048,1280]{1,0:T(8,128)(2,1)}, bf16[2048,1024]{1,0:T(8,128)(2,1)}, f32[4,32,16]{2,1,0:T(8,128)}, f32[1,2048]{1,0:T(1,128)}, f32[1,2048]...) custom-call(bf16[1,512,1024]{2,1,0:T(8,128)(2,1)} %rest_0_.1, bf16[1,512,512]{2,1,0:T(8,128)(2,1)} %rest_1_.1, ...), custom_call_target="tpu_custom_call" | custom-call | tf_op jit(solution)/shard_map/share_weights/pallas_call | solution.py:993
  51.6 0.8 dynamic-slice_select_fusion
  52.3 0.2 convert_reduce_fusion
  52.5 0.5 fusion.1
  53.1 0.8 pad_maximum_fusion
  53.9 1.2 broadcast_select_fusion.4
  55.1 0.7 maximum_maximum_fusion.1
  55.8 0.8 fusion.mask_ref
  56.6 0.8 constant_dynamic-slice_fusion.1
  57.4 1.3 broadcast_select_fusion
  58.8 58.8 %attn_forward.2 = (f32[64,2048]{1,0:T(8,128)}, bf16[64,2176]{1,0:T(8,128)(2,1)}, bf16[2,128,2048]{2,1,0:T(8,128)(2,1)}, f32[256,1280]{1,0:T(8,128)}, bf16[256,10...) custom-call(bf16[64,2048]{1,0:T(8,128)(2,1)} %bitcast.53, ...), custom_call_target="tpu_custom_call" | custom-call | tf_op jit(solution)/shard_map/attn_forward/pallas_call | solution.py:1519
  117.6 0.0 collective-permute-done.wg_other
  117.6 0.0 collective-permute-done.1.wu_other
  117.6 90.6 %moe_forward.2 = (bf16[64,2048]{1,0:T(8,128)(2,1)}, bf16[1024,2048]{1,0:T(8,128)(2,1)}, f32[1024,1]{1,0:T(8,128)}, bf16[1024,768]{1,0:T(8,128)(2,1)}, bf16[1024,...) custom-call(f32[64,2048]{1,0:T(8,128)} %get-tuple-element.99.mid_ref, bf16[64,2176]{1,0:T(8,128)(2,1)} %get-tuple-element.100.pay_ref, ...), custom_call_target="tpu_custom_call" | custom-call | tf_op jit(solution)/shard_map/moe_forward/pallas_call | solution.py:594
  208.3 49.8 %attn_forward.3 = (f32[64,2048]{1,0:T(8,128)}, bf16[64,2176]{1,0:T(8,128)(2,1)}, bf16[2,128,2048]{2,1,0:T(8,128)(2,1)}, f32[256,1280]{1,0:T(8,128)}, bf16[256,10...) custom-call(bf16[64,2048]{1,0:T(8,128)(2,1)} %get-tuple-element.101., ...), custom_call_target="tpu_custom_call" | custom-call | tf_op jit(solution)/shard_map/attn_forward/pallas_call | solution.py:1519
  258.1 79.6 %moe_forward.3 = (bf16[64,2048]{1,0:T(8,128)(2,1)}, bf16[1024,2048]{1,0:T(8,128)(2,1)}, f32[1024,1]{1,0:T(8,128)}, bf16[1024,768]{1,0:T(8,128)(2,1)}, bf16[1024,...) custom-call(f32[64,2048]{1,0:T(8,128)} %get-tuple-element.104.mid_ref, bf16[64,2176]{1,0:T(8,128)(2,1)} %get-tuple-element.105.pay_ref, ...), custom_call_target="tpu_custom_call" | custom-call | tf_op jit(solution)/shard_map/moe_forward/pallas_call | solution.py:594
  337.7 79.0 %moe_backward.2 = (f32[64,2048]{1,0:T(8,128)}, f32[1,2048]{1,0:T(1,128)}, bf16[2048,768]{1,0:T(8,128)(2,1)}, bf16[2048,768]{1,0:T(8,128)(2,1)}, bf16[768,2048]{1...) custom-call(bf16[64,2048]{1,0:T(8,128)(2,1)} %bitcast.57, ...), custom_call_target="tpu_custom_call" | custom-call | tf_op jit(solution)/shard_map/moe_backward/pallas_call | solution.py:811
  416.7 47.3 %attn_backward.2 = (bf16[64,2048]{1,0:T(8,128)(2,1)}, f32[1,2048]{1,0:T(1,128)}, f32[1,128]{1,0:T(1,128)}, f32[1,128]{1,0:T(1,128)}, bf16[2048,2304]{1,0:T(8,128)(2,1)}) custom-call(f32[64,2048]{1,0:T(8,128)} %get-tuple-element.111.dmid_ref, bf16[64,2048]{1,0:T(8,128)(2,1)} %get-tuple-element.101.x_ref.refs_1_, f32[1,2048]{1,0:T(1,128)} %get-tuple-element.219.gain_attn, ...), custom_call_target="tpu_custom_call" | custom-call | tf_op jit(solution)/shard_map/attn_backward/pallas_call | solution.py:1875
  464.0 77.9 %moe_backward.3 = (f32[64,2048]{1,0:T(8,128)}, f32[1,2048]{1,0:T(1,128)}, bf16[2048,768]{1,0:T(8,128)(2,1)}, bf16[2048,768]{1,0:T(8,128)(2,1)}, bf16[768,2048]{1...) custom-call(bf16[64,2048]{1,0:T(8,128)(2,1)} %get-tuple-element.119., ...), custom_call_target="tpu_custom_call", output_to_operand_aliasing={{2}: (14, {}), {3}: (15, {}), {4}: (16, {}), {5}: (17, {}),... | custom-call | tf_op jit(solution)/shard_map/moe_backward/pallas_call | solution.py:811
  542.0 89.7 %attn_backward.3 = (bf16[64,2048]{1,0:T(8,128)(2,1)}, f32[1,2048]{1,0:T(1,128)}, f32[1,128]{1,0:T(1,128)}, f32[1,128]{1,0:T(1,128)}, f32[512,1024]{1,0:T(8,128)}...) custom-call(f32[64,2048]{1,0:T(8,128)} %get-tuple-element.131.dmid_r, ...), custom_call_target="tpu_custom_call" | custom-call | tf_op jit(solution)/shard_map/attn_backward/pallas_call | solution.py:1875
  631.7 21.2 %finish_line.1 = (f32[2,4352]{1,0:T(2,128)}, f32[512,512]{1,0:T(8,128)}, f32[512,512]{1,0:T(8,128)}) custom-call(f32[1,2048]{1,0:T(1,128)} %get-tuple-element.143.refs_0_, f32[1,2048]{1,0:T(1,128)} %get-tuple-element.144.refs_1_, f32[1,128]{1,0:T(1,128)} %get-tuple-element.145.refs_2_, f32[1,128]{1,0:T(1,128)} %get-tuple-element.146.refs_3_, ...), custom_call_target="tpu_custom_call" | custom-call | tf_op jit(solution)/shard_map/finish_line/pallas_call | solution.py:1056
  652.9 4.2 finish_pair.1
  657.2 6.4 add_bitcast_fusion.2
  663.6 3.9 add_bitcast_fusion.1
  667.5 1.2 copy-done.4
  668.7 4.0 add_bitcast_fusion
  672.8 0.8 copy.60
  673.6 0.8 copy.61
  674.4 0.6 copy.62
  675.0 0.6 copy.63
  675.6 0.5 copy.64
  676.1 0.5 copy.65
  676.6 1.3 copy.66
  677.9 1.0 copy.67
  678.9 1.0 copy.68
  679.9 0.1 copy-done.6
  680.0 1.3 copy.69
  (46 shorter events, 0.1 us)
Async XLA Ops:
  0.6 50.9 %copy-start = (s32[4,1,128]{2,1,0:T(1,128)S(1)}, s32[4,1,128]{2,1,0:T(1,128)}, u32[]{:S(2)}) copy-start(s32[4,1,128]{2,1,0:T(1,128)} %param.18) | copy-start | bytes 6148
  0.7 53.3 %copy-start.20 = (f32[1,128]{1,0:T(1,128)S(1)}, f32[1,128]{1,0:T(1,128)}, u32[]{:S(2)}) copy-start(f32[1,128]{1,0:T(1,128)} %refs_8_.1) | copy-start | bytes 1540
  0.7 53.3 %copy-start.19 = (f32[1,128]{1,0:T(1,128)S(1)}, f32[1,128]{1,0:T(1,128)}, u32[]{:S(2)}) copy-start(f32[1,128]{1,0:T(1,128)} %refs_7_.1) | copy-start | bytes 1540
  0.7 56.7 %copy-start.16 = (f32[1,2048]{1,0:T(1,128)S(1)}, f32[1,2048]{1,0:T(1,128)}, u32[]{:S(2)}) copy-start(f32[1,2048]{1,0:T(1,128)} %refs_6_.1) | copy-start | bytes 24580
  0.7 56.7 %copy-start.15 = (f32[1,2048]{1,0:T(1,128)S(1)}, f32[1,2048]{1,0:T(1,128)}, u32[]{:S(2)}) copy-start(f32[1,2048]{1,0:T(1,128)} %refs_5_.1) | copy-start | bytes 24580
  0.7 55.9 %copy-start.14 = (bf16[4,1,32,2048]{3,2,1,0:T(8,128)(2,1)S(1)}, bf16[4,1,32,2048]{3,2,1,0:T(8,128)(2,1)}, u32[]{:S(2)}) copy-start(bf16[4,1,32,2048]{3,2,1,0:T(8,128)(2,1)} %param.17) | copy-start | bytes 1572868
  0.7 55.9 %copy-start.13 = (bf16[4,1,32,2048]{3,2,1,0:T(8,128)(2,1)S(1)}, bf16[4,1,32,2048]{3,2,1,0:T(8,128)(2,1)}, u32[]{:S(2)}) copy-start(bf16[4,1,32,2048]{3,2,1,0:T(8,128)(2,1)} %param.16) | copy-start | bytes 1572868
  0.7 116.9 %collective-permute-start = (bf16[2048,768]{1,0:T(8,128)(2,1)}, bf16[2048,768]{1,0:T(8,128)(2,1)}, u32[]{:S(2)}, u32[]{:S(2)}) collective-permute-start(bf16[2048,768]{1,0:T(8,128)(2,1)} %bitcast.38), channel_id=1, source_target_pairs={{0,16},{16,0},{1,17},{17,1},{2,18},{18,2},{3,19},{19,3},{4,20},{20... | collective-permute-start | bytes 9437192 | tf_op jit(solution)/shard_map/ppermute | solution.py:92
  1.3 116.3 %collective-permute-start.1 = (bf16[2048,768]{1,0:T(8,128)(2,1)}, bf16[2048,768]{1,0:T(8,128)(2,1)}, u32[]{:S(2)}, u32[]{:S(2)}) collective-permute-start(bf16[2048,768]{1,0:T(8,128)(2,1)} %bitcast.43), channel_id=1, source_target_pairs={{0,16},{16,0},{1,17},{17,1},{2,18},{18,2},{3,19},{19,3},{4,20},{20... | collective-permute-start | bytes 9437192 | tf_op jit(solution)/shard_map/ppermute | solution.py:92
  1.4 116.3 %collective-permute-start.2 = (bf16[768,2048]{1,0:T(8,128)(2,1)}, bf16[768,2048]{1,0:T(8,128)(2,1)}, u32[]{:S(2)}, u32[]{:S(2)}) collective-permute-start(bf16[768,2048]{1,0:T(8,128)(2,1)} %bitcast.48), channel_id=1, source_target_pairs={{0,16},{16,0},{1,17},{17,1},{2,18},{18,2},{3,19},{19,3},{4,20},{20... | collective-permute-start | bytes 9437192 | tf_op jit(solution)/shard_map/ppermute | solution.py:92
  3.3 48.3 %copy-start.12 = (f32[4,32,16]{2,1,0:T(8,128)S(1)}, f32[4,32,16]{2,1,0:T(8,128)}, u32[]{:S(2)}) copy-start(f32[4,32,16]{2,1,0:T(8,128)} %copy.39.refs_4_) | copy-start | bytes 24580
  657.2 6.4 copy-start.2
  657.2 6.4 copy-start.5
  663.6 3.9 copy-start.3
  663.6 5.1 copy-start.4
  668.7 4.1 copy-start.11
  668.7 4.9 copy-start.10
  668.7 5.7 copy-start.18
  668.7 6.3 copy-start.17
  668.7 6.9 %copy-start.22 = (f32[1,128]{1,0:T(1,128)S(1)}, f32[1,128]{1,0:T(1,128)}, u32[]{:S(2)}) copy-start(f32[1,128]{1,0:T(1,128)} %get-tuple-element.243) | copy-start | bytes 1540
  668.7 7.4 %copy-start.21 = (f32[1,128]{1,0:T(1,128)S(1)}, f32[1,128]{1,0:T(1,128)}, u32[]{:S(2)}) copy-start(f32[1,128]{1,0:T(1,128)} %get-tuple-element.244) | copy-start | bytes 1540
  672.8 3.8 copy-start.7
  672.8 5.1 copy-start.9
  676.6 2.3 copy-start.8
  677.9 2.1 copy-start.6
  677.9 3.4 copy-start.1
